TPU v7x, 32 devices: a whole 2x2x4 slice. The times are simulated.
32 devices in a mesh: dp: 4 (over x, core), ctx: 8 (over z, y).
Axes of the slice: x: 2, y: 2, z: 4, core: 2. Of those that a mesh axis runs over, the one named last changes fastest.
Arguments:
- tokens: bfloat16 [4, 1024, 1024], P('dp', 'ctx'), may hold values from -6 to 6
- doc_lengths: int32 [4, 8], P('dp'), may hold values from 1 to 512, 1024 in all within a row
- first_gain: float32 [1024], P(('dp', 'ctx')), may hold values from 0.5 to 1.5
- factor_weights: float32 [1024, 800], P(('dp', 'ctx')), may hold values from -0.25 to 0.25
- output_weights: float32 [1024, 1024], P(('dp', 'ctx')), may hold values from -1.5 to 1.5
- second_gain: float32 [1024], P(('dp', 'ctx')), may hold values from 0.5 to 1.5
- gate_weights: float32 [1024, 2816], P(('dp', 'ctx')), may hold values from -0.1875 to 0.1875
- up_weights: float32 [1024, 2816], P(('dp', 'ctx')), may hold values from -0.1875 to 0.1875
- down_weights: float32 [2816, 1024], P(('dp', 'ctx')), may hold values from -0.109375 to 0.109375
- cotangent: bfloat16 [4, 1024, 1024], P('dp', 'ctx'), may hold values from -6 to 6
Outputs:
- layer_output: bfloat16 [4, 1024, 1024], P('dp', 'ctx')
- input_grad: bfloat16 [4, 1024, 1024], P('dp', 'ctx')
- first_grads: float32 [1024], P(('dp', 'ctx'))
- factor_grads: float32 [1024, 800], P(('dp', 'ctx'))
- output_grads: float32 [1024, 1024], P(('dp', 'ctx'))
- second_grads: float32 [1024], P(('dp', 'ctx'))
- gate_grads: float32 [1024, 2816], P(('dp', 'ctx'))
- up_grads: float32 [1024, 2816], P(('dp', 'ctx'))
- down_grads: float32 [2816, 1024], P(('dp', 'ctx'))
Inputs may be any that keep to these rules, and one draw needn't show every extreme that they name: `doc_lengths`: each stream's 8 document lengths sum to 1024; the documents lie end to end from position 0.
All inputs are finite; a program needn't handle non-finite values.
Results may differ from a plain program's by a relative error of at most 0.018.
The roundings to bfloat16 on the way count: a program that leaves them out, or rounds other values in their place, can miss the bound.
Values may be sent and summed in bfloat16 or wider, within the bound.
A program may use at most 256 MiB of HBM per device.

v0:
```python
import math

import jax
import jax.numpy as jnp
from jax import lax
from jax.sharding import PartitionSpec as P

H = 16
DH = 64
RQ = 6
RKV = 2
FF = 2816
HD = 1024


EPS = 1e-05
HIGH = lax.Precision.HIGHEST


def rms_scale(values_in, gain):
    return (
        values_in * lax.rsqrt(jnp.mean(values_in * values_in, axis=-1, keepdims=True) + EPS) * gain
    )


def rope_tables(positions):
    inverse = 10000.0 ** (-(jnp.arange(DH // 2, dtype=jnp.float32) * 2.0 / DH))
    angles = positions[:, None] * inverse[None, :]
    return (jnp.cos(angles), jnp.sin(angles))


def rotate(vector, cosine, sine):
    half_width = vector.shape[-1] // 2
    lower_half = vector[..., :half_width]
    upper_half = vector[..., half_width:]
    return jnp.concatenate(
        [lower_half * cosine - upper_half * sine, upper_half * cosine + lower_half * sine], axis=-1
    )


def split_factors(factors, cosine, sine):
    leading = factors.shape[:-1]
    edge_one = RQ * H
    edge_two = edge_one + RQ * DH
    edge_three = edge_two + RKV * H
    edge_four = edge_three + RKV * DH
    cos_rank = cosine[:, None, :]
    sin_rank = sine[:, None, :]
    a_query = factors[..., :edge_one].reshape(leading + (RQ, H))
    b_query = rotate(
        factors[..., edge_one:edge_two].reshape(leading + (RQ, DH)), cos_rank, sin_rank
    )
    b_key = rotate(
        factors[..., edge_three:edge_four].reshape(leading + (RKV, DH)), cos_rank, sin_rank
    )
    query = jnp.einsum("btrh,btre->bthe", a_query, b_query, precision=HIGH) / RQ
    packed = jnp.concatenate(
        [
            factors[..., edge_two:edge_three],
            b_key.reshape(leading + (RKV * DH,)),
            factors[..., edge_four:],
        ],
        axis=-1,
    )
    return (query, packed)


def expand_parts(parts):
    group_count = parts.shape[0]
    count = parts.shape[2]
    edge_one = RKV * H
    edge_two = edge_one + RKV * DH
    edge_three = edge_two + RKV * H
    a_key = parts[:, :edge_one].reshape(group_count, RKV, H, count)
    b_key = parts[:, edge_one:edge_two].reshape(group_count, RKV, DH, count)
    a_value = parts[:, edge_two:edge_three].reshape(group_count, RKV, H, count)
    b_value = parts[:, edge_three:].reshape(group_count, RKV, DH, count)
    keys = jnp.einsum("brhk,brek->bhek", a_key, b_key, precision=HIGH) / RKV
    values = jnp.einsum("brhk,brek->bhek", a_value, b_value, precision=HIGH) / RKV
    return (keys, values)


def body(
    tokens,
    doc_lengths,
    first_gain,
    factor_weights,
    output_weights,
    second_gain,
    gate_weights,
    up_weights,
    down_weights,
    cotangent,
):
    groups, seq_len, model_width = tokens.shape
    length = seq_len * lax.axis_size("ctx")
    row_count = groups * seq_len
    pack_width = 2 * RKV * (H + DH)
    score_scale = DH ** (-0.5)
    all_count = lax.axis_size("dp") * lax.axis_size("ctx")
    gathered = (
        lax.all_gather(first_gain.astype(jnp.bfloat16), ("dp", "ctx"), axis=0, tiled=True),
        lax.all_gather(factor_weights.astype(jnp.bfloat16), ("dp", "ctx"), axis=0, tiled=True),
        lax.all_gather(output_weights.astype(jnp.bfloat16), ("dp", "ctx"), axis=0, tiled=True),
        lax.all_gather(second_gain.astype(jnp.bfloat16), ("dp", "ctx"), axis=0, tiled=True),
        lax.all_gather(gate_weights.astype(jnp.bfloat16), ("dp", "ctx"), axis=0, tiled=True),
        lax.all_gather(up_weights.astype(jnp.bfloat16), ("dp", "ctx"), axis=0, tiled=True),
        lax.all_gather(down_weights.astype(jnp.bfloat16), ("dp", "ctx"), axis=0, tiled=True),
    )
    gain_one, weight_fac, weight_out, gain_two, weight_gate, weight_up, weight_down = gathered
    inputs_f = tokens.astype(jnp.float32).reshape(row_count, model_width)
    gain_first = gain_one.astype(jnp.float32)
    normed_in_f, pull_first = jax.vjp(rms_scale, inputs_f, gain_first)
    normed_in = normed_in_f.astype(jnp.bfloat16)
    factors = jnp.dot(normed_in, weight_fac, preferred_element_type=jnp.float32).reshape(
        groups, seq_len, -1
    )
    offset = lax.axis_index("ctx") * seq_len
    query_pos = offset + jnp.arange(seq_len, dtype=jnp.int32)
    cosine_table, sine_table = rope_tables(query_pos.astype(jnp.float32))

    def split_local(factor_values):
        return split_factors(factor_values, cosine_table, sine_table)

    (query_f, packed_f), pull_split = jax.vjp(split_local, factors)
    query = query_f.astype(jnp.bfloat16)
    packet = packed_f.astype(jnp.bfloat16).transpose(0, 2, 1).reshape(groups * pack_width, seq_len)
    doc_ends = jnp.cumsum(doc_lengths, axis=1, dtype=jnp.int32)
    doc_starts = doc_ends - doc_lengths
    all_pos = jnp.arange(length, dtype=jnp.int32)
    doc_all = (
        jnp.sum(
            (all_pos[None, :, None] >= doc_starts[:, None, :]).astype(jnp.int32),
            axis=2,
            dtype=jnp.int32,
        )
        - 1
    )
    query_doc = lax.dynamic_slice_in_dim(doc_all, offset, seq_len, 1)

    def make_mask(key_first, count):
        key_pos = key_first + jnp.arange(count, dtype=jnp.int32)
        key_doc = lax.dynamic_slice_in_dim(doc_all, key_first, count, 1)
        return (key_doc[:, None, :] == query_doc[:, :, None]) & (
            key_pos[None, None, :] <= query_pos[None, :, None]
        )

    def attend_block(carry, piece, key_first):
        allowed = make_mask(key_first, piece.shape[1])
        numer_in, total_in = carry
        keys_f, values_f = expand_parts(
            piece.astype(jnp.float32).reshape(groups, pack_width, piece.shape[1])
        )
        keys = keys_f.astype(jnp.bfloat16)
        values = values_f.astype(jnp.bfloat16)
        score = (
            jnp.einsum("bqhe,bhek->bhqk", query, keys, preferred_element_type=jnp.float32)
            * score_scale
        )
        expo = jnp.where(allowed[:, None], jnp.exp(score), 0.0)
        numer_out = numer_in + jnp.einsum(
            "bhqk,bhek->bqhe", expo.astype(jnp.bfloat16), values, preferred_element_type=jnp.float32
        )
        return (numer_out, total_in + jnp.sum(expo, axis=-1))

    start_state = (
        jnp.zeros((groups, seq_len, H, DH), jnp.float32),
        jnp.zeros((groups, H, seq_len), jnp.float32),
    )
    piece = lax.all_gather(packet, "ctx", axis=1, tiled=True)
    count = piece.shape[1]
    fold_block_len = math.gcd(count, 512)

    def inner_step(state, block_index):
        key_first = block_index * fold_block_len
        sub_piece = lax.dynamic_slice_in_dim(piece, key_first, fold_block_len, 1)
        return (attend_block(state, sub_piece, key_first), None)

    carry_out, unused = lax.scan(
        inner_step, start_state, jnp.arange(count // fold_block_len, dtype=jnp.int32)
    )
    numer, total = carry_out

    def normalize(numer_in, total_in):
        return numer_in / total_in.transpose(0, 2, 1)[..., None]

    attn_f, pull_divide = jax.vjp(normalize, numer, total)
    attn = attn_f.astype(jnp.bfloat16).reshape(row_count, H * DH)
    branch = jnp.dot(attn, weight_out, preferred_element_type=jnp.float32)
    middle = inputs_f + branch
    gain_second = gain_two.astype(jnp.float32)
    normed_mid_f, pull_second = jax.vjp(rms_scale, middle, gain_second)
    normed_mid = normed_mid_f.astype(jnp.bfloat16)
    gate = jnp.dot(normed_mid, weight_gate, preferred_element_type=jnp.float32)
    upward = jnp.dot(normed_mid, weight_up, preferred_element_type=jnp.float32)

    def swiglu(gate_in, up_in):
        return jax.nn.silu(gate_in) * up_in

    hidden_f, pull_glu = jax.vjp(swiglu, gate, upward)
    hidden = hidden_f.astype(jnp.bfloat16)
    layer_output = (
        middle + jnp.dot(hidden, weight_down, preferred_element_type=jnp.float32)
    ).astype(jnp.bfloat16)
    regathered = (
        lax.all_gather(first_gain.astype(jnp.bfloat16), ("dp", "ctx"), axis=0, tiled=True),
        lax.all_gather(factor_weights.astype(jnp.bfloat16), ("dp", "ctx"), axis=0, tiled=True),
        lax.all_gather(output_weights.astype(jnp.bfloat16), ("dp", "ctx"), axis=0, tiled=True),
        lax.all_gather(second_gain.astype(jnp.bfloat16), ("dp", "ctx"), axis=0, tiled=True),
        lax.all_gather(gate_weights.astype(jnp.bfloat16), ("dp", "ctx"), axis=0, tiled=True),
        lax.all_gather(up_weights.astype(jnp.bfloat16), ("dp", "ctx"), axis=0, tiled=True),
        lax.all_gather(down_weights.astype(jnp.bfloat16), ("dp", "ctx"), axis=0, tiled=True),
    )
    back_fac = regathered[1]
    back_out = regathered[2]
    back_gate = regathered[4]
    back_up = regathered[5]
    back_down = regathered[6]
    cot_low = cotangent.reshape(row_count, model_width)
    cot_f = cot_low.astype(jnp.float32)
    d_hidden = jnp.einsum("td,fd->tf", cot_low, back_down, preferred_element_type=jnp.float32)
    d_gate_f, d_up_f = pull_glu(d_hidden)
    d_gate = d_gate_f.astype(jnp.bfloat16)
    d_up = d_up_f.astype(jnp.bfloat16)
    d_norm_mid = jnp.einsum(
        "tf,df->td", d_gate, back_gate, preferred_element_type=jnp.float32
    ) + jnp.einsum("tf,df->td", d_up, back_up, preferred_element_type=jnp.float32)
    d_mid_norm, second_grad = pull_second(d_norm_mid)
    d_middle = cot_f + d_mid_norm
    d_branch = d_middle.astype(jnp.bfloat16)
    d_attn = jnp.einsum(
        "td,cd->tc", d_branch, back_out, preferred_element_type=jnp.float32
    ).reshape(groups, seq_len, H, DH)
    d_numer_f, d_total = pull_divide(d_attn)
    d_numer = d_numer_f.astype(jnp.bfloat16)
    whole = lax.all_gather(packet, "ctx", axis=1, tiled=True)
    block_len = math.gcd(length, 512)

    def back_step(block_index, state):
        dquery, terms = state
        key_first = block_index * block_len
        sub_piece = lax.dynamic_slice_in_dim(whole, key_first, block_len, 1)
        allowed = make_mask(key_first, block_len)
        parts = sub_piece.astype(jnp.float32).reshape(groups, pack_width, block_len)
        (keys_f, values_f), pull_expand = jax.vjp(expand_parts, parts)
        keys = keys_f.astype(jnp.bfloat16)
        values = values_f.astype(jnp.bfloat16)
        score = (
            jnp.einsum("bqhe,bhek->bhqk", query, keys, preferred_element_type=jnp.float32)
            * score_scale
        )
        expo = jnp.where(allowed[:, None], jnp.exp(score), 0.0)
        d_prob = jnp.einsum("bqhe,bhek->bhqk", d_numer, values, preferred_element_type=jnp.float32)
        d_score = (expo * (d_prob + d_total[..., None])).astype(jnp.bfloat16)
        dquery_out = (
            dquery
            + jnp.einsum("bhqk,bhek->bqhe", d_score, keys, preferred_element_type=jnp.float32)
            * score_scale
        )
        d_keys = (
            jnp.einsum("bhqk,bqhe->bhek", d_score, query, preferred_element_type=jnp.float32)
            * score_scale
        )
        d_values = jnp.einsum(
            "bhqk,bqhe->bhek",
            expo.astype(jnp.bfloat16),
            d_numer,
            preferred_element_type=jnp.float32,
        )
        d_parts = pull_expand((d_keys, d_values))[0]
        term_block = d_parts.reshape(groups * pack_width, block_len)
        return (dquery_out, lax.dynamic_update_slice_in_dim(terms, term_block, key_first, 1))

    start_back = (
        jnp.zeros((groups, seq_len, H, DH), jnp.float32),
        jnp.zeros((groups * pack_width, length), jnp.float32),
    )
    d_query, factor_terms = lax.fori_loop(0, length // block_len, back_step, start_back)
    d_packet = lax.psum_scatter(factor_terms, "ctx", scatter_dimension=1, tiled=True)
    d_packed = d_packet.reshape(groups, pack_width, seq_len).transpose(0, 2, 1)
    d_factors = pull_split((d_query, d_packed))[0].reshape(row_count, -1).astype(jnp.bfloat16)
    d_norm_in = jnp.einsum("tf,df->td", d_factors, back_fac, preferred_element_type=jnp.float32)
    d_in_norm, first_grad = pull_first(d_norm_in)
    input_grad = (d_middle + d_in_norm).astype(jnp.bfloat16)
    fac_width = d_factors.shape[1]
    ff_width = d_gate.shape[1]
    fac_part = jnp.einsum("td,tf->df", normed_in, d_factors, preferred_element_type=jnp.float32)
    gate_part = jnp.einsum("td,tf->df", normed_mid, d_gate, preferred_element_type=jnp.float32)
    up_part = jnp.einsum("td,tf->df", normed_mid, d_up, preferred_element_type=jnp.float32)
    first_part = first_grad[:, None]
    second_part = second_grad[:, None]
    row_sums = lax.psum_scatter(
        jnp.concatenate([fac_part, gate_part, up_part, first_part, second_part], axis=1),
        ("dp", "ctx"),
        scatter_dimension=0,
        tiled=True,
    )
    fac_sum = row_sums[:, :fac_width]
    gate_sum = row_sums[:, fac_width : fac_width + ff_width]
    up_sum = row_sums[:, fac_width + ff_width : fac_width + 2 * ff_width]
    first_sum = row_sums[:, fac_width + 2 * ff_width]
    second_sum = row_sums[:, fac_width + 2 * ff_width + 1]
    head_dev = HD // all_count
    hidden_dev = FF // all_count
    stack_dev = head_dev + hidden_dev
    block_count = stack_dev * lax.axis_size(("dp", "ctx")) // stack_dev
    out_part = jnp.einsum("tc,td->cd", attn, d_branch, preferred_element_type=jnp.float32).reshape(
        block_count, head_dev, model_width
    )
    down_part = jnp.einsum(
        "tf,td->fd", hidden, cot_low, preferred_element_type=jnp.float32
    ).reshape(block_count, hidden_dev, model_width)
    col_sums = lax.psum_scatter(
        jnp.concatenate([out_part, down_part], axis=1).reshape(
            stack_dev * lax.axis_size(("dp", "ctx")), model_width
        ),
        ("dp", "ctx"),
        scatter_dimension=0,
        tiled=True,
    )
    out_sum = col_sums[:head_dev]
    down_sum = col_sums[head_dev:]
    return (
        layer_output.reshape(groups, seq_len, model_width),
        input_grad.reshape(groups, seq_len, model_width),
        first_sum,
        fac_sum,
        out_sum,
        second_sum,
        gate_sum,
        up_sum,
        down_sum,
    )


def solution(mesh):
    return jax.shard_map(
        body,
        mesh=mesh,
        in_specs=(
            P("dp", "ctx", None),
            P("dp", None),
            P(("dp", "ctx")),
            P(("dp", "ctx"), None),
            P(("dp", "ctx"), None),
            P(("dp", "ctx")),
            P(("dp", "ctx"), None),
            P(("dp", "ctx"), None),
            P(("dp", "ctx"), None),
            P("dp", "ctx", None),
        ),
        out_specs=(
            P("dp", "ctx", None),
            P("dp", "ctx", None),
            P(("dp", "ctx")),
            P(("dp", "ctx"), None),
            P(("dp", "ctx"), None),
            P(("dp", "ctx")),
            P(("dp", "ctx"), None),
            P(("dp", "ctx"), None),
            P(("dp", "ctx"), None),
        ),
        check_vma=False,
    )
```

profile of v0, /device:TPU:0, one launch (start us, length us, event | category | flops | bytes accessed | tf_op | source)
XLA Modules:
  0.0 981.9 jit_solution(15002311745306689250)
XLA Ops:
  15.4 42.2 %all-reduce.15 = (bf16[1024]{0:T(1024)(128)(2,1)S(1)}, bf16[1024]{0:T(1024)(128)(2,1)S(1)}) all-reduce(bf16[1024]{0:T(1024)(128)(2,1)S(1)} %dynamic-update-slice, bf16[1024]{0:T(1024)(128)(2,1)S(1)} %dynamic-update-slice.1), channel_id=1, replica_groups=mesh['dp'=4,'ctx'=8] {'dp','ctx'}, use_global_device_ids=true, to_apply=%add.13 | all-reduce | flops 2048 | bytes 8192
  58.5 11.7 %all-gather.7.cloned.1.call-done = bf16[1024,800]{1,0:T(8,128)(2,1)} async-done(((bf16[32,800]{1,0:T(8,128)(2,1)}), bf16[1024,800]{1,0:T(8,128)(2,1)}) %all-gather.7.cloned.1.call-update) | async-done | bytes 1638416 | tf_op jit(solution)/shard_map/all_gather | solution.py:103
  77.1 29.7 %all-gather = bf16[1,320,1024]{2,1,0:T(8,128)(2,1)} all-gather(bf16[1,320,128]{2,1,0:T(8,128)(2,1)S(1)} %maximum_bitcast_fusion.3), channel_id=2, replica_groups=mesh['dp'=4,'ctx'=8] {'ctx'}, dimensions={2}, use_global_device_ids=true | all-gather | bytes 737280 | tf_op jit(solution)/shard_map/all_gather | solution.py:170
  106.8 28.0 %while.31 = (s32[]{:T(128)}, f32[1,128,16,64]{1,3,2,0:T(8,128)S(1)}, f32[1,16,128]{2,1,0:T(8,128)S(1)}, s32[2]{0:T(128)S(1)}, bf16[320,1024]{1,0:T(8,128)(2,1)},...) while((s32[]{:T(128)}, ...), condition=%wide.region_5.6_spmd.clone, body=%wide.region_3.5_spmd.clone.sunk | while | flops 281479808 | bytes 16428762 | solution.py:179
  116.4 4.4 fusion.212
  130.4 4.4 fusion.212
  137.4 62.0 %all-gather.11.cloned.1.call-done = bf16[1024,2816]{1,0:T(8,128)(2,1)} async-done(((bf16[32,2816]{1,0:T(8,128)(2,1)}), bf16[1024,2816]{1,0:T(8,128)(2,1)}) %all-gather.11.cloned.1.call-update) | async-done | bytes 5767184 | tf_op jit(solution)/shard_map/all_gather | solution.py:106
  199.4 4.7 fusion.111
  204.1 64.7 %all-gather.13.cloned.1.call-done = bf16[1024,2816]{1,0:T(8,128)(2,1)} async-done(((bf16[32,2816]{1,0:T(8,128)(2,1)}), bf16[1024,2816]{1,0:T(8,128)(2,1)}) %all-gather.13.cloned.1.call-update) | async-done | bytes 5767184 | tf_op jit(solution)/shard_map/all_gather | solution.py:107
  268.8 5.7 fusion.53
  274.4 63.7 %all-gather.15.cloned.1.call-done = bf16[2816,1024]{1,0:T(8,128)(2,1)} async-done(((bf16[88,1024]{1,0:T(8,128)(2,1)}), bf16[2816,1024]{1,0:T(8,128)(2,1)}) %all-gather.15.cloned.1.call-update) | async-done | bytes 5767184 | tf_op jit(solution)/shard_map/all_gather | solution.py:108
  338.1 5.9 multiply_convert_fusion.4
  352.9 117.1 %while.32 = (s32[]{:T(128)}, f32[1,128,16,64]{1,3,2,0:T(8,128)}, f32[320,1024]{1,0:T(8,128)}, bf16[320,1024]{1,0:T(8,128)(2,1)}, s32[1,1024]{1,0:T(1,128)S(1)}, ...) while((s32[]{:T(128)}, f32[1,128,16,64]{1,3,2,0:T(8,128)}, ...), condition=%wide.region_10.11_spmd.clone, body=%wide.region_9.10_spmd.clone.sunk | while | flops 738230912 | bytes 78073920 | solution.py:278
  384.3 3.9 copy.288
  388.2 5.6 convolution_bitcast_fusion.11
  393.9 4.6 convolution_bitcast_fusion.12
  401.8 3.8 copy.291
  405.7 5.6 convolution_bitcast_fusion.13
  411.5 4.6 convolution_bitcast_fusion.14
  436.6 3.9 copy.288
  440.5 5.6 convolution_bitcast_fusion.11
  446.3 4.6 convolution_bitcast_fusion.12
  458.0 5.6 convolution_bitcast_fusion.13
  463.8 4.6 convolution_bitcast_fusion.14
  474.3 6.3 pad_maximum_fusion
  490.3 5.9 fusion.113
  496.2 5.9 fusion.114
  502.1 32.3 %reduce-scatter.4.cloned.1.call-done = f32[320,128]{1,0:T(8,128)} async-done(((f32[320,1024]{1,0:T(8,128)}), f32[320,128]{1,0:T(8,128)}) %reduce-scatter.4.cloned.1.call-update) | async-done | bytes 163856 | tf_op jit(solution)/shard_map/reduce_scatter | solution.py:279
  542.2 34.1 %concatenate.31 = f32[1024,6434]{1,0:T(8,128)} concatenate(f32[1024,800]{1,0:T(8,128)} %fusion.79, f32[1024,2816]{1,0:T(8,128)} %fusion.113, f32[1024,2816]{1,0:T(8,128)} %fusion.114, f32[1024,1]{1,0:T(8,128)S(1)} %copy.235, f32[1024,1]{1,0:T(8,128)S(1)} %copy.236), dimensions={1} | concatenate | bytes 52707328 | tf_op jit(solution)/shard_map/concatenate | solution.py:293
  577.9 5.3 fusion.61
  584.1 126.0 %reduce-scatter.8.cloned.1.call-done = f32[120,1024]{1,0:T(8,128)} async-done(((f32[3840,1024]{1,0:T(8,128)}), f32[120,1024]{1,0:T(8,128)}) %reduce-scatter.8.cloned.1.call-update) | async-done | bytes 491536 | tf_op jit(solution)/shard_map/reduce_scatter | solution.py:313
  713.4 256.0 %reduce-scatter.6.cloned.1.call-done = f32[32,6434]{1,0:T(8,128)} async-done(((f32[1024,6434]{1,0:T(8,128)}), f32[32,6434]{1,0:T(8,128)}) %reduce-scatter.6.cloned.1.call-update) | async-done | bytes 823568 | tf_op jit(solution)/shard_map/reduce_scatter | solution.py:292
  (332 shorter events, 127.8 us)
Async XLA Ops:
  7.2 6.9 copy-start.45
  7.2 7.7 copy-start.56
  7.2 7.7 copy-start.57
  7.2 50.4 %copy-start.58 = (s32[1,8]{1,0:T(1,128)S(1)}, s32[1,8]{1,0:T(1,128)}, u32[]{:S(2)}) copy-start(s32[1,8]{1,0:T(1,128)} %param.15) | copy-start | bytes 100
  7.2 51.1 %copy-start.18 = (bf16[1,128,1024]{2,1,0:T(8,128)(2,1)S(1)}, bf16[1,128,1024]{2,1,0:T(8,128)(2,1)}, u32[]{:S(2)}) copy-start(bf16[1,128,1024]{2,1,0:T(8,128)(2,1)} %param.14) | copy-start | bytes 786436
  7.2 62.9 %all-gather.7.cloned.1.call-start = ((), (), s32[]{:S(2)}) async-start(), calls=%async_computation.3 | async-start | bytes 1892352 | tf_op jit(solution)/shard_map/all_gather | solution.py:103
  8.9 126.0 %all-gather.9.cloned.1.call-start = ((), (), s32[]{:S(2)}) async-start(), calls=%async_computation.4 | async-start | bytes 2162688 | tf_op jit(solution)/shard_map/all_gather | solution.py:104
  10.5 188.8 %all-gather.11.cloned.1.call-start = ((), (), s32[]{:S(2)}) async-start(), calls=%async_computation.5 | async-start | bytes 5947392 | tf_op jit(solution)/shard_map/all_gather | solution.py:106
  12.3 256.5 %all-gather.13.cloned.1.call-start = ((), (), s32[]{:S(2)}) async-start(), calls=%async_computation.6 | async-start | bytes 5947392 | tf_op jit(solution)/shard_map/all_gather | solution.py:107
  14.0 324.1 %all-gather.15.cloned.1.call-start = ((), (), s32[]{:S(2)}) async-start(), calls=%async_computation.7 | async-start | bytes 5947392 | tf_op jit(solution)/shard_map/all_gather | solution.py:108
  14.8 519.6 %reduce-scatter.4.cloned.1.call-start = ((), (), s32[]{:S(2)}) async-start(), calls=%async_computation.8 | async-start | bytes 1474560 | tf_op jit(solution)/shard_map/reduce_scatter | solution.py:279
  57.6 15.3 %copy-start.50 = (f32[1024]{0:T(1024)}, f32[1024]{0:T(1024)S(1)}, u32[]{:S(2)}) copy-start(f32[1024]{0:T(1024)S(1)} %convert_element_type.206) | copy-start | bytes 12292
  57.9 19.1 %copy-start.46 = (f32[128,32]{0,1:T(8,128)}, f32[128,32]{0,1:T(8,128)S(1)}, u32[]{:S(2)}) copy-start(f32[128,32]{0,1:T(8,128)S(1)} %get-tuple-element.538) | copy-start | bytes 49156
  57.9 19.1 %copy-start.48 = (f32[128,32]{0,1:T(8,128)}, f32[128,32]{0,1:T(8,128)S(1)}, u32[]{:S(2)}) copy-start(f32[128,32]{0,1:T(8,128)S(1)} %get-tuple-element.539) | copy-start | bytes 49156
  58.0 15.4 %copy-start.41 = (f32[128,32]{1,0:T(8,128)}, f32[128,32]{1,0:T(8,128)S(1)}, u32[]{:S(2)}) copy-start(f32[128,32]{1,0:T(8,128)S(1)} %copy.224) | copy-start | bytes 49156
  58.1 15.3 %copy-start.43 = (f32[128,32]{1,0:T(8,128)}, f32[128,32]{1,0:T(8,128)S(1)}, u32[]{:S(2)}) copy-start(f32[128,32]{1,0:T(8,128)S(1)} %copy.222) | copy-start | bytes 49156
  58.5 14.4 %copy-start.54 = (f32[128]{0:T(128)}, f32[128]{0:T(128)S(1)}, u32[]{:S(2)}) copy-start(f32[128]{0:T(128)S(1)} %fusion.70) | copy-start | bytes 1540
  58.5 14.4 %copy-start.52 = (f32[128]{0:T(128)}, f32[128]{0:T(128)S(1)}, u32[]{:S(2)}) copy-start(f32[128]{0:T(128)S(1)} %fusion.99) | copy-start | bytes 1540
  134.9 69.2 %copy-start.34 = (bf16[1,128,16,64]{1,3,2,0:T(8,128)(2,1)}, bf16[1,128,16,64]{1,3,2,0:T(8,128)(2,1)S(1)}, u32[]{:S(2)}) copy-start(bf16[1,128,16,64]{1,3,2,0:T(8,128)(2,1)S(1)} %divide_convert_fusion.1) | copy-start | bytes 786436
  137.3 212.0 %copy-start.11 = (f32[128,1024]{1,0:T(8,128)}, f32[128,1024]{1,0:T(8,128)S(1)}, u32[]{:S(2)}) copy-start(f32[128,1024]{1,0:T(8,128)S(1)} %get-tuple-element.543) | copy-start | bytes 1572868
  137.4 131.3 %copy-start.16 = (bf16[128,1024]{1,0:T(8,128)(2,1)}, bf16[128,1024]{1,0:T(8,128)(2,1)S(1)}, u32[]{:S(2)}) copy-start(bf16[128,1024]{1,0:T(8,128)(2,1)S(1)} %multiply_convert_fusion.7) | copy-start | bytes 786436
  204.1 134.0 %copy-start.39 = (bf16[1,128,1024]{2,1,0:T(8,128)(2,1)S(1)}, bf16[1,128,1024]{2,1,0:T(8,128)(2,1)}, u32[]{:S(2)}) copy-start(bf16[1,128,1024]{2,1,0:T(8,128)(2,1)} %param.23) | copy-start | bytes 786436
  268.8 75.3 %slice-start = ((s8[5767168]{0:T(1024)(128)(4,1)}), s8[1572864]{0:T(1024)(128)(4,1)S(1)}, s32[]{:S(2)}) async-start(s8[5767168]{0:T(1024)(128)(4,1)} %bitcast.441), calls=%async_computation.11 | async-start | bytes 3145728
  338.1 5.9 slice-start.1
  470.1 240.0 %reduce-scatter.8.cloned.1.call-start = ((), (), s32[]{:S(2)}) async-start(), calls=%async_computation.10 | async-start | bytes 16220160 | tf_op jit(solution)/shard_map/reduce_scatter | solution.py:313
  480.6 488.9 %reduce-scatter.6.cloned.1.call-start = ((), (), s32[]{:S(2)}) async-start(), calls=%async_computation.9 | async-start | bytes 27574272 | tf_op jit(solution)/shard_map/reduce_scatter | solution.py:292
  490.3 5.9 copy-start.31
  496.2 40.7 %copy-start.47 = (f32[128,32]{0,1:T(8,128)S(1)}, f32[128,32]{0,1:T(8,128)}, u32[]{:S(2)}) copy-start(f32[128,32]{0,1:T(8,128)} %copy-done.46) | copy-start | bytes 49156
  496.2 40.7 %copy-start.49 = (f32[128,32]{0,1:T(8,128)S(1)}, f32[128,32]{0,1:T(8,128)}, u32[]{:S(2)}) copy-start(f32[128,32]{0,1:T(8,128)} %copy-done.48) | copy-start | bytes 49156
  496.2 40.8 %copy-start.19 = (bf16[1,128,1024]{2,1,0:T(8,128)(2,1)S(1)}, bf16[1,128,1024]{2,1,0:T(8,128)(2,1)}, u32[]{:S(2)}) copy-start(bf16[1,128,1024]{2,1,0:T(8,128)(2,1)} %param.14) | copy-start | bytes 786436
  496.2 40.8 %copy-start.51 = (f32[1024]{0:T(1024)S(1)}, f32[1024]{0:T(1024)}, u32[]{:S(2)}) copy-start(f32[1024]{0:T(1024)} %copy-done.50) | copy-start | bytes 12292
  496.2 40.8 %copy-start.53 = (f32[128]{0:T(128)S(1)}, f32[128]{0:T(128)}, u32[]{:S(2)}) copy-start(f32[128]{0:T(128)} %copy-done.52) | copy-start | bytes 1540
  (50 other events, 137.9 us)
Sparse Core Ops, SparseCore 0:
  11.5 58.6 all-gather.6
  73.7 55.9 all-gather.8
  133.2 66.1 all-gather.10
  202.7 65.9 all-gather.12
  272.1 65.9 all-gather.14
  470.2 64.2 reduce-scatter.3
  540.5 169.5 reduce-scatter.7
  716.5 252.8 reduce-scatter.5
where the time goes:
time: 989 us; the launch traced here: 982 us
  waiting for transfers between devices  616 us (62%)
  matrix products  152 us (15%)
  local copies, waits for them, and re-layouts  91.8 us (9%)
  blocking collectives  71.8 us (7%)
  other arithmetic  18.5 us (2%)
  loops' own time  15.7 us (2%)
  between operations  15.4 us (2%)
    reduce_scatter x1, waiting for transfers between devices, body(): lax.psum_scatter(jnp.concatenate([fac_part, gate_part, up_part, first_par...  256 us
    reduce_scatter x1, waiting for transfers between devices, body(): lax.psum_scatter(jnp.concatenate([out_part, down_part], axis=1).reshape(s...  126 us
    all_gather x1, waiting for transfers between devices, body(): lax.all_gather(up_weights.astype(jnp.bfloat16), ('dp', 'ctx'), axis=0, ti...  64.7 us
    all_gather x1, waiting for transfers between devices, body(): lax.all_gather(down_weights.astype(jnp.bfloat16), ('dp', 'ctx'), axis=0,...  63.7 us
    all_gather x1, waiting for transfers between devices, body(): lax.all_gather(gate_weights.astype(jnp.bfloat16), ('dp', 'ctx'), axis=0,...  62 us
    unnamed x1, blocking collectives  42.2 us
    concatenate x1, local copies, waits for them, and re-layouts, body(): jnp.concatenate([fac_part, gate_part, up_part, first_part, second_part],...  34.1 us
    reduce_scatter x1, waiting for transfers between devices, body(): lax.psum_scatter(factor_terms, 'ctx', scatter_dimension=1, tiled=True)  32.3 us
  transfers between devices with their start and end apart: 8, of which 7 were waited for; matrix products, arithmetic and copies ran while one was open for 14% of the time, Pallas kernels for 0%

commit v1 on v0

v1 whole, which is shorter than its diff:
```python
import functools

import jax
import jax.numpy as jnp
import numpy as np
from jax import lax
from jax.experimental import pallas as pl
from jax.experimental.pallas import tpu as pltpu
from jax.sharding import PartitionSpec as P

H = 16
DH = 64
RQ = 6
RKV = 2
EPS = 1e-05
BF = jnp.bfloat16
F32 = jnp.float32
AQ = RQ * H
BQ = RQ * DH
AK = RKV * H
BK = RKV * DH
PACK = 2 * (AK + BK)
KEY_ROWS = AK + BK
FDIM = AQ + BQ + PACK
FPAD = 896
LOG2E = 1.4426950408889634
NEG = -1e30


def nt(a, b):
    return lax.dot_general(a, b, (((1,), (1,)), ((), ())), preferred_element_type=F32)


def nn(a, b):
    return jnp.dot(a, b, preferred_element_type=F32)


def blocks(count, step, state):
    if count <= 8:
        for j in range(count):
            state = step(j, state)
        return state
    return lax.fori_loop(0, count, step, state)


def lane_block(j, size):
    if isinstance(j, int):
        return pl.ds(j * size, size)
    return pl.ds(pl.multiple_of(j * size, size), size)


def rope(b, cosine, sine, ranks):
    parts = []
    half = DH // 2
    for r in range(ranks):
        u1 = b[r * DH : r * DH + half]
        u2 = b[r * DH + half : (r + 1) * DH]
        parts += [u1 * cosine - u2 * sine, u2 * cosine + u1 * sine]
    return jnp.concatenate(parts, axis=0)


def rope_back(v, cosine, sine, ranks):
    return rope(v, cosine, -sine, ranks)


def pre_kernel(x_ref, g_ref, w_ref, cos_ref, sin_ref, nt_ref, q_ref, p_ref, a_ref, b_ref):
    x = x_ref[...].astype(F32)
    r1 = lax.rsqrt(jnp.mean(x * x, axis=-1, keepdims=True) + EPS)
    n = (x * r1 * g_ref[...]).astype(BF)
    nt_ref[...] = n.T
    ft = nn(n, w_ref[...]).T
    cosine, sine = cos_ref[...], sin_ref[...]
    a = ft[:AQ]
    b = rope(ft[AQ : AQ + BQ], cosine, sine, RQ)
    for i in range(AQ):
        a_ref[i] = a[i : i + 1]
    b_ref[...] = b
    k0 = AQ + BQ
    bk = rope(ft[k0 + AK : k0 + AK + BK], cosine, sine, RKV)
    p_ref[...] = jnp.concatenate(
        [ft[k0 : k0 + AK], bk, ft[k0 + KEY_ROWS : k0 + PACK]], axis=0
    ).astype(BF)
    for h in range(H):
        acc = a[h : h + 1] * b[:DH]
        for r in range(1, RQ):
            acc = acc + a[r * H + h : r * H + h + 1] * b[r * DH : (r + 1) * DH]
        q_ref[h * DH : (h + 1) * DH, :] = (acc * (1.0 / RQ)).astype(BF)


def expand_pair(ka, kb, side, p, lanes):
    rows = []
    for hh in range(2):
        acc = 0.0
        for r in range(RKV):
            a = ka[side * AK + r * H + 2 * p + hh, :, lanes]
            b = kb[side * BK + r * DH : side * BK + (r + 1) * DH, lanes]
            acc = acc + a * b
        rows.append(acc * (1.0 / RKV))
    return jnp.concatenate(rows, axis=0)


def unpack(kv_ref, ka, kb):
    for side in range(2):
        first = side * KEY_ROWS
        a = kv_ref[first : first + AK, :].astype(F32)
        for i in range(AK):
            ka[side * AK + i] = a[i : i + 1]
        kb[side * BK : (side + 1) * BK, :] = kv_ref[first + AK : first + KEY_ROWS, :].astype(F32)


def diagonal(pair):
    zero = jnp.zeros((DH, pair.shape[1]), pair.dtype)
    left = jnp.concatenate([pair[:DH], zero], axis=0)
    right = jnp.concatenate([zero, pair[DH:]], axis=0)
    return jnp.concatenate([left, right], axis=1)


def undiagonal(wide):
    t = wide.shape[1] // 2
    return jnp.concatenate([wide[:DH, :t], wide[DH:, t:]], axis=0)


def attend_kernel(nblk, base_ref, len_ref, q_ref, kv_ref, at_ref, af_ref, inv_ref, p_ref, ka, kb, bias):
    t = q_ref.shape[1]
    c = lax.axis_index("ctx")
    tpos = c * t + lax.broadcasted_iota(jnp.int32, (1, t), 1)
    start = jnp.zeros((1, t), jnp.int32)
    run = jnp.int32(0)
    for j in range(len_ref.shape[1]):
        start = jnp.where(tpos >= run, run, start)
        run = run + len_ref[0, j]
    unpack(kv_ref, ka, kb)

    def bias_block(j, _):
        spos = base_ref[0] + j * t + lax.broadcasted_iota(jnp.int32, (t, t), 0)
        ok = (spos >= start) & (spos <= tpos)
        bias[lane_block(j, t), :] = jnp.where(ok, 0.0, NEG)
        return _

    blocks(nblk, bias_block, 0)

    def pair(p, _):
        rows = pl.ds(pl.multiple_of(p * 2 * DH, 2 * DH), 2 * DH)
        qd = diagonal(q_ref[rows, :])

        def step(j, state):
            num, tot = state
            lanes = lane_block(j, t)
            k = expand_pair(ka, kb, 0, p, lanes).T.astype(BF)
            v = expand_pair(ka, kb, 1, p, lanes).astype(BF)
            b = bias[lanes, :]
            s = nn(k, qd) * (LOG2E * DH**-0.5) + jnp.concatenate([b, b], axis=1)
            e = jnp.exp2(s)
            tot = tot + jnp.sum(e, axis=0, keepdims=True)
            pb = e.astype(BF)
            p_ref[p, lanes, :] = pb
            return (num + nn(v, pb), tot)

        num, tot = blocks(
            nblk, step, (jnp.zeros((2 * DH, 2 * t), F32), jnp.zeros((1, 2 * t), F32))
        )
        inv = 1.0 / tot
        af = undiagonal(num * inv)
        af_ref[rows, :] = af
        at_ref[rows, :] = af.astype(BF)
        inv_ref[p] = jnp.broadcast_to(inv, (8, 2 * t))
        return _

    lax.fori_loop(0, H // 2, pair, 0)


def attend_back_kernel(
    nblk, da_ref, af_ref, inv_ref, p_ref, q_ref, kv_ref, a_ref, b_ref, cos_ref, sin_ref,
    dq_ref, dkv_ref, ka, kb, dka, dqa, db,
):
    t = q_ref.shape[1]
    unpack(kv_ref, ka, kb)
    db[...] = jnp.zeros_like(db)
    for side in range(2):
        first = side * KEY_ROWS + AK
        dkv_ref[first : first + BK, :] = jnp.zeros((BK, nblk * t), F32)

    def factor_back(dwide, side, p, lanes):
        for hh in range(2):
            d = dwide[hh * DH : (hh + 1) * DH] * (1.0 / RKV)
            for r in range(RKV):
                row = side * AK + r * H + 2 * p + hh
                first = side * KEY_ROWS + AK + r * DH
                b = kb[side * BK + r * DH : side * BK + (r + 1) * DH, lanes]
                dka[row, :, lanes] = jnp.sum(d * b, axis=0, keepdims=True)
                dkv_ref[first : first + DH, lanes] += d * ka[row, :, lanes]

    def pair(p, _):
        rows = pl.ds(pl.multiple_of(p * 2 * DH, 2 * DH), 2 * DH)
        da = da_ref[rows, :]
        inv = inv_ref[p][:1]
        dd = diagonal(da)
        dn = (dd * inv).astype(BF)
        dtot = -jnp.sum(dd * diagonal(af_ref[rows, :]), axis=0, keepdims=True) * inv
        qd = diagonal(q_ref[rows, :])

        def step(j, dq):
            lanes = lane_block(j, t)
            k = expand_pair(ka, kb, 0, p, lanes).astype(BF)
            v = expand_pair(ka, kb, 1, p, lanes).T.astype(BF)
            pb = p_ref[p, lanes, :]
            ds = (pb.astype(F32) * (nn(v, dn) + dtot)).astype(BF)
            dq = dq + nn(k, ds)
            factor_back(nt(qd, ds) * (DH**-0.5), 0, p, lanes)
            factor_back(nt(dn, pb), 1, p, lanes)
            return dq

        dq = undiagonal(blocks(nblk, step, jnp.zeros((2 * DH, 2 * t), F32)))
        dq = dq * (DH**-0.5 / RQ)
        for hh in range(2):
            d = dq[hh * DH : (hh + 1) * DH]
            for r in range(RQ):
                row = r * H + 2 * p + hh
                dqa[row] = jnp.sum(d * b_ref[r * DH : (r + 1) * DH, :], axis=0, keepdims=True)
                db[r * DH : (r + 1) * DH, :] += d * a_ref[row]
        return _

    lax.fori_loop(0, H // 2, pair, 0)
    for i in range(AQ):
        dq_ref[i : i + 1, :] = dqa[i]
    for side in range(2):
        for i in range(AK):
            dkv_ref[side * KEY_ROWS + i : side * KEY_ROWS + i + 1, :] = dka[side * AK + i]
    dq_ref[AQ : AQ + BQ, :] = rope_back(db[...], cos_ref[...], sin_ref[...], RQ)


def vmem(n):
    return [pl.BlockSpec(memory_space=pltpu.VMEM)] * n


SMEM = pl.BlockSpec(memory_space=pltpu.SMEM)


def silu_parts(gate):
    s = jax.nn.sigmoid(gate)
    return s, gate * s


def body(
    tokens,
    doc_lengths,
    first_gain,
    factor_weights,
    output_weights,
    second_gain,
    gate_weights,
    up_weights,
    down_weights,
    cotangent,
):
    _, t, width = tokens.shape
    n_ctx, n_dp = lax.axis_size("ctx"), lax.axis_size("dp")
    n_all = n_ctx * n_dp
    both = ("dp", "ctx")
    length = t * n_ctx
    nblk = min(n_ctx, -(-(length // 2 - 1) // t) + 1)
    ff = gate_weights.shape[1]
    ffq = ff // n_dp
    rows = width // n_all
    c = lax.axis_index("ctx")

    pack = jnp.concatenate(
        [factor_weights, first_gain[:, None], second_gain[:, None],
         jnp.zeros((rows, FPAD - FDIM - 2), F32)], axis=1).astype(BF)
    fac = lax.all_gather(pack, both, axis=0, tiled=True)
    wo = lax.all_gather(output_weights.astype(BF), both, axis=0, tiled=True)
    gu = jnp.stack([gate_weights, up_weights]).astype(BF).reshape(2, rows, n_dp, ffq)
    gu = lax.all_to_all(gu.transpose(2, 0, 1, 3), "dp", 0, 0, tiled=False)
    gu = lax.all_gather(gu, "ctx", axis=2, tiled=False)
    gu = gu.transpose(1, 0, 2, 3, 4).reshape(2, width, ffq)
    wg, wu = gu[0], gu[1]
    wd = lax.all_gather(down_weights.astype(BF), "ctx", axis=0, tiled=True)
    g1 = fac[:, FDIM].reshape(1, width).astype(F32)
    g2 = fac[:, FDIM + 1].reshape(1, width).astype(F32)

    half = DH // 2
    freq = 10000.0 ** (-(np.arange(half) * 2.0 / DH))
    pos = (c * t + jnp.arange(t, dtype=jnp.int32)).astype(F32)
    angles = jnp.asarray(freq, F32)[:, None] * pos[None, :]
    cosine, sine = jnp.cos(angles), jnp.sin(angles)

    x16 = tokens.reshape(t, width)
    normed_t, q_t, packet, a_t, b_t = pl.pallas_call(
        pre_kernel,
        out_shape=(
            jax.ShapeDtypeStruct((width, t), BF),
            jax.ShapeDtypeStruct((H * DH, t), BF),
            jax.ShapeDtypeStruct((PACK, t), BF),
            jax.ShapeDtypeStruct((AQ, 1, t), F32),
            jax.ShapeDtypeStruct((BQ, t), F32),
        ),
        in_specs=vmem(5),
        out_specs=tuple(vmem(5)),
        name="pre",
    )(x16, g1, fac, cosine, sine)

    whole = lax.all_gather(packet, "ctx", axis=1, tiled=True)
    base = jnp.maximum(c - nblk + 1, 0) * t
    kv = lax.dynamic_slice_in_dim(whole, base, nblk * t, 1)
    attn_t, attn_f, inv, probs = pl.pallas_call(
        functools.partial(attend_kernel, nblk),
        out_shape=(
            jax.ShapeDtypeStruct((H * DH, t), BF),
            jax.ShapeDtypeStruct((H * DH, t), F32),
            jax.ShapeDtypeStruct((H // 2, 8, 2 * t), F32),
            jax.ShapeDtypeStruct((H // 2, nblk * t, 2 * t), BF),
        ),
        in_specs=[SMEM, SMEM] + vmem(2),
        out_specs=tuple(vmem(4)),
        scratch_shapes=[
            pltpu.VMEM((2 * AK, 1, nblk * t), F32),
            pltpu.VMEM((2 * BK, nblk * t), F32),
            pltpu.VMEM((nblk * t, t), F32),
        ],
        name="attend",
    )(base[None], doc_lengths, q_t, kv)

    x = x16.astype(F32)
    middle = x + nn(attn_t.T, wo)
    r2 = lax.rsqrt(jnp.mean(middle * middle, axis=-1, keepdims=True) + EPS)
    nm = (middle * r2 * g2).astype(BF)
    cot_own = cotangent.reshape(t, width)
    cot = lax.all_gather(cot_own, "dp", axis=0, tiled=True)
    nm_all = lax.all_gather(nm, "dp", axis=0, tiled=True)
    gate = nn(nm_all, wg)
    upward = nn(nm_all, wu)
    sig, act = silu_parts(gate)
    hidden = (act * upward).astype(BF)
    d_hidden = nt(cot, wd)
    d_gate = (d_hidden * upward * sig * (1.0 + gate * (1.0 - sig))).astype(BF)
    d_up = (d_hidden * act).astype(BF)
    dn_part = nt(d_gate, wg) + nt(d_up, wu)
    d_norm_mid = lax.psum_scatter(dn_part.astype(BF), "dp", scatter_dimension=0, tiled=True).astype(F32)
    out_part = nn(hidden, wd)
    out_sum = lax.psum_scatter(out_part.astype(BF), "dp", scatter_dimension=0, tiled=True)
    layer_output = (middle + out_sum.astype(F32)).astype(BF)

    def tn(a, b):
        return lax.dot_general(a, b, (((0,), (0,)), ((), ())), preferred_element_type=F32)

    gu_part = jnp.stack([tn(nm_all, d_gate), tn(nm_all, d_up)]).astype(BF)
    gu_part = gu_part.reshape(2, n_dp, n_ctx, rows, ffq).transpose(2, 1, 0, 3, 4)
    gu_part = gu_part.reshape(n_ctx * n_dp * 2 * rows, ffq)
    gu_own = lax.psum_scatter(gu_part, "ctx", scatter_dimension=0, tiled=True)
    gu_own = gu_own.reshape(n_dp, 2, rows, ffq)
    gu_own = lax.all_to_all(gu_own, "dp", 0, 0, tiled=False)
    gu_own = gu_own.astype(F32).transpose(1, 2, 0, 3).reshape(2, rows, ff)
    down_sum = lax.psum_scatter(
        tn(hidden, cot).astype(BF), "ctx", scatter_dimension=0, tiled=True
    ).astype(F32)

    second_part = jnp.sum(d_norm_mid * middle * r2, axis=0)
    u2 = d_norm_mid * g2
    d_middle = (
        cot_own.astype(F32)
        + r2 * u2
        - middle * (r2**3 * jnp.mean(u2 * middle, axis=-1, keepdims=True))
    )
    d_branch = d_middle.astype(BF)
    d_attn_t = nt(wo, d_branch)
    out_grad_part = nn(attn_t, d_branch)

    dq_rows, dkv = pl.pallas_call(
        functools.partial(attend_back_kernel, nblk),
        out_shape=(
            jax.ShapeDtypeStruct((AQ + BQ, t), F32),
            jax.ShapeDtypeStruct((PACK, nblk * t), F32),
        ),
        in_specs=vmem(10),
        out_specs=tuple(vmem(2)),
        scratch_shapes=[
            pltpu.VMEM((2 * AK, 1, nblk * t), F32),
            pltpu.VMEM((2 * BK, nblk * t), F32),
            pltpu.VMEM((2 * AK, 1, nblk * t), F32),
            pltpu.VMEM((AQ, 1, t), F32),
            pltpu.VMEM((BQ, t), F32),
        ],
        name="attend_back",
    )(d_attn_t, attn_f, inv, probs, q_t, kv, a_t, b_t, cosine, sine)

    spread = lax.dynamic_update_slice_in_dim(
        jnp.zeros((PACK, length), BF), dkv.astype(BF), base, 1
    )
    d_packet = lax.psum_scatter(spread, "ctx", scatter_dimension=1, tiled=True).astype(F32)
    d_bk = rope_back(d_packet[AK : AK + BK], cosine, sine, RKV)
    d_fac_t = jnp.concatenate([dq_rows, d_packet[:AK], d_bk, d_packet[KEY_ROWS:]], axis=0).astype(BF)
    d_fac = d_fac_t.T
    d_norm_in = nt(d_fac, fac[:, :FDIM])
    r1 = lax.rsqrt(jnp.mean(x * x, axis=-1, keepdims=True) + EPS)
    first_part = jnp.sum(d_norm_in * x * r1, axis=0)
    u1 = d_norm_in * g1
    input_grad = (
        d_middle + r1 * u1 - x * (r1**3 * jnp.mean(u1 * x, axis=-1, keepdims=True))
    ).astype(BF)
    fac_part = nt(normed_t, d_fac_t)
    out_own = lax.psum_scatter(out_grad_part.astype(BF), both, scatter_dimension=0, tiled=True)
    last = jnp.concatenate(
        [fac_part, first_part[:, None], second_part[:, None],
         jnp.zeros((width, FPAD - FDIM - 2), F32)], axis=1).astype(BF)
    last_own = lax.psum_scatter(last, both, scatter_dimension=0, tiled=True).astype(F32)
    return (
        layer_output.reshape(1, t, width),
        input_grad.reshape(1, t, width),
        last_own[:, FDIM],
        last_own[:, :FDIM],
        out_own.astype(F32),
        last_own[:, FDIM + 1],
        gu_own[0],
        gu_own[1],
        down_sum,
    )


def solution(mesh):
    return jax.shard_map(
        body,
        mesh=mesh,
        in_specs=(
            P("dp", "ctx", None),
            P("dp", None),
            P(("dp", "ctx")),
            P(("dp", "ctx"), None),
            P(("dp", "ctx"), None),
            P(("dp", "ctx")),
            P(("dp", "ctx"), None),
            P(("dp", "ctx"), None),
            P(("dp", "ctx"), None),
            P("dp", "ctx", None),
        ),
        out_specs=(
            P("dp", "ctx", None),
            P("dp", "ctx", None),
            P(("dp", "ctx")),
            P(("dp", "ctx"), None),
            P(("dp", "ctx"), None),
            P(("dp", "ctx")),
            P(("dp", "ctx"), None),
            P(("dp", "ctx"), None),
            P(("dp", "ctx"), None),
        ),
        check_vma=False,
    )
```

time: 989 us -> 848 us (0.86)
  matrix products: 152 us -> 33.5 us
  local copies, waits for them, and re-layouts: 91.8 us -> 22.8 us
  waiting for transfers between devices: 616 us -> 685 us
  blocking collectives: 71.8 us -> 40.6 us
  Pallas kernels: 0 us -> 24.9 us
  loops' own time: 15.7 us -> 0 us
    unnamed x8 -> x15, waiting for transfers between devices: 0.13 us -> 180 us
    dot_general x48 -> x14, matrix products: 152 us -> 33.5 us  [the longest x5 13.9 us: nn(): return jnp.dot(a, b, preferred_element_type=F32)]
    reduce_scatter x3 -> x5, waiting for transfers between devices: 414 us -> 310 us  [the longest x1 127 us: body(): lax.psum_scatter(out_grad_part.astype(BF), both, scatter_dimension=0, til...]
    unnamed x1 -> x0, blocking collectives: 42.2 us -> none
    concatenate x1 -> x2, local copies, waits for them, and re-layouts: 34.1 us -> 0.09 us  [the longest x1 0.08 us: body(): jnp.concatenate([factor_weights, first_gain[:, None], second_gain[:, None...]
    pallas_call x0 -> x3, Pallas kernels: none -> 24.9 us  [the longest x1 14.2 us: body(): pl.pallas_call(functools.partial(attend_back_kernel, nblk), out_shape=(ja...]
    another operation x24 -> x4, local copies, waits for them, and re-layouts: 23.1 us -> 4.79 us
    another operation x2 -> x0, loops' own time: 15.7 us -> none  [the longest x1 14.2 us: body(): lax.fori_loop(0, length // block_len, back_step, start_back)]
  transfers between devices with their start and end apart: 8 -> 14, of which waited for: 7 -> 14; matrix products, arithmetic and copies ran while one was open for 14% -> 7% of each run, Pallas kernels for 0% -> 1%
where the time goes in v1:
time: 848 us; the launch traced here: 847 us
  waiting for transfers between devices  685 us (81%)
  blocking collectives  40.6 us (5%)
  matrix products  33.5 us (4%)
  Pallas kernels  24.9 us (3%)
  local copies, waits for them, and re-layouts  22.8 us (3%)
  other arithmetic  21.7 us (3%)
  between operations  14.3 us (2%)
    unnamed x15, waiting for transfers between devices  180 us
    reduce_scatter x1, waiting for transfers between devices, body(): lax.psum_scatter(out_grad_part.astype(BF), both, scatter_dimension=0, til...  127 us
    reduce_scatter x1, waiting for transfers between devices, body(): gu_own = lax.psum_scatter(gu_part, 'ctx', scatter_dimension=0, tiled=True)  75 us
    reduce_scatter x1, waiting for transfers between devices, body(): lax.psum_scatter(tn(hidden, cot).astype(BF), 'ctx', scatter_dimension=0,...  61.8 us
    all_gather x1, waiting for transfers between devices, body(): gu = lax.all_gather(gu, 'ctx', axis=2, tiled=False)  56.5 us
    all_gather x1, waiting for transfers between devices, body(): wd = lax.all_gather(down_weights.astype(BF), 'ctx', axis=0, tiled=True)  45.4 us
    all_gather x1, waiting for transfers between devices, body(): fac = lax.all_gather(pack, both, axis=0, tiled=True)  43.6 us
    all_gather x1, blocking collectives, body(): whole = lax.all_gather(packet, 'ctx', axis=1, tiled=True)  29 us
  transfers between devices with their start and end apart: 14, of which 14 were waited for; matrix products, arithmetic and copies ran while one was open for 7% of the time, Pallas kernels for 1%

profile of v1, /device:TPU:0, one launch (start us, length us, event | category | flops | bytes accessed | tf_op | source)
XLA Modules:
  0.0 847.4 jit_solution(16612492514663938870)
XLA Ops:
  14.1 11.6 %all_to_all.10 = bf16[4,2,32,704]{3,2,1,0:T(8,128)(2,1)} all-to-all(bf16[4,2,32,704]{3,2,1,0:T(8,128)(2,1)S(1)} %copy.54), channel_id=1, replica_groups=mesh['dp'=4,'ctx'=8] {'dp'}, dimensions={0} | all-to-all | bytes 720896 | tf_op jit(solution)/shard_map/all_to_all | solution.py:273
  26.5 43.6 %all-gather.9.cloned.1.call-done.w_ref = bf16[1024,896]{1,0:T(8,128)(2,1)} async-done(((bf16[32,896]{1,0:T(8,128)(2,1)}), bf16[1024,896]{1,0:T(8,128)(2,1)}) %all-gather.9.cloned.1.call-update) | async-done | bytes 1835024 | tf_op jit(solution)/shard_map/all_gather | solution.py:270
  70.2 2.1 convert_reduce_fusion
  72.2 3.2 pre.1
  75.5 29.0 %all_gather.25 = bf16[320,1024]{1,0:T(8,128)(2,1)S(1)} all-gather(bf16[320,128]{1,0:T(8,128)(2,1)} %get-tuple-element.21), channel_id=1, replica_groups=mesh['dp'=4,'ctx'=8] {'ctx'}, dimensions={1}, use_global_device_ids=true | all-gather | bytes 737280 | tf_op jit(solution)/shard_map/all_gather | solution.py:302
  105.3 7.5 attend.1
  112.8 17.8 %all-gather.11.cloned.1.call-done = bf16[1024,1024]{1,0:T(8,128)(2,1)} async-done(((bf16[32,1024]{1,0:T(8,128)(2,1)}), bf16[1024,1024]{1,0:T(8,128)(2,1)}) %all-gather.11.cloned.1.call-update) | async-done | bytes 2097168 | tf_op jit(solution)/shard_map/all_gather | solution.py:271
  130.6 2.3 multiply_reduce_fusion
  135.1 56.5 %all-gather.17.cloned.1.call-done = bf16[4,2,256,704]{3,2,1,0:T(8,128)(2,1)} async-done(((bf16[4,2,32,704]{3,2,1,0:T(8,128)(2,1)}), bf16[4,2,256,704]{3,2,1,0:T(8,128)(2,1)}) %all-gather.17.cloned.1.call-update) | async-done | bytes 2883600 | tf_op jit(solution)/shard_map/all_gather | solution.py:274
  191.7 2.1 copy.69
  195.3 13.8 %all-gather.13.cloned.1.call-done = bf16[512,1024]{1,0:T(8,128)(2,1)} async-done(((bf16[128,1024]{1,0:T(8,128)(2,1)}), bf16[512,1024]{1,0:T(8,128)(2,1)}) %all-gather.13.cloned.1.call-update) | async-done | bytes 1048592 | tf_op jit(solution)/shard_map/all_gather | solution.py:329
  209.1 3.9 fusion.39
  212.9 2.1 fusion.40
  215.1 12.2 %all-gather.19.cloned.1.call-done = bf16[1,512,1024]{2,1,0:T(8,128)(2,1)} async-done(((bf16[1,128,1024]{2,1,0:T(8,128)(2,1)}), bf16[1,512,1024]{2,1,0:T(8,128)(2,1)}) %all-gather.19.cloned.1.call-update) | async-done | bytes 1048592 | tf_op jit(solution)/shard_map/all_gather | solution.py:328
  227.2 45.4 %all-gather.15.cloned.1.call-done = bf16[704,1024]{1,0:T(8,128)(2,1)} async-done(((bf16[88,1024]{1,0:T(8,128)(2,1)}), bf16[704,1024]{1,0:T(8,128)(2,1)}) %all-gather.15.cloned.1.call-update) | async-done | bytes 1441808 | tf_op jit(solution)/shard_map/all_gather | solution.py:277
  272.6 5.0 multiply_convert_fusion
  280.8 3.6 convolution_convert_fusion.5
  284.7 19.7 %reduce-scatter.14.cloned.1.call-done = bf16[128,1024]{1,0:T(8,128)(2,1)} async-done(((bf16[512,1024]{1,0:T(8,128)(2,1)}), bf16[128,1024]{1,0:T(8,128)(2,1)}) %reduce-scatter.14.cloned.1.call-update) | async-done | bytes 262160 | tf_op jit(solution)/shard_map/reduce_scatter | solution.py:338
  305.5 26.2 %reduce-scatter.12.cloned.1.call-done = bf16[128,1024]{1,0:T(8,128)(2,1)} async-done(((bf16[512,1024]{1,0:T(8,128)(2,1)}), bf16[128,1024]{1,0:T(8,128)(2,1)}) %reduce-scatter.12.cloned.1.call-update) | async-done | bytes 262160 | tf_op jit(solution)/shard_map/reduce_scatter | solution.py:340
  335.4 14.2 %attend_back.1 = (f32[480,128]{1,0:T(8,128)}, f32[320,640]{1,0:T(8,128)}) custom-call(f32[1024,128]{1,0:T(8,128)} %convolution_bitcast_fusion.da_ref, f32[1024,128]{1,0:T(8,128)} %get-tuple-element.23.af_ref, f32[8,8,256]{2,1,0:T(8,128)} %get-tuple-element.24.inv_ref, bf16[8,640,256]{2,1,0:T(8,128)(2,1)} %get-tuple-element.25.p_ref, ...), custom_call_target="tpu_custom_call" | custom-call | tf_op jit(solution)/shard_map/attend_back/pallas_call | solution.py:368
  352.2 3.4 convolution_convert_fusion.4
  359.4 3.1 convolution_convert_fusion.3
  362.5 2.6 copy.57
  369.7 2.1 convolution_convert_fusion
  372.7 42.7 %reduce-scatter.22.cloned.1.call-done = bf16[128,320]{1,0:T(8,128)(2,1)} async-done(((bf16[1024,320]{1,0:T(8,128)(2,1)}), bf16[128,320]{1,0:T(8,128)(2,1)}) %reduce-scatter.22.cloned.1.call-update) | async-done | bytes 81936
  419.0 2.5 copy.66
  421.5 61.8 %reduce-scatter.20.cloned.1.call-done = bf16[88,1024]{1,0:T(8,128)(2,1)} async-done(((bf16[704,1024]{1,0:T(8,128)(2,1)}), bf16[88,1024]{1,0:T(8,128)(2,1)}) %reduce-scatter.20.cloned.1.call-update) | async-done | bytes 180240 | tf_op jit(solution)/shard_map/reduce_scatter | solution.py:353
  485.1 75.0 %reduce-scatter.18.cloned.1.call-done = bf16[256,704]{1,0:T(8,128)(2,1)} async-done(((bf16[2048,704]{1,0:T(8,128)(2,1)}), bf16[256,704]{1,0:T(8,128)(2,1)}) %reduce-scatter.18.cloned.1.call-update) | async-done | bytes 360464 | tf_op jit(solution)/shard_map/reduce_scatter | solution.py:349
  560.1 3.5 all-to-all-start.1
  564.5 6.5 all-to-all-done.1
  573.6 127.1 %reduce-scatter.16.cloned.1.call-done = bf16[32,1024]{1,0:T(8,128)(2,1)} async-done(((bf16[1024,1024]{1,0:T(8,128)(2,1)}), bf16[32,1024]{1,0:T(8,128)(2,1)}) %reduce-scatter.16.cloned.1.call-update) | async-done | bytes 65552 | tf_op jit(solution)/shard_map/reduce_scatter | solution.py:401
  702.2 136.3 %reduce-scatter.24.cloned.1.call-done = bf16[32,896]{1,0:T(8,128)(2,1)} async-done(((bf16[1024,896]{1,0:T(8,128)(2,1)}), bf16[32,896]{1,0:T(8,128)(2,1)}) %reduce-scatter.24.cloned.1.call-update) | async-done | bytes 57360
  (126 shorter events, 44.8 us)
Async XLA Ops:
  7.2 6.3 copy-start.5
  7.2 63.0 %all-gather.9.cloned.1.call-start = ((), (), s32[]{:S(2)}) async-start(), calls=%async_computation.9 | async-start | bytes 1892352 | tf_op jit(solution)/shard_map/all_gather | solution.py:270
  10.5 120.1 %all-gather.11.cloned.1.call-start = ((), (), s32[]{:S(2)}) async-start(), calls=%async_computation.10 | async-start | bytes 2162688 | tf_op jit(solution)/shard_map/all_gather | solution.py:271
  12.1 179.6 %all-gather.17.cloned.1.call-start = ((), (), s32[]{:S(2)}) async-start(), calls=%async_computation.18 | async-start | bytes 3538944 | tf_op jit(solution)/shard_map/all_gather | solution.py:274
  13.5 12.3 %copy-start.10 = (f32[32]{0:T(128)S(1)}, f32[32]{0:T(128)}, u32[]{:S(2)}) copy-start(f32[32]{0:T(128)} %constant.34.clone) | copy-start | bytes 388
  25.7 183.3 %all-gather.13.cloned.1.call-start = ((), (), s32[]{:S(2)}) async-start(), calls=%async_computation.11 | async-start | bytes 1310720 | tf_op jit(solution)/shard_map/all_gather | solution.py:329
  75.5 55.1 %copy-start.1 = (bf16[1,128,1024]{2,1,0:T(8,128)(2,1)S(1)}, bf16[1,128,1024]{2,1,0:T(8,128)(2,1)}, u32[]{:S(2)}) copy-start(bf16[1,128,1024]{2,1,0:T(8,128)(2,1)} %param.11) | copy-start | bytes 786436
  130.6 3.8 copy-start.6
  133.7 93.5 %all-gather.19.cloned.1.call-start = ((), (), s32[]{:S(2)}) async-start(), calls=%async_computation.19 | async-start | bytes 1310720 | tf_op jit(solution)/shard_map/all_gather | solution.py:328
  134.3 138.3 %all-gather.15.cloned.1.call-start = ((), (), s32[]{:S(2)}) async-start(), calls=%async_computation.12 | async-start | bytes 1622016 | tf_op jit(solution)/shard_map/all_gather | solution.py:277
  135.1 169.3 %reduce-scatter.14.cloned.1.call-start = ((), (), s32[]{:S(2)}) async-start(), calls=%async_computation.14 | async-start | bytes 1310720 | tf_op jit(solution)/shard_map/reduce_scatter | solution.py:338
  209.1 3.9 copy-start.11
  272.6 5.0 copy-start.3
  277.6 1.1 copy-start.15
  277.6 1.1 copy-start.13
  280.8 51.0 %reduce-scatter.12.cloned.1.call-start = ((), (), s32[]{:S(2)}) async-start(), calls=%async_computation.13 | async-start | bytes 1310720 | tf_op jit(solution)/shard_map/reduce_scatter | solution.py:340
  284.5 49.4 %copy-start = (bf16[1024,1024]{1,0:T(8,128)(2,1)S(1)}, bf16[1024,1024]{1,0:T(8,128)(2,1)}, u32[]{:S(2)}) copy-start(bf16[1024,1024]{1,0:T(8,128)(2,1)} %all-gather.11.cloned.1.call-done) | copy-start | bytes 6291460
  284.5 130.9 %reduce-scatter.22.cloned.1.call-start = ((), (), s32[]{:S(2)}) async-start(), calls=%async_computation.20 | async-start | bytes 884736
  349.6 2.6 copy-start.16
  352.1 3.5 copy-start.12
  352.1 3.5 copy-start.14
  352.1 131.3 %reduce-scatter.20.cloned.1.call-start = ((), (), s32[]{:S(2)}) async-start(), calls=%async_computation.17 | async-start | bytes 1622016 | tf_op jit(solution)/shard_map/reduce_scatter | solution.py:353
  355.6 204.5 %reduce-scatter.18.cloned.1.call-start = ((), (), s32[]{:S(2)}) async-start(), calls=%async_computation.16 | async-start | bytes 3538944 | tf_op jit(solution)/shard_map/reduce_scatter | solution.py:349
  368.7 1.0 copy-start.4
  368.8 331.9 %reduce-scatter.16.cloned.1.call-start = ((), (), s32[]{:S(2)}) async-start(), calls=%async_computation.15 | async-start | bytes 2162688 | tf_op jit(solution)/shard_map/reduce_scatter | solution.py:401
  371.8 0.9 copy-start.8
  371.8 45.3 %copy-start.2 = (bf16[1024,896]{1,0:T(8,128)(2,1)S(1)}, bf16[1024,896]{1,0:T(8,128)(2,1)}, u32[]{:S(2)}) copy-start(bf16[1024,896]{1,0:T(8,128)(2,1)} %all-gather.9.cloned.1.call-done.w_ref) | copy-start | bytes 5505028
  371.8 45.3 %copy-start.9 = (f32[1024]{0:T(1024)S(1)}, f32[1024]{0:T(1024)}, u32[]{:S(2)}) copy-start(f32[1024]{0:T(1024)} %get-tuple-element.77) | copy-start | bytes 12292
  371.8 466.7 %reduce-scatter.24.cloned.1.call-start = ((), (), s32[]{:S(2)}) async-start(), calls=%async_computation.21 | async-start | bytes 1892352
  417.1 1.0 copy-start.7
  560.1 10.8 %all-to-all-start.1 = ((bf16[4,2,32,704]{3,2,1,0:T(8,128)(2,1)}), bf16[4,2,32,704]{3,2,1,0:T(8,128)(2,1)S(1)}, u32[]{:S(2)}, u32[]{:S(2)}) async-start(bf16[4,2,32,704]{3,2,1,0:T(8,128)(2,1)} %bitcast.85), calls=%async_computation.5 | async-start | bytes 786432 | tf_op jit(solution)/shard_map/all_to_all | solution.py:351
Sparse Core Ops, SparseCore 0:
  11.5 58.6 all-gather.8
  73.7 56.8 all-gather.10
  132.8 58.8 all-gather.16
  193.7 15.3 all-gather.12
  210.5 16.6 all-gather.18
  229.8 42.7 all-gather.14
  280.9 23.4 reduce-scatter.13
  306.9 24.8 reduce-scatter.11
  352.2 63.1 reduce-scatter.21
  418.6 64.6 reduce-scatter.19
  487.0 73.0 reduce-scatter.17
  562.2 138.4 reduce-scatter.15
  702.9 135.4 reduce-scatter.23

commit v2 on v1

--- a/solution.py
+++ b/solution.py
@@ -34,6 +34,179 @@
 def nn(a, b):
     return jnp.dot(a, b, preferred_element_type=F32)
 
+MESH = pl.DeviceIdType.MESH
+
+
+def ring_place(c, n):
+    z = c // 2
+    return z + (c % 2) * (n - 1 - 2 * z)
+
+
+def ring_index(p, n):
+    p = (p + 2 * n) % n
+    q = p // (n // 2)
+    return (1 - q) * (2 * p) + q * (2 * (n - 1 - p) + 1)
+
+
+def remote(src, dst, send, recv, dev):
+    return pltpu.make_async_remote_copy(
+        src_ref=src, dst_ref=dst, send_sem=send, recv_sem=recv, device_id=dev, device_id_type=MESH
+    )
+
+
+def places():
+    d, c = lax.axis_index("dp"), lax.axis_index("ctx")
+    core = d % 2
+    return d, c, core, d + 1 - 2 * core, (d + 2) % 4
+
+
+def meet(n, near):
+    d, c, _, _, _ = places()
+    barrier = pltpu.get_barrier_semaphore()
+    count = 0
+    n_dp = lax.axis_size("dp")
+    for k in range(1, n_dp):
+        pl.semaphore_signal(barrier, inc=1, device_id=((d + k) % n_dp, c), device_id_type=MESH)
+        count += 1
+    if near:
+        r = ring_place(c, n)
+        for way in (1, -1):
+            pl.semaphore_signal(
+                barrier, inc=1, device_id=(d, ring_index(r + way, n)), device_id_type=MESH
+            )
+            count += 1
+    else:
+        for k in range(1, n):
+            pl.semaphore_signal(barrier, inc=1, device_id=(d, (c + k) % n), device_id_type=MESH)
+            count += 1
+    pl.semaphore_wait(barrier, count)
+
+
+def steps(lo, hi, step):
+    if isinstance(lo, int) and isinstance(hi, int) and hi - lo <= 4:
+        for s in range(lo, hi):
+            step(s)
+    elif not (isinstance(lo, int) and isinstance(hi, int) and hi <= lo):
+        lax.fori_loop(lo, hi, lambda s, _: (step(s), _)[1], 0)
+
+
+class GatherRing:
+    def __init__(self, n, slot, half, send, recv):
+        self.n, self.h, self.slot, self.half, self.send, self.recv = n, n // 2, slot, half, send, recv
+        self.d, c, _, _, _ = places()
+        self.r = ring_place(c, n)
+
+    def copy(self, s, i, arriving=False):
+        way = 1 - 2 * i
+        last = isinstance(s, int) and s == self.h - 1
+        owner = ring_index(self.r - way * (s + (1 if arriving else 0)), self.n)
+        ref = self.half(owner, i) if last else self.slot(owner)
+        to = (self.d, ring_index(self.r + way, self.n))
+        return remote(ref, ref, self.send.at[i, s], self.recv.at[i, s], to)
+
+    def start(self, s):
+        for i in range(2):
+            self.copy(s, i).start()
+
+    def arrive(self, s):
+        for i in range(2):
+            self.copy(s, i, True).wait_recv()
+
+    def step(self, s):
+        for i in range(2):
+            self.copy(s - 1, i, True).wait_recv()
+            self.copy(s, i).start()
+
+    def last(self):
+        self.step(self.h - 1)
+
+    def drain(self):
+        steps(0, self.h - 1, lambda s: [self.copy(s, i).wait_send() for i in range(2)])
+        for i in range(2):
+            self.copy(self.h - 1, i).wait_send()
+
+
+class ScatterRing:
+    def __init__(self, n, part, half, land, whole_of, half_of, send, recv):
+        self.n, self.h, self.part, self.half = n, n // 2, part, half
+        self.land, self.whole_of, self.half_of = land, whole_of, half_of
+        self.send, self.recv = send, recv
+        self.d, c, _, _, _ = places()
+        self.c, self.r = c, ring_place(c, n)
+
+    def copy(self, s, i):
+        way = 1 - 2 * i
+        to = (self.d, ring_index(self.r + way, self.n))
+        first = isinstance(s, int) and s == 0
+        if first:
+            owner = ring_index(self.r + way * self.h, self.n)
+            src, dst = self.half(owner, i), self.half_of(self.land.at[i, 0], i)
+        else:
+            src, dst = self.land.at[i, s - 1], self.land.at[i, s]
+        return remote(src, dst, self.send.at[i, s], self.recv.at[i, s], to)
+
+    def start(self):
+        for i in range(2):
+            self.copy(0, i).start()
+
+    def step(self, s):
+        first = isinstance(s, int) and s == 1
+        for i in range(2):
+            way = 1 - 2 * i
+            self.copy(s - 1, i).wait_recv()
+            owner = ring_index(self.r + way * (self.h - s), self.n)
+            held = self.land.at[i, s - 1]
+            if first:
+                mine = self.half_of(held, i)
+                mine[...] = (mine[...].astype(F32) + self.half(owner, i)[...].astype(F32)).astype(BF)
+                self.half_of(held, 1 - i)[...] = self.half(owner, 1 - i)[...]
+            else:
+                held[...] = (held[...].astype(F32) + self.part(owner)[...].astype(F32)).astype(BF)
+            self.copy(s, i).start()
+
+    def rest(self, lo, hi):
+        if lo == 1 and hi > 1:
+            self.step(1)
+            lo = 2
+        steps(lo, hi, self.step)
+
+    def result(self):
+        for i in range(2):
+            self.copy(self.h - 1, i).wait_recv()
+        out = self.part(self.c)[...].astype(F32)
+        for i in range(2):
+            out = out + self.land[i, self.h - 1].astype(F32)
+        return out
+
+    def drain(self):
+        for i in range(2):
+            self.copy(0, i).wait_send()
+        steps(1, self.h, lambda s: [self.copy(s, i).wait_send() for i in range(2)])
+
+
+class Spread:
+    def __init__(self, ref, send, recv):
+        d, c, _, cd, xd = places()
+        self.copies = [
+            remote(ref.at[d], ref.at[d], send.at[0], recv.at[0], (cd, c)),
+            remote(ref.at[d], ref.at[d], send.at[1], recv.at[1], (xd, c)),
+            remote(ref.at[xd], ref.at[xd], send.at[2], recv.at[2], (cd, c)),
+        ]
+
+    def start(self):
+        self.copies[1].start()
+        self.copies[0].start()
+
+    def forward(self):
+        self.copies[1].wait_recv()
+        self.copies[2].start()
+
+    def finish(self):
+        self.copies[0].wait_recv()
+        self.copies[2].wait_recv()
+        for copy in self.copies:
+            copy.wait_send()
+
 
 def blocks(count, step, state):
     if count <= 8:
@@ -63,13 +236,11 @@
     return rope(v, cosine, -sine, ranks)
 
 
-def pre_kernel(x_ref, g_ref, w_ref, cos_ref, sin_ref, nt_ref, q_ref, p_ref, a_ref, b_ref):
-    x = x_ref[...].astype(F32)
+def pre_part(x, g1, w, cosine, sine, nt_ref, q_ref, p_ref, a_ref, b_ref):
     r1 = lax.rsqrt(jnp.mean(x * x, axis=-1, keepdims=True) + EPS)
-    n = (x * r1 * g_ref[...]).astype(BF)
+    n = (x * r1 * g1).astype(BF)
     nt_ref[...] = n.T
-    ft = nn(n, w_ref[...]).T
-    cosine, sine = cos_ref[...], sin_ref[...]
+    ft = nn(n, w).T
     a = ft[:AQ]
     b = rope(ft[AQ : AQ + BQ], cosine, sine, RQ)
     for i in range(AQ):
@@ -120,7 +291,7 @@
     return jnp.concatenate([wide[:DH, :t], wide[DH:, t:]], axis=0)
 
 
-def attend_kernel(nblk, base_ref, len_ref, q_ref, kv_ref, at_ref, af_ref, inv_ref, p_ref, ka, kb, bias):
+def attend_part(nblk, len_ref, q_ref, kv_ref, at_ref, af_ref, inv_ref, p_ref, ka, kb, bias):
     t = q_ref.shape[1]
     c = lax.axis_index("ctx")
     tpos = c * t + lax.broadcasted_iota(jnp.int32, (1, t), 1)
@@ -132,7 +303,7 @@
     unpack(kv_ref, ka, kb)
 
     def bias_block(j, _):
-        spos = base_ref[0] + j * t + lax.broadcasted_iota(jnp.int32, (t, t), 0)
+        spos = (c - nblk + 1 + j) * t + lax.broadcasted_iota(jnp.int32, (t, t), 0)
         ok = (spos >= start) & (spos <= tpos)
         bias[lane_block(j, t), :] = jnp.where(ok, 0.0, NEG)
         return _
@@ -169,8 +340,8 @@
     lax.fori_loop(0, H // 2, pair, 0)
 
 
-def attend_back_kernel(
-    nblk, da_ref, af_ref, inv_ref, p_ref, q_ref, kv_ref, a_ref, b_ref, cos_ref, sin_ref,
+def attend_back_part(
+    nblk, serve, da_ref, af_ref, inv_ref, p_ref, q_ref, kv_ref, a_ref, b_ref, cos_ref, sin_ref,
     dq_ref, dkv_ref, ka, kb, dka, dqa, db,
 ):
     t = q_ref.shape[1]
@@ -218,6 +389,7 @@
                 row = r * H + 2 * p + hh
                 dqa[row] = jnp.sum(d * b_ref[r * DH : (r + 1) * DH, :], axis=0, keepdims=True)
                 db[r * DH : (r + 1) * DH, :] += d * a_ref[row]
+        serve(p)
         return _
 
     lax.fori_loop(0, H // 2, pair, 0)
@@ -229,11 +401,361 @@
     dq_ref[AQ : AQ + BQ, :] = rope_back(db[...], cos_ref[...], sin_ref[...], RQ)
 
 
+def front_kernel(
+    n, nblk,
+    len_ref, x_ref, cos_ref, sin_ref, fac_in, wo_in, gu_in, wd_in, cot_in,
+    nt_ref, q_ref, a_ref, b_ref, kv_ref, at_ref, af_ref, inv_ref, p_ref,
+    fac, wo, gu, wd, nm, cot, mid_ref,
+    ka, kb, bias,
+    own_sem, near_send, near_recv, ring_send, ring_recv, kv_send, kv_recv, sp_send, sp_recv,
+):
+    d, c, core, cd, xd = places()
+    t = x_ref.shape[0]
+    n_dp = 4
+    locals_ = [
+        pltpu.make_async_copy(fac_in, fac.at[d, c], own_sem.at[0]),
+        pltpu.make_async_copy(wo_in, wo.at[d, c], own_sem.at[1]),
+        pltpu.make_async_copy(gu_in.at[d], gu.at[:, d, c], own_sem.at[2]),
+        pltpu.make_async_copy(wd_in, wd.at[c], own_sem.at[3]),
+        pltpu.make_async_copy(cot_in, cot.at[d], own_sem.at[4]),
+    ]
+    for copy in locals_:
+        copy.start()
+    for k in range(1, nblk):
+        @pl.when(c - k < 0)
+        def _():
+            kv_ref[:, (nblk - 1 - k) * t : (nblk - k) * t] = jnp.zeros((PACK, t), BF)
+    meet(n, False)
+    for copy in locals_:
+        copy.wait()
+
+    def ring(i, slot, half):
+        return GatherRing(n, slot, half, ring_send.at[i], ring_recv.at[i])
+
+    rows = fac_in.shape[0] // 2
+
+    def shard(ref, dd):
+        return (lambda o: ref.at[dd, o]), (lambda o, w: ref.at[dd, o, w * rows : (w + 1) * rows])
+
+    fo, fx = ring(0, *shard(fac, d)), ring(1, *shard(fac, xd))
+    oo, ox = ring(2, *shard(wo, d)), ring(3, *shard(wo, xd))
+    cut = -(-wd_in.shape[0] // 16) * 8
+    gr = ring(4, lambda o: gu.at[:, :, o], lambda o, w: gu.at[w, :, o])
+    dr = ring(
+        5, lambda o: wd.at[o],
+        lambda o, w: wd.at[o, :cut] if w == 0 else wd.at[o, cut:],
+    )
+    fswap = remote(fac.at[d, c], fac.at[d, c], near_send.at[0], near_recv.at[0], (xd, c))
+    oswap = remote(wo.at[d, c], wo.at[d, c], near_send.at[1], near_recv.at[1], (xd, c))
+    fswap.start()
+    fo.start(0)
+    oswap.start()
+    a2a = []
+    for k in range(1, n_dp):
+        to = (d + k) % n_dp
+        a2a.append(
+            (
+                remote(gu_in.at[to], gu.at[:, d, c], near_send.at[1 + k], near_recv.at[1 + k], (to, c)),
+                remote(
+                    gu_in.at[to], gu.at[:, (d + n_dp - k) % n_dp, c],
+                    near_send.at[1 + k], near_recv.at[1 + k], (to, c),
+                ),
+            )
+        )
+        a2a[-1][0].start()
+    cots = Spread(cot, sp_send.at[0], sp_recv.at[0])
+    nms = Spread(nm, sp_send.at[1], sp_recv.at[1])
+    cots.start()
+    fswap.wait_recv()
+    fx.start(0)
+    for s in range(1, n // 2 - 1) if n <= 8 else ():
+        fo.step(s)
+        fx.step(s)
+    if n > 8:
+        steps(1, n // 2 - 1, lambda s: (fo.step(s), fx.step(s)))
+    fo.last()
+    fx.last()
+    oswap.wait_recv()
+    for _, arrival in a2a:
+        arrival.wait_recv()
+    rest = (gr, dr, oo, ox)
+    for one in rest:
+        one.start(0)
+    fo.arrive(n // 2 - 1)
+    fx.arrive(n // 2 - 1)
+    fcore = [
+        (
+            remote(fac.at[dd], fac.at[dd], near_send.at[5 + i], near_recv.at[5 + i], (cd, c)),
+            remote(fac.at[da], fac.at[da], near_send.at[5 + i], near_recv.at[5 + i], (cd, c)),
+        )
+        for i, (dd, da) in enumerate(((d, cd), (xd, (cd + 2) % 4)))
+    ]
+    for out, _ in fcore:
+        out.start()
+    cots.forward()
+    for _, arrival in fcore:
+        arrival.wait_recv()
+
+    width = x_ref.shape[1]
+    x = x_ref[...].astype(F32)
+    w = fac[...].reshape(width, FPAD)
+    gains = w[:, FPAD - 128 :].astype(F32).T
+    g1 = gains[FDIM - (FPAD - 128) : FDIM - (FPAD - 128) + 1]
+    g2 = gains[FDIM - (FPAD - 128) + 1 : FDIM - (FPAD - 128) + 2]
+    own_kv = kv_ref.at[:, (nblk - 1) * t : nblk * t]
+    pre_part(x, g1, w, cos_ref[...], sin_ref[...], nt_ref, q_ref, own_kv, a_ref, b_ref)
+
+    def kv_copy(k):
+        dst = kv_ref.at[:, (nblk - 1 - k) * t : (nblk - k) * t]
+        return remote(own_kv, dst, kv_send.at[k - 1], kv_recv.at[k - 1], (d, (c + k) % n))
+
+    for k in range(1, nblk):
+        @pl.when(c + k < n)
+        def _():
+            kv_copy(k).start()
+
+    full = n // 2 - 1
+    one_third = 1 + (full - 1) // 2
+
+    def advance(lo, hi):
+        steps(lo, hi, lambda s: [one.step(s) for one in rest])
+
+    advance(1, one_third)
+    for k in range(1, nblk):
+        @pl.when(c - k >= 0)
+        def _():
+            kv_copy(k).wait_recv()
+    attend_part(nblk, len_ref, q_ref, kv_ref, at_ref, af_ref, inv_ref, p_ref, ka, kb, bias)
+    advance(one_third, full)
+    for one in rest:
+        one.last()
+    for one in (oo, ox, gr, dr):
+        one.arrive(n // 2 - 1)
+    ocore = [
+        (
+            remote(wo.at[dd], wo.at[dd], near_send.at[7 + i], near_recv.at[7 + i], (cd, c)),
+            remote(wo.at[da], wo.at[da], near_send.at[7 + i], near_recv.at[7 + i], (cd, c)),
+        )
+        for i, (dd, da) in enumerate(((d, cd), (xd, (cd + 2) % 4)))
+    ]
+    for out, _ in ocore:
+        out.start()
+    for _, arrival in ocore:
+        arrival.wait_recv()
+    middle = x + nn(at_ref[...].T, wo[...].reshape(width, width))
+    mid_ref[...] = middle
+    r2 = lax.rsqrt(jnp.mean(middle * middle, axis=-1, keepdims=True) + EPS)
+    nm[d] = (middle * r2 * g2).astype(BF)
+    nms.start()
+    nms.forward()
+    nms.finish()
+    cots.finish()
+    for k in range(1, nblk):
+        @pl.when(c + k < n)
+        def _():
+            kv_copy(k).wait_send()
+    fswap.wait_send()
+    oswap.wait_send()
+    for out, _ in a2a + fcore + ocore:
+        out.wait_send()
+    for one in (fo, fx, oo, ox, gr, dr):
+        one.drain()
+
+
+def mid_kernel(dn_in, out_in, dn_ref, out_ref, land, send, recv):
+    d, c, core, cd, xd = places()
+    barrier = pltpu.get_barrier_semaphore()
+    for to in (cd, xd):
+        pl.semaphore_signal(barrier, inc=1, device_id=(to, c), device_id_type=MESH)
+    pl.semaphore_wait(barrier, 2)
+    parts = (dn_in, out_in)
+    first = []
+    x = d // 2
+    for i, part in enumerate(parts):
+        for j, xx in enumerate((1 - x, x)):
+            first.append(
+                remote(part.at[2 * xx + 1 - core], land.at[i, j], send.at[i, j], recv.at[i, j], (cd, c))
+            )
+    for j in (0, 1):
+        for i in range(2):
+            first[2 * i + j].start()
+    second = []
+    for i, part in enumerate(parts):
+        first[2 * i].wait_recv()
+        land[i, 0] = (land[i, 0].astype(F32) + part[xd].astype(F32)).astype(BF)
+        second.append(remote(land.at[i, 0], land.at[i, 2], send.at[i, 2], recv.at[i, 2], (xd, c)))
+        second[-1].start()
+    for i, (part, ref) in enumerate(zip(parts, (dn_ref, out_ref))):
+        first[2 * i + 1].wait_recv()
+        second[i].wait_recv()
+        ref[...] = part[d].astype(F32) + land[i, 1].astype(F32) + land[i, 2].astype(F32)
+    for copy in first + second:
+        copy.wait_send()
+
+
+def back_kernel(
+    n, nblk,
+    gu_part, wd_part, da_ref, af_ref, inv_ref, p_ref, q_ref, kv_ref, a_ref, b_ref, cos_ref, sin_ref,
+    dq_ref, dp_ref, gu_ref, wd_ref,
+    ka, kb, dka, dqa, db, dkv, dkv16, kv_land, gu_land, wd_land, gu_own,
+    own_sem, ring_send, ring_recv, kv_send, kv_recv, near_send, near_recv,
+):
+    d, c, core, cd, xd = places()
+    t = q_ref.shape[1]
+    n_dp = 4
+    meet(n, False)
+    cut = -(-wd_part.shape[1] // 16) * 8
+
+    def wd_half(ref, w):
+        return ref.at[:cut] if w == 0 else ref.at[cut:]
+
+    gr = ScatterRing(
+        n, lambda o: gu_part.at[:, :, o], lambda o, w: gu_part.at[w, :, o], gu_land,
+        None, lambda ref, w: ref.at[w], ring_send.at[0], ring_recv.at[0],
+    )
+    dr = ScatterRing(
+        n, lambda o: wd_part.at[o], lambda o, w: wd_half(wd_part.at[o], w), wd_land,
+        None, wd_half, ring_send.at[1], ring_recv.at[1],
+    )
+    rings = (gr, dr)
+    for one in rings:
+        one.start()
+
+    def advance(s):
+        for one in rings:
+            one.step(s)
+
+    h = n // 2
+    pairs = H // 2
+
+    def serve(p):
+        @pl.when(p == 1)
+        def _():
+            advance(1)
+
+        @pl.when(p > 1)
+        def _():
+            lo = 2 + (p - 2) * (h - 2) // (pairs - 2)
+            hi = 2 + (p - 1) * (h - 2) // (pairs - 2)
+            steps(lo, hi, advance)
+
+    attend_back_part(
+        nblk, serve, da_ref, af_ref, inv_ref, p_ref, q_ref, kv_ref, a_ref, b_ref, cos_ref, sin_ref,
+        dq_ref, dkv, ka, kb, dka, dqa, db,
+    )
+    dkv16[...] = dkv[...].astype(BF)
+
+    def kv_copy(k):
+        src = dkv16.at[:, (nblk - 1 - k) * t : (nblk - k) * t]
+        return remote(src, kv_land.at[k - 1], kv_send.at[k - 1], kv_recv.at[k - 1], (d, (c + n - k) % n))
+
+    for k in range(1, nblk):
+        @pl.when(c - k >= 0)
+        def _():
+            kv_copy(k).start()
+    dp_ref[...] = dkv[:, (nblk - 1) * t :]
+    for k in range(1, nblk):
+        @pl.when(c + k < n)
+        def _():
+            kv_copy(k).wait_recv()
+            dp_ref[...] += kv_land[k - 1].astype(F32)
+    total = gr.result().astype(BF)
+    for dd in range(n_dp):
+        gu_own[dd] = total[:, dd]
+    keep = pltpu.make_async_copy(gu_own.at[d], gu_ref.at[d], own_sem)
+    keep.start()
+    a2a = []
+    for k in range(1, n_dp):
+        to = (d + k) % n_dp
+        a2a.append(
+            (
+                remote(gu_own.at[to], gu_ref.at[d], near_send.at[k - 1], near_recv.at[k - 1], (to, c)),
+                remote(
+                    gu_own.at[to], gu_ref.at[(d + n_dp - k) % n_dp],
+                    near_send.at[k - 1], near_recv.at[k - 1], (to, c),
+                ),
+            )
+        )
+        a2a[-1][0].start()
+    wd_ref[...] = dr.result()
+    for out, arrival in a2a:
+        arrival.wait_recv()
+        out.wait_send()
+    keep.wait()
+    for k in range(1, nblk):
+        @pl.when(c - k >= 0)
+        def _():
+            kv_copy(k).wait_send()
+    for one in rings:
+        one.drain()
+
+
+def last_kernel(
+    n, fac_part, wo_part, fac_ref, wo_ref,
+    fac_core, wo_core, fac_land, wo_land, fac_x, wo_x,
+    near_send, near_recv, ring_send, ring_recv,
+):
+    d, c, core, cd, xd = places()
+    meet(n, True)
+    x = d // 2
+    rings, swaps = [], []
+    for i, (part, held) in enumerate(((fac_part, fac_core), (wo_part, wo_core))):
+        for xx in range(2):
+            swaps.append(
+                remote(
+                    part.at[2 * xx + 1 - core], held.at[xx],
+                    near_send.at[i, xx], near_recv.at[i, xx], (cd, c),
+                )
+            )
+            swaps[-1].start()
+    jobs = ((fac_part, fac_core, fac_land, fac_x, fac_ref), (wo_part, wo_core, wo_land, wo_x, wo_ref))
+    for i, (part, held, land, _, _) in enumerate(jobs):
+        for xx in range(2):
+            swaps[2 * i + xx].wait_recv()
+            held[xx] = (held[xx].astype(F32) + part[2 * xx + core].astype(F32)).astype(BF)
+        ring = ScatterRing(
+            n, lambda o, held=held: held.at[:, o], lambda o, w, held=held: held.at[w, o], land,
+            None, lambda ref, w: ref.at[w], ring_send.at[i], ring_recv.at[i],
+        )
+        ring.start()
+        rings.append(ring)
+    h = n // 2
+    for s in range(1, min(h, 2)):
+        for ring in rings:
+            ring.step(s)
+    steps(2, h, lambda s: [ring.step(s) for ring in rings])
+    ends = []
+    for i, (ring, (part, held, land, xbuf, ref)) in enumerate(zip(rings, jobs)):
+        total = ring.result()
+        for xx in range(2):
+            xbuf[xx] = total[xx].astype(BF)
+        ends.append(remote(xbuf.at[1 - x], xbuf.at[2], near_send.at[i, 2], near_recv.at[i, 2], (xd, c)))
+        ends[-1].start()
+    for end, ring, (_, _, _, xbuf, ref) in zip(ends, rings, jobs):
+        end.wait_recv()
+        ref[...] = xbuf[x].astype(F32) + xbuf[2].astype(F32)
+    for copy in swaps + ends:
+        copy.wait_send()
+    for ring in rings:
+        ring.drain()
+
+
 def vmem(n):
     return [pl.BlockSpec(memory_space=pltpu.VMEM)] * n
 
 
+def hbm(n):
+    return [pl.BlockSpec(memory_space=pl.ANY)] * n
+
+
 SMEM = pl.BlockSpec(memory_space=pltpu.SMEM)
+DMA = pltpu.SemaphoreType.DMA
+
+
+def talks(i):
+    return pltpu.CompilerParams(
+        collective_id=i, has_side_effects=True, vmem_limit_bytes=60 * 1024 * 1024
+    )
 
 
 def silu_parts(gate):
@@ -264,19 +786,13 @@
     rows = width // n_all
     c = lax.axis_index("ctx")
 
+    h = n_ctx // 2
+
     pack = jnp.concatenate(
         [factor_weights, first_gain[:, None], second_gain[:, None],
          jnp.zeros((rows, FPAD - FDIM - 2), F32)], axis=1).astype(BF)
-    fac = lax.all_gather(pack, both, axis=0, tiled=True)
-    wo = lax.all_gather(output_weights.astype(BF), both, axis=0, tiled=True)
-    gu = jnp.stack([gate_weights, up_weights]).astype(BF).reshape(2, rows, n_dp, ffq)
-    gu = lax.all_to_all(gu.transpose(2, 0, 1, 3), "dp", 0, 0, tiled=False)
-    gu = lax.all_gather(gu, "ctx", axis=2, tiled=False)
-    gu = gu.transpose(1, 0, 2, 3, 4).reshape(2, width, ffq)
-    wg, wu = gu[0], gu[1]
-    wd = lax.all_gather(down_weights.astype(BF), "ctx", axis=0, tiled=True)
-    g1 = fac[:, FDIM].reshape(1, width).astype(F32)
-    g2 = fac[:, FDIM + 1].reshape(1, width).astype(F32)
+    gu_in = jnp.stack([gate_weights, up_weights]).astype(BF).reshape(2, rows, n_dp, ffq)
+    gu_in = gu_in.transpose(2, 0, 1, 3)
 
     half = DH // 2
     freq = 10000.0 ** (-(np.arange(half) * 2.0 / DH))
@@ -285,48 +801,64 @@
     cosine, sine = jnp.cos(angles), jnp.sin(angles)
 
     x16 = tokens.reshape(t, width)
-    normed_t, q_t, packet, a_t, b_t = pl.pallas_call(
-        pre_kernel,
+    cot_own = cotangent.reshape(t, width)
+    sds = jax.ShapeDtypeStruct
+    down_rows = down_weights.shape[0]
+    (
+        normed_t, q_t, a_t, b_t, kv, attn_t, attn_f, inv, probs, fac, wo, gu, wd, nm_all, cot, middle
+    ) = pl.pallas_call(
+        functools.partial(front_kernel, n_ctx, nblk),
         out_shape=(
-            jax.ShapeDtypeStruct((width, t), BF),
-            jax.ShapeDtypeStruct((H * DH, t), BF),
-            jax.ShapeDtypeStruct((PACK, t), BF),
-            jax.ShapeDtypeStruct((AQ, 1, t), F32),
-            jax.ShapeDtypeStruct((BQ, t), F32),
+            sds((width, t), BF),
+            sds((H * DH, t), BF),
+            sds((AQ, 1, t), F32),
+            sds((BQ, t), F32),
+            sds((PACK, nblk * t), BF),
+            sds((H * DH, t), BF),
+            sds((H * DH, t), F32),
+            sds((H // 2, 8, 2 * t), F32),
+            sds((H // 2, nblk * t, 2 * t), BF),
+            sds((n_dp, n_ctx, rows, FPAD), BF),
+            sds((n_dp, n_ctx, rows, width), BF),
+            sds((2, n_dp, n_ctx, rows, ffq), BF),
+            sds((n_ctx, down_rows, width), BF),
+            sds((n_dp, t, width), BF),
+            sds((n_dp, t, width), BF),
+            sds((t, width), F32),
         ),
-        in_specs=vmem(5),
-        out_specs=tuple(vmem(5)),
-        name="pre",
-    )(x16, g1, fac, cosine, sine)
-
-    whole = lax.all_gather(packet, "ctx", axis=1, tiled=True)
-    base = jnp.maximum(c - nblk + 1, 0) * t
-    kv = lax.dynamic_slice_in_dim(whole, base, nblk * t, 1)
-    attn_t, attn_f, inv, probs = pl.pallas_call(
-        functools.partial(attend_kernel, nblk),
-        out_shape=(
-            jax.ShapeDtypeStruct((H * DH, t), BF),
-            jax.ShapeDtypeStruct((H * DH, t), F32),
-            jax.ShapeDtypeStruct((H // 2, 8, 2 * t), F32),
-            jax.ShapeDtypeStruct((H // 2, nblk * t, 2 * t), BF),
-        ),
-        in_specs=[SMEM, SMEM] + vmem(2),
-        out_specs=tuple(vmem(4)),
+        in_specs=[SMEM] + vmem(5) + hbm(3),
+        out_specs=tuple(vmem(11) + hbm(2) + vmem(1) + hbm(1) + vmem(1)),
         scratch_shapes=[
             pltpu.VMEM((2 * AK, 1, nblk * t), F32),
             pltpu.VMEM((2 * BK, nblk * t), F32),
             pltpu.VMEM((nblk * t, t), F32),
+            DMA((5,)),
+            DMA((9,)),
+            DMA((9,)),
+            DMA((6, 2, h)),
+            DMA((6, 2, h)),
+            DMA((nblk - 1,)),
+            DMA((nblk - 1,)),
+            DMA((2, 3)),
+            DMA((2, 3)),
         ],
-        name="attend",
-    )(base[None], doc_lengths, q_t, kv)
+        compiler_params=talks(0),
+        name="front",
+    )(doc_lengths, x16, cosine, sine, pack, output_weights.astype(BF), gu_in,
+      down_weights.astype(BF), cot_own)
+
+    fac = fac.reshape(width, FPAD)
+    wo = wo.reshape(width, width)
+    gu = gu.reshape(2, width, ffq)
+    wg, wu = gu[0], gu[1]
+    wd = wd.reshape(n_ctx * down_rows, width)
+    nm_all = nm_all.reshape(n_dp * t, width)
+    cot = cot.reshape(n_dp * t, width)
+    g1 = fac[:, FDIM].reshape(1, width).astype(F32)
+    g2 = fac[:, FDIM + 1].reshape(1, width).astype(F32)
 
     x = x16.astype(F32)
-    middle = x + nn(attn_t.T, wo)
     r2 = lax.rsqrt(jnp.mean(middle * middle, axis=-1, keepdims=True) + EPS)
-    nm = (middle * r2 * g2).astype(BF)
-    cot_own = cotangent.reshape(t, width)
-    cot = lax.all_gather(cot_own, "dp", axis=0, tiled=True)
-    nm_all = lax.all_gather(nm, "dp", axis=0, tiled=True)
     gate = nn(nm_all, wg)
     upward = nn(nm_all, wu)
     sig, act = silu_parts(gate)
@@ -334,25 +866,25 @@
     d_hidden = nt(cot, wd)
     d_gate = (d_hidden * upward * sig * (1.0 + gate * (1.0 - sig))).astype(BF)
     d_up = (d_hidden * act).astype(BF)
-    dn_part = nt(d_gate, wg) + nt(d_up, wu)
-    d_norm_mid = lax.psum_scatter(dn_part.astype(BF), "dp", scatter_dimension=0, tiled=True).astype(F32)
-    out_part = nn(hidden, wd)
-    out_sum = lax.psum_scatter(out_part.astype(BF), "dp", scatter_dimension=0, tiled=True)
-    layer_output = (middle + out_sum.astype(F32)).astype(BF)
+    dn_part = (nt(d_gate, wg) + nt(d_up, wu)).astype(BF).reshape(n_dp, t, width)
+    out_part = nn(hidden, wd).astype(BF).reshape(n_dp, t, width)
+    d_norm_mid, out_sum = pl.pallas_call(
+        mid_kernel,
+        out_shape=(sds((t, width), F32), sds((t, width), F32)),
+        in_specs=vmem(2),
+        out_specs=tuple(vmem(2)),
+        scratch_shapes=[pltpu.VMEM((2, 3, t, width), BF), DMA((2, 3)), DMA((2, 3))],
+        compiler_params=talks(1),
+        name="mid",
+    )(dn_part, out_part)
+    layer_output = (middle + out_sum).astype(BF)
 
     def tn(a, b):
         return lax.dot_general(a, b, (((0,), (0,)), ((), ())), preferred_element_type=F32)
 
     gu_part = jnp.stack([tn(nm_all, d_gate), tn(nm_all, d_up)]).astype(BF)
-    gu_part = gu_part.reshape(2, n_dp, n_ctx, rows, ffq).transpose(2, 1, 0, 3, 4)
-    gu_part = gu_part.reshape(n_ctx * n_dp * 2 * rows, ffq)
-    gu_own = lax.psum_scatter(gu_part, "ctx", scatter_dimension=0, tiled=True)
-    gu_own = gu_own.reshape(n_dp, 2, rows, ffq)
-    gu_own = lax.all_to_all(gu_own, "dp", 0, 0, tiled=False)
-    gu_own = gu_own.astype(F32).transpose(1, 2, 0, 3).reshape(2, rows, ff)
-    down_sum = lax.psum_scatter(
-        tn(hidden, cot).astype(BF), "ctx", scatter_dimension=0, tiled=True
-    ).astype(F32)
+    gu_part = gu_part.reshape(2, n_dp, n_ctx, rows, ffq)
+    wd_part = tn(hidden, cot).astype(BF).reshape(n_ctx, down_rows, width)
 
     second_part = jnp.sum(d_norm_mid * middle * r2, axis=0)
     u2 = d_norm_mid * g2
@@ -365,28 +897,41 @@
     d_attn_t = nt(wo, d_branch)
     out_grad_part = nn(attn_t, d_branch)
 
-    dq_rows, dkv = pl.pallas_call(
-        functools.partial(attend_back_kernel, nblk),
+    dq_rows, d_packet, gu_own, down_sum = pl.pallas_call(
+        functools.partial(back_kernel, n_ctx, nblk),
         out_shape=(
-            jax.ShapeDtypeStruct((AQ + BQ, t), F32),
-            jax.ShapeDtypeStruct((PACK, nblk * t), F32),
+            sds((AQ + BQ, t), F32),
+            sds((PACK, t), F32),
+            sds((n_dp, 2, rows, ffq), BF),
+            sds((down_rows, width), F32),
         ),
-        in_specs=vmem(10),
-        out_specs=tuple(vmem(2)),
+        in_specs=vmem(12),
+        out_specs=tuple(vmem(4)),
         scratch_shapes=[
             pltpu.VMEM((2 * AK, 1, nblk * t), F32),
             pltpu.VMEM((2 * BK, nblk * t), F32),
             pltpu.VMEM((2 * AK, 1, nblk * t), F32),
             pltpu.VMEM((AQ, 1, t), F32),
             pltpu.VMEM((BQ, t), F32),
+            pltpu.VMEM((PACK, nblk * t), F32),
+            pltpu.VMEM((PACK, nblk * t), BF),
+            pltpu.VMEM((nblk - 1, PACK, t), BF),
+            pltpu.VMEM((2, h, 2, n_dp, rows, ffq), BF),
+            pltpu.VMEM((2, h, down_rows, width), BF),
+            pltpu.VMEM((n_dp, 2, rows, ffq), BF),
+            DMA,
+            DMA((2, 2, h)),
+            DMA((2, 2, h)),
+            DMA((nblk - 1,)),
+            DMA((nblk - 1,)),
+            DMA((3,)),
+            DMA((3,)),
         ],
-        name="attend_back",
-    )(d_attn_t, attn_f, inv, probs, q_t, kv, a_t, b_t, cosine, sine)
-
-    spread = lax.dynamic_update_slice_in_dim(
-        jnp.zeros((PACK, length), BF), dkv.astype(BF), base, 1
-    )
-    d_packet = lax.psum_scatter(spread, "ctx", scatter_dimension=1, tiled=True).astype(F32)
+        compiler_params=talks(2),
+        name="back",
+    )(gu_part, wd_part, d_attn_t, attn_f, inv, probs, q_t, kv, a_t, b_t, cosine, sine)
+    gu_own = gu_own.astype(F32).transpose(1, 2, 0, 3).reshape(2, rows, ff)
+
     d_bk = rope_back(d_packet[AK : AK + BK], cosine, sine, RKV)
     d_fac_t = jnp.concatenate([dq_rows, d_packet[:AK], d_bk, d_packet[KEY_ROWS:]], axis=0).astype(BF)
     d_fac = d_fac_t.T
@@ -398,17 +943,35 @@
         d_middle + r1 * u1 - x * (r1**3 * jnp.mean(u1 * x, axis=-1, keepdims=True))
     ).astype(BF)
     fac_part = nt(normed_t, d_fac_t)
-    out_own = lax.psum_scatter(out_grad_part.astype(BF), both, scatter_dimension=0, tiled=True)
     last = jnp.concatenate(
         [fac_part, first_part[:, None], second_part[:, None],
          jnp.zeros((width, FPAD - FDIM - 2), F32)], axis=1).astype(BF)
-    last_own = lax.psum_scatter(last, both, scatter_dimension=0, tiled=True).astype(F32)
+    last_own, out_own = pl.pallas_call(
+        functools.partial(last_kernel, n_ctx),
+        out_shape=(sds((rows, FPAD), F32), sds((rows, width), F32)),
+        in_specs=vmem(2),
+        out_specs=tuple(vmem(2)),
+        scratch_shapes=[
+            pltpu.VMEM((2, n_ctx, rows, FPAD), BF),
+            pltpu.VMEM((2, n_ctx, rows, width), BF),
+            pltpu.VMEM((2, h, 2, rows, FPAD), BF),
+            pltpu.VMEM((2, h, 2, rows, width), BF),
+            pltpu.VMEM((3, rows, FPAD), BF),
+            pltpu.VMEM((3, rows, width), BF),
+            DMA((2, 3)),
+            DMA((2, 3)),
+            DMA((2, 2, h)),
+            DMA((2, 2, h)),
+        ],
+        compiler_params=talks(3),
+        name="last",
+    )(last.reshape(n_dp, n_ctx, rows, FPAD), out_grad_part.astype(BF).reshape(n_dp, n_ctx, rows, width))
     return (
         layer_output.reshape(1, t, width),
         input_grad.reshape(1, t, width),
         last_own[:, FDIM],
         last_own[:, :FDIM],
-        out_own.astype(F32),
+        out_own,
         last_own[:, FDIM + 1],
         gu_own[0],
         gu_own[1],

time: 848 us -> 290 us (0.34)
  waiting for transfers between devices: 685 us -> 0 us
  Pallas kernels: 24.9 us -> 230 us
  blocking collectives: 40.6 us -> 0 us
  between operations: 14.3 us -> 1.07 us
  matrix products: 33.5 us -> 22.4 us
    reduce_scatter x5 -> x0, waiting for transfers between devices: 310 us -> none  [the longest x1 127 us: body(): lax.psum_scatter(out_grad_part.astype(BF), both, scatter_dimension=0, til...]
    pallas_call x3 -> x4, Pallas kernels: 24.9 us -> 230 us  [the longest x1 107 us: body(): pl.pallas_call(functools.partial(front_kernel, n_ctx, nblk), out_shape=(s...]
    all_gather x6 -> x0, waiting for transfers between devices: 189 us -> none  [the longest x1 56.5 us: body(): gu = lax.all_gather(gu, 'ctx', axis=2, tiled=False)]
    unnamed x15 -> x0, waiting for transfers between devices: 180 us -> none
    all_gather x1 -> x0, blocking collectives: 29 us -> none  [body(): whole = lax.all_gather(packet, 'ctx', axis=1, tiled=True)]
    all_to_all x1 -> x0, blocking collectives: 11.6 us -> none  [body(): gu = lax.all_to_all(gu.transpose(2, 0, 1, 3), 'dp', 0, 0, tiled=False)]
  transfers between devices with their start and end apart: 14 -> 0, of which waited for: 14 -> 0; matrix products, arithmetic and copies ran while one was open for 7% -> 0% of each run, Pallas kernels for 1% -> 0%
where the time goes in v2:
time: 290 us; the launch traced here: 289 us
  Pallas kernels  230 us (79%)
  matrix products  22.4 us (8%)
  other arithmetic  20.5 us (7%)
  local copies, waits for them, and re-layouts  15 us (5%)
    pallas_call x1, Pallas kernels, body(): pl.pallas_call(functools.partial(front_kernel, n_ctx, nblk), out_shape=(s...  107 us
    pallas_call x1, Pallas kernels, body(): pl.pallas_call(functools.partial(back_kernel, n_ctx, nblk), out_shape=(sd...  72.9 us
    pallas_call x1, Pallas kernels, body(): pl.pallas_call(functools.partial(last_kernel, n_ctx), out_shape=(sds((row...  31.3 us
    pallas_call x1, Pallas kernels, body(): pl.pallas_call(mid_kernel, out_shape=(sds((t, width), F32), sds((t, width...  18.5 us
    dot_general x6, matrix products, nt(): lax.dot_general(a, b, (((1,), (1,)), ((), ())), preferred_element_type=F32)  10.5 us
    dot_general x4, matrix products, nn(): return jnp.dot(a, b, preferred_element_type=F32)  6.52 us

profile of v2, /device:TPU:0, one launch (start us, length us, event | category | flops | bytes accessed | tf_op | source)
XLA Modules:
  0.0 289.0 jit_solution(1297655839823296716)
XLA Ops:
  0.7 1.5 multiply_sine_fusion
  2.2 0.9 convert.67
  5.3 1.1 convert.70
  9.1 107.3 %front.1 = (bf16[1024,128]{1,0:T(8,128)(2,1)}, bf16[1024,128]{1,0:T(8,128)(2,1)}, f32[96,1,128]{2,1,0:T(1,128)}, f32[384,128]{1,0:T(8,128)}, bf16[320,640]{1,0:T...) custom-call(s32[1,8]{1,0:T(1,128)} %len_ref.1, ...), custom_call_target="tpu_custom_call" | custom-call | tf_op jit(solution)/shard_map/front/pallas_call | solution.py:809
  116.4 2.3 fusion.32
  118.8 1.0 fusion.35
  120.4 0.9 fusion.34
  121.4 1.6 multiply_convert_fusion
  123.0 2.0 convolution_convert_fusion.5
  125.0 1.0 fusion.36
  126.0 2.0 add_convert_fusion
  128.1 18.5 %mid.1 = (f32[128,1024]{1,0:T(8,128)}, f32[128,1024]{1,0:T(8,128)}) custom-call(bf16[4,128,1024]{2,1,0:T(8,128)(2,1)} %bitcast.85, bf16[4,128,1024]{2,1,0:T(8,128)(2,1)} %bitcast.84), custom_call_target="tpu_custom_call" | custom-call | tf_op jit(solution)/shard_map/mid/pallas_call | solution.py:871
  146.8 1.3 slice_convert_fusion
  148.5 0.9 multiply_subtract_fusion
  149.4 2.0 convolution_convert_fusion
  151.4 1.5 fusion.16.da_ref
  153.0 2.1 convolution_convert_fusion.4
  155.9 2.2 fusion.2
  158.1 1.0 fusion.3
  159.1 2.0 pad_maximum_fusion.gu_part
  161.1 72.9 %back.1 = (f32[480,128]{1,0:T(8,128)}, f32[320,128]{1,0:T(8,128)}, bf16[4,2,32,704]{3,2,1,0:T(8,128)(2,1)}, f32[88,1024]{1,0:T(8,128)}) custom-call(bf16[2,4,8,32,704]{4,3,2,1,0:T(8,128)(2,1)} %pad_maximum_fusion.gu_part, bf16[8,88,1024]{2,1,0:T(8,128)(2,1)} %bitcast.80, f32[1024,128]{1,0:T(8,128)} %fusion.16.da_ref, f32[1024,128]{1,0:T(8,128)} %get-tuple-element.42.af_ref, ...), custom_call_target="tpu_custom_call" | custom-call | tf_op jit(solution)/shard_map/back/pallas_call | solution.py:900
  234.0 1.0 convert_dynamic-update-slice_fusion
  234.9 0.9 convert.75
  235.9 0.9 constant_dynamic-update-slice_fusion.3
  239.5 1.9 convolution_convert_fusion.1
  241.4 3.1 %copy.31 = bf16[1024,800]{1,0:T(8,128)(2,1)S(1)} copy(bf16[1024,800]{0,1:T(8,128)(2,1)} %convolution_convert_fusion.1) | data formatting | bytes 3276800 | tf_op jit(solution)/shard_map/convert.9
  244.8 3.1 %fusion.12 = (bf16[1024]{0:T(1024)(128)(2,1)S(1)}, f32[128]{0:T(128)S(1)}, f32[128,1024]{1,0:T(8,128)}) fusion(f32[128]{0:T(128)S(1)} %add_rsqrt_fusion, bf16[1,128,1024]{2,1,0:T(8,128)(2,1)S(1)} %copy-done.1, f32[1024]{0:T(1024)S(1)} %bitcast.94, bf16[800,128]{1,0:T(8,128)(2,1)S(1)} %slice_dynamic-update-slice_fusion, bf16[1024,896]{1,0:T(8,128)(2,1)} %bitcast.91), kind=kOutput, calls=%fused_computation.30 | convolution fusion | flops 210631552 | bytes 2833408 | tf_op jit(solution)/shard_map/dot_general | solution.py:31
  248.8 1.8 maximum_maximum_fusion.fac_part
  250.6 31.3 %last.1 = (f32[32,896]{1,0:T(8,128)}, f32[32,1024]{1,0:T(8,128)}) custom-call(bf16[4,8,32,896]{3,2,1,0:T(8,128)(2,1)} %maximum_maximum_fusion.fac_part, bf16[4,8,32,1024]{3,2,1,0:T(8,128)(2,1)} %bitcast.72), custom_call_target="tpu_custom_call" | custom-call | tf_op jit(solution)/shard_map/last/pallas_call | solution.py:949
  281.9 1.5 slice_reduce_fusion
  283.8 1.0 squeeze.22
  285.1 1.0 squeeze.23
  (95 shorter events, 14.5 us)
Async XLA Ops:
  0.6 6.1 %copy-start.10 = (f32[32,2816]{1,0:T(8,128)S(1)}, f32[32,2816]{1,0:T(8,128)}, u32[]{:S(2)}) copy-start(f32[32,2816]{1,0:T(8,128)} %param.18) | copy-start | bytes 1081348
  5.3 2.5 copy-start.11
  6.6 1.9 copy-start.16
  116.4 2.3 copy-start.4
  118.8 1.4 copy-start.19
  118.8 1.6 copy-start.20
  122.9 2.0 copy-start.24
  123.0 3.1 %copy-start.26 = (bf16[512,704]{0,1:T(8,128)(2,1)}, bf16[512,704]{0,1:T(8,128)(2,1)S(1)}, u32[]{:S(2)}) copy-start(bf16[512,704]{0,1:T(8,128)(2,1)S(1)} %get-tuple-element.66) | copy-start | bytes 2162692
  123.0 3.1 %copy-start.22 = (bf16[512,704]{0,1:T(8,128)(2,1)}, bf16[512,704]{0,1:T(8,128)(2,1)S(1)}, u32[]{:S(2)}) copy-start(bf16[512,704]{0,1:T(8,128)(2,1)S(1)} %get-tuple-element.67) | copy-start | bytes 2162692
  128.1 18.5 %copy-start = (f32[128,1024]{1,0:T(8,128)S(1)}, f32[128,1024]{1,0:T(8,128)}, u32[]{:S(2)}) copy-start(f32[128,1024]{1,0:T(8,128)} %get-tuple-element.33) | copy-start | bytes 1572868
  146.6 1.7 copy-start.2
  146.7 1.7 copy-start.6
  146.7 1.7 copy-start.7
  148.4 1.0 copy-start.14
  149.4 2.0 copy-start.3
  151.4 1.5 copy-start.21
  151.4 1.5 copy-start.25
  153.0 2.1 copy-start.5
  155.9 2.2 copy-start.23
  161.1 74.8 %copy-start.18 = (f32[32]{0:T(128)S(1)}, f32[32]{0:T(128)}, u32[]{:S(2)}) copy-start(f32[32]{0:T(128)} %constant.24.clone) | copy-start | bytes 388
  161.1 78.4 %copy-start.13 = (bf16[1024,128]{1,0:T(8,128)(2,1)S(1)}, bf16[1024,128]{1,0:T(8,128)(2,1)}, u32[]{:S(2)}) copy-start(bf16[1024,128]{1,0:T(8,128)(2,1)} %get-tuple-element.51) | copy-start | bytes 786436
  241.4 3.2 %copy-start.1 = (bf16[1,128,1024]{2,1,0:T(8,128)(2,1)S(1)}, bf16[1,128,1024]{2,1,0:T(8,128)(2,1)}, u32[]{:S(2)}) copy-start(bf16[1,128,1024]{2,1,0:T(8,128)(2,1)} %param.11) | copy-start | bytes 786436
  250.6 32.8 %copy-start.9 = (bf16[4,2,32,704]{3,2,1,0:T(8,128)(2,1)S(1)}, bf16[4,2,32,704]{3,2,1,0:T(8,128)(2,1)}, u32[]{:S(2)}) copy-start(bf16[4,2,32,704]{3,2,1,0:T(8,128)(2,1)} %get-tuple-element.55) | copy-start | bytes 1081348
  283.5 2.5 copy-start.8
  284.8 2.2 copy-start.15
  284.8 2.8 copy-start.17
  285.1 3.2 %copy-start.12 = (f32[88,1024]{1,0:T(8,128)S(1)}, f32[88,1024]{1,0:T(8,128)}, u32[]{:S(2)}) copy-start(f32[88,1024]{1,0:T(8,128)} %get-tuple-element.94) | copy-start | bytes 1081348

commit v3 on v2

--- a/solution.py
+++ b/solution.py
@@ -341,7 +341,7 @@
 
 
 def attend_back_part(
-    nblk, serve, da_ref, af_ref, inv_ref, p_ref, q_ref, kv_ref, a_ref, b_ref, cos_ref, sin_ref,
+    nblk, serve, da_ref, af_ref, inv_ref, p_copy, pbuf, q_ref, kv_ref, a_ref, b_ref, cos_ref, sin_ref,
     dq_ref, dkv_ref, ka, kb, dka, dqa, db,
 ):
     t = q_ref.shape[1]
@@ -361,7 +361,12 @@
                 dka[row, :, lanes] = jnp.sum(d * b, axis=0, keepdims=True)
                 dkv_ref[first : first + DH, lanes] += d * ka[row, :, lanes]
 
-    def pair(p, _):
+    def pair(p, carry):
+        @pl.when(p + 1 < H // 2)
+        def _():
+            p_copy(p + 1).start()
+
+        p_copy(p).wait()
         rows = pl.ds(pl.multiple_of(p * 2 * DH, 2 * DH), 2 * DH)
         da = da_ref[rows, :]
         inv = inv_ref[p][:1]
@@ -374,7 +379,7 @@
             lanes = lane_block(j, t)
             k = expand_pair(ka, kb, 0, p, lanes).astype(BF)
             v = expand_pair(ka, kb, 1, p, lanes).T.astype(BF)
-            pb = p_ref[p, lanes, :]
+            pb = pbuf[p % 2, lanes, :]
             ds = (pb.astype(F32) * (nn(v, dn) + dtot)).astype(BF)
             dq = dq + nn(k, ds)
             factor_back(nt(qd, ds) * (DH**-0.5), 0, p, lanes)
@@ -390,7 +395,7 @@
                 dqa[row] = jnp.sum(d * b_ref[r * DH : (r + 1) * DH, :], axis=0, keepdims=True)
                 db[r * DH : (r + 1) * DH, :] += d * a_ref[row]
         serve(p)
-        return _
+        return carry
 
     lax.fori_loop(0, H // 2, pair, 0)
     for i in range(AQ):
@@ -445,11 +450,13 @@
         5, lambda o: wd.at[o],
         lambda o, w: wd.at[o, :cut] if w == 0 else wd.at[o, cut:],
     )
+    small, large = (fo, fx, oo, ox), (gr, dr)
     fswap = remote(fac.at[d, c], fac.at[d, c], near_send.at[0], near_recv.at[0], (xd, c))
     oswap = remote(wo.at[d, c], wo.at[d, c], near_send.at[1], near_recv.at[1], (xd, c))
     fswap.start()
+    oswap.start()
     fo.start(0)
-    oswap.start()
+    oo.start(0)
     a2a = []
     for k in range(1, n_dp):
         to = (d + k) % n_dp
@@ -468,40 +475,36 @@
     cots.start()
     fswap.wait_recv()
     fx.start(0)
-    for s in range(1, n // 2 - 1) if n <= 8 else ():
-        fo.step(s)
-        fx.step(s)
-    if n > 8:
-        steps(1, n // 2 - 1, lambda s: (fo.step(s), fx.step(s)))
-    fo.last()
-    fx.last()
     oswap.wait_recv()
+    ox.start(0)
+    steps(1, n // 2 - 1, lambda s: [one.step(s) for one in small])
+    for one in small:
+        one.last()
     for _, arrival in a2a:
         arrival.wait_recv()
-    rest = (gr, dr, oo, ox)
-    for one in rest:
+    for one in large:
         one.start(0)
-    fo.arrive(n // 2 - 1)
-    fx.arrive(n // 2 - 1)
-    fcore = [
-        (
-            remote(fac.at[dd], fac.at[dd], near_send.at[5 + i], near_recv.at[5 + i], (cd, c)),
-            remote(fac.at[da], fac.at[da], near_send.at[5 + i], near_recv.at[5 + i], (cd, c)),
+    def core_swap(ref, i, dd, da):
+        return (
+            remote(ref.at[dd], ref.at[dd], near_send.at[5 + i], near_recv.at[5 + i], (cd, c)),
+            remote(ref.at[da], ref.at[da], near_send.at[5 + i], near_recv.at[5 + i], (cd, c)),
         )
-        for i, (dd, da) in enumerate(((d, cd), (xd, (cd + 2) % 4)))
-    ]
-    for out, _ in fcore:
-        out.start()
+
+    near = []
+    for i, (one, ref, dd, da) in enumerate(
+        ((fo, fac, d, cd), (fx, fac, xd, (cd + 2) % 4), (oo, wo, d, cd), (ox, wo, xd, (cd + 2) % 4))
+    ):
+        one.arrive(n // 2 - 1)
+        near.append(core_swap(ref, i, dd, da))
+        near[-1][0].start()
     cots.forward()
-    for _, arrival in fcore:
+    for _, arrival in near[:2]:
         arrival.wait_recv()
 
     width = x_ref.shape[1]
     x = x_ref[...].astype(F32)
     w = fac[...].reshape(width, FPAD)
-    gains = w[:, FPAD - 128 :].astype(F32).T
-    g1 = gains[FDIM - (FPAD - 128) : FDIM - (FPAD - 128) + 1]
-    g2 = gains[FDIM - (FPAD - 128) + 1 : FDIM - (FPAD - 128) + 2]
+    g1, g2 = gain_rows(w)
     own_kv = kv_ref.at[:, (nblk - 1) * t : nblk * t]
     pre_part(x, g1, w, cos_ref[...], sin_ref[...], nt_ref, q_ref, own_kv, a_ref, b_ref)
 
@@ -513,34 +516,16 @@
         @pl.when(c + k < n)
         def _():
             kv_copy(k).start()
-
-    full = n // 2 - 1
-    one_third = 1 + (full - 1) // 2
-
-    def advance(lo, hi):
-        steps(lo, hi, lambda s: [one.step(s) for one in rest])
-
-    advance(1, one_third)
     for k in range(1, nblk):
         @pl.when(c - k >= 0)
         def _():
             kv_copy(k).wait_recv()
     attend_part(nblk, len_ref, q_ref, kv_ref, at_ref, af_ref, inv_ref, p_ref, ka, kb, bias)
-    advance(one_third, full)
-    for one in rest:
-        one.last()
-    for one in (oo, ox, gr, dr):
-        one.arrive(n // 2 - 1)
-    ocore = [
-        (
-            remote(wo.at[dd], wo.at[dd], near_send.at[7 + i], near_recv.at[7 + i], (cd, c)),
-            remote(wo.at[da], wo.at[da], near_send.at[7 + i], near_recv.at[7 + i], (cd, c)),
-        )
-        for i, (dd, da) in enumerate(((d, cd), (xd, (cd + 2) % 4)))
-    ]
-    for out, _ in ocore:
-        out.start()
-    for _, arrival in ocore:
+
+    full = n // 2 - 1
+    middle_step = 1 + full // 2
+    steps(1, middle_step, lambda s: [one.step(s) for one in large])
+    for _, arrival in near[2:]:
         arrival.wait_recv()
     middle = x + nn(at_ref[...].T, wo[...].reshape(width, width))
     mid_ref[...] = middle
@@ -550,60 +535,105 @@
     nms.forward()
     nms.finish()
     cots.finish()
+    steps(middle_step, full, lambda s: [one.step(s) for one in large])
+    for one in large:
+        one.last()
+    for one in large:
+        one.arrive(n // 2 - 1)
     for k in range(1, nblk):
         @pl.when(c + k < n)
         def _():
             kv_copy(k).wait_send()
     fswap.wait_send()
     oswap.wait_send()
-    for out, _ in a2a + fcore + ocore:
+    for out, _ in a2a + near:
         out.wait_send()
-    for one in (fo, fx, oo, ox, gr, dr):
+    for one in small + large:
         one.drain()
 
 
-def mid_kernel(dn_in, out_in, dn_ref, out_ref, land, send, recv):
+def gain_rows(w):
+    first = FPAD - 128
+    gains = w[:, first:].astype(F32).T
+    return gains[FDIM - first : FDIM - first + 1], gains[FDIM - first + 1 : FDIM - first + 2]
+
+
+class PairScatter:
+    def __init__(self, n, part, held, land, own, send, recv, ring_send, ring_recv):
+        d, c, core, cd, xd = places()
+        self.core, self.x, self.part, self.held, self.own = core, d // 2, part, held, own
+        self.swaps = [
+            remote(part.at[2 * xx + 1 - core], held.at[xx], send.at[xx], recv.at[xx], (cd, c))
+            for xx in range(2)
+        ]
+        self.end = remote(own.at[1 - self.x], own.at[2], send.at[2], recv.at[2], (xd, c))
+        self.ring = ScatterRing(
+            n, lambda o: held.at[:, o], lambda o, w: held.at[w, o], land,
+            None, lambda ref, w: ref.at[w], ring_send, ring_recv,
+        )
+
+    def start(self):
+        for swap in self.swaps:
+            swap.start()
+
+    def enter(self):
+        for xx in range(2):
+            self.swaps[xx].wait_recv()
+            mine = self.part[2 * xx + self.core].astype(F32)
+            self.held[xx] = (self.held[xx].astype(F32) + mine).astype(BF)
+        self.ring.start()
+
+    def leave(self):
+        total = self.ring.result()
+        for xx in range(2):
+            self.own[xx] = total[xx].astype(BF)
+        self.end.start()
+
+    def result(self):
+        self.end.wait_recv()
+        return self.own[self.x].astype(F32) + self.own[2].astype(F32)
+
+    def drain(self):
+        for copy in self.swaps + [self.end]:
+            copy.wait_send()
+        self.ring.drain()
+
+
+def back_kernel(
+    n, nblk,
+    gu_part, wd_part, dn_in, out_in, mid_ref, cot_ref, x_ref, fac, wo, at_ref, nt_ref,
+    af_ref, inv_ref, p_ref, q_ref, kv_ref, a_ref, b_ref, cos_ref, sin_ref,
+    y_ref, dx_ref, fac_ref, wo_ref, gu_ref, wd_ref,
+    ka, kb, dka, dqa, db, dkv, dkv16, kv_land, gu_land, wd_land, gu_own,
+    da_ref, dq_ref, dmid_ref, dp_land, fac_part, wo_part, fac_held, wo_held, fac_land, wo_land,
+    fac_own, wo_own,
+    own_sem, ring_send, ring_recv, kv_send, kv_recv, near_send, near_recv, dp_send, dp_recv,
+    pair_send, pair_recv, pbuf, p_sem,
+):
     d, c, core, cd, xd = places()
-    barrier = pltpu.get_barrier_semaphore()
-    for to in (cd, xd):
-        pl.semaphore_signal(barrier, inc=1, device_id=(to, c), device_id_type=MESH)
-    pl.semaphore_wait(barrier, 2)
+    x_at = d // 2
+    t = q_ref.shape[1]
+    n_dp = 4
+    width = x_ref.shape[1]
+
+    def p_copy(p):
+        return pltpu.make_async_copy(p_ref.at[p], pbuf.at[p % 2], p_sem.at[p % 2])
+
+    p_copy(0).start()
+    meet(n, False)
     parts = (dn_in, out_in)
     first = []
-    x = d // 2
     for i, part in enumerate(parts):
-        for j, xx in enumerate((1 - x, x)):
+        for j, xx in enumerate((1 - x_at, x_at)):
             first.append(
-                remote(part.at[2 * xx + 1 - core], land.at[i, j], send.at[i, j], recv.at[i, j], (cd, c))
+                remote(
+                    part.at[2 * xx + 1 - core], dp_land.at[i, j],
+                    dp_send.at[i, j], dp_recv.at[i, j], (cd, c),
+                )
             )
     for j in (0, 1):
         for i in range(2):
             first[2 * i + j].start()
-    second = []
-    for i, part in enumerate(parts):
-        first[2 * i].wait_recv()
-        land[i, 0] = (land[i, 0].astype(F32) + part[xd].astype(F32)).astype(BF)
-        second.append(remote(land.at[i, 0], land.at[i, 2], send.at[i, 2], recv.at[i, 2], (xd, c)))
-        second[-1].start()
-    for i, (part, ref) in enumerate(zip(parts, (dn_ref, out_ref))):
-        first[2 * i + 1].wait_recv()
-        second[i].wait_recv()
-        ref[...] = part[d].astype(F32) + land[i, 1].astype(F32) + land[i, 2].astype(F32)
-    for copy in first + second:
-        copy.wait_send()
-
-
-def back_kernel(
-    n, nblk,
-    gu_part, wd_part, da_ref, af_ref, inv_ref, p_ref, q_ref, kv_ref, a_ref, b_ref, cos_ref, sin_ref,
-    dq_ref, dp_ref, gu_ref, wd_ref,
-    ka, kb, dka, dqa, db, dkv, dkv16, kv_land, gu_land, wd_land, gu_own,
-    own_sem, ring_send, ring_recv, kv_send, kv_recv, near_send, near_recv,
-):
-    d, c, core, cd, xd = places()
-    t = q_ref.shape[1]
-    n_dp = 4
-    meet(n, False)
     cut = -(-wd_part.shape[1] // 16) * 8
 
     def wd_half(ref, w):
@@ -617,31 +647,74 @@
         n, lambda o: wd_part.at[o], lambda o, w: wd_half(wd_part.at[o], w), wd_land,
         None, wd_half, ring_send.at[1], ring_recv.at[1],
     )
-    rings = (gr, dr)
-    for one in rings:
+    large = (gr, dr)
+    for one in large:
         one.start()
+    second = []
+    for i, part in enumerate(parts):
+        first[2 * i].wait_recv()
+        dp_land[i, 0] = (dp_land[i, 0].astype(F32) + part[xd].astype(F32)).astype(BF)
+        second.append(
+            remote(dp_land.at[i, 0], dp_land.at[i, 2], dp_send.at[i, 2], dp_recv.at[i, 2], (xd, c))
+        )
+        second[-1].start()
+    fs = PairScatter(
+        n, fac_part, fac_held, fac_land, fac_own, pair_send.at[0], pair_recv.at[0],
+        ring_send.at[2], ring_recv.at[2],
+    )
+    ws = PairScatter(
+        n, wo_part, wo_held, wo_land, wo_own, pair_send.at[1], pair_recv.at[1],
+        ring_send.at[3], ring_recv.at[3],
+    )
+    h = n // 2
 
     def advance(s):
-        for one in rings:
+        for one in large:
             one.step(s)
 
-    h = n // 2
-    pairs = H // 2
-
-    def serve(p):
-        @pl.when(p == 1)
+    advance(1)
+    for i in range(2):
+        first[2 * i + 1].wait_recv()
+    second[0].wait_recv()
+    middle = mid_ref[...]
+    r2 = lax.rsqrt(jnp.mean(middle * middle, axis=-1, keepdims=True) + EPS)
+    w = fac[...].reshape(width, FPAD)
+    g1, g2 = gain_rows(w)
+    dn = dn_in[d].astype(F32) + dp_land[0, 1].astype(F32) + dp_land[0, 2].astype(F32)
+    second_part = jnp.sum(dn * middle * r2, axis=0, keepdims=True)
+    u2 = dn * g2
+    d_middle = (
+        cot_ref[...].astype(F32)
+        + r2 * u2
+        - middle * (r2 * r2 * r2 * jnp.mean(u2 * middle, axis=-1, keepdims=True))
+    )
+    dmid_ref[...] = d_middle
+    d_branch = d_middle.astype(BF)
+    wo_part[...] = nn(at_ref[...], d_branch).astype(BF).reshape(wo_part.shape)
+    ws.start()
+    da_ref[...] = nt(wo[...].reshape(width, width), d_branch)
+    second[1].wait_recv()
+    y_ref[...] = (
+        mid_ref[...]
+        + (out_in[d].astype(F32) + dp_land[1, 1].astype(F32) + dp_land[1, 2].astype(F32))
+    ).astype(BF)
+    ws.enter()
+    points = 3
+
+    def serve(k):
+        steps(2 + -(-(k - 1) * (h - 2) // points), 2 + -(-k * (h - 2) // points), advance)
+
+    serve(1)
+
+    def serve_pair(p):
+        @pl.when(p == H // 2 - 3)
         def _():
-            advance(1)
-
-        @pl.when(p > 1)
-        def _():
-            lo = 2 + (p - 2) * (h - 2) // (pairs - 2)
-            hi = 2 + (p - 1) * (h - 2) // (pairs - 2)
-            steps(lo, hi, advance)
+            ws.ring.step(1)
+            serve(2)
 
     attend_back_part(
-        nblk, serve, da_ref, af_ref, inv_ref, p_ref, q_ref, kv_ref, a_ref, b_ref, cos_ref, sin_ref,
-        dq_ref, dkv, ka, kb, dka, dqa, db,
+        nblk, serve_pair, da_ref, af_ref, inv_ref, p_copy, pbuf, q_ref, kv_ref, a_ref, b_ref,
+        cos_ref, sin_ref, dq_ref, dkv, ka, kb, dka, dqa, db,
     )
     dkv16[...] = dkv[...].astype(BF)
 
@@ -653,12 +726,37 @@
         @pl.when(c - k >= 0)
         def _():
             kv_copy(k).start()
-    dp_ref[...] = dkv[:, (nblk - 1) * t :]
+    own_kv = dkv.at[:, (nblk - 1) * t :]
+    serve(3)
     for k in range(1, nblk):
         @pl.when(c + k < n)
         def _():
             kv_copy(k).wait_recv()
-            dp_ref[...] += kv_land[k - 1].astype(F32)
+            own_kv[...] += kv_land[k - 1].astype(F32)
+    steps(2, h, ws.ring.step)
+    dp = own_kv[...]
+    d_bk = rope_back(dp[AK : AK + BK], cos_ref[...], sin_ref[...], RKV)
+    d_fac_t = jnp.concatenate(
+        [dq_ref[...], dp[:AK], d_bk, dp[KEY_ROWS:], jnp.zeros((FPAD - FDIM, t), F32)], axis=0
+    ).astype(BF)
+    x = x_ref[...].astype(F32)
+    r1 = lax.rsqrt(jnp.mean(x * x, axis=-1, keepdims=True) + EPS)
+    d_norm_in = nt(d_fac_t.T, w)
+    first_part = jnp.sum(d_norm_in * x * r1, axis=0, keepdims=True)
+    tail = FPAD - 128
+    gains = jnp.concatenate(
+        [jnp.zeros((FDIM - tail, width), F32), first_part, second_part,
+         jnp.zeros((FPAD - FDIM - 2, width), F32)], axis=0).T
+    product = nt(nt_ref[...], d_fac_t)
+    shape = fac_part.shape[:3]
+    fac_part[:, :, :, :tail] = product[:, :tail].astype(BF).reshape(shape + (tail,))
+    fac_part[:, :, :, tail:] = (product[:, tail:] + gains).astype(BF).reshape(shape + (128,))
+    fs.start()
+    u1 = d_norm_in * g1
+    dx_ref[...] = (
+        dmid_ref[...] + r1 * u1 - x * (r1 * r1 * r1 * jnp.mean(u1 * x, axis=-1, keepdims=True))
+    ).astype(BF)
+    fs.enter()
     total = gr.result().astype(BF)
     for dd in range(n_dp):
         gu_own[dd] = total[:, dd]
@@ -677,67 +775,25 @@
             )
         )
         a2a[-1][0].start()
+    ws.leave()
+    fs.ring.step(1)
     wd_ref[...] = dr.result()
+    steps(2, h, fs.ring.step)
+    wo_ref[...] = ws.result()
+    fs.leave()
     for out, arrival in a2a:
         arrival.wait_recv()
         out.wait_send()
     keep.wait()
+    fac_ref[...] = fs.result()
     for k in range(1, nblk):
         @pl.when(c - k >= 0)
         def _():
             kv_copy(k).wait_send()
-    for one in rings:
+    for copy in first + second:
+        copy.wait_send()
+    for one in large + (ws, fs):
         one.drain()
-
-
-def last_kernel(
-    n, fac_part, wo_part, fac_ref, wo_ref,
-    fac_core, wo_core, fac_land, wo_land, fac_x, wo_x,
-    near_send, near_recv, ring_send, ring_recv,
-):
-    d, c, core, cd, xd = places()
-    meet(n, True)
-    x = d // 2
-    rings, swaps = [], []
-    for i, (part, held) in enumerate(((fac_part, fac_core), (wo_part, wo_core))):
-        for xx in range(2):
-            swaps.append(
-                remote(
-                    part.at[2 * xx + 1 - core], held.at[xx],
-                    near_send.at[i, xx], near_recv.at[i, xx], (cd, c),
-                )
-            )
-            swaps[-1].start()
-    jobs = ((fac_part, fac_core, fac_land, fac_x, fac_ref), (wo_part, wo_core, wo_land, wo_x, wo_ref))
-    for i, (part, held, land, _, _) in enumerate(jobs):
-        for xx in range(2):
-            swaps[2 * i + xx].wait_recv()
-            held[xx] = (held[xx].astype(F32) + part[2 * xx + core].astype(F32)).astype(BF)
-        ring = ScatterRing(
-            n, lambda o, held=held: held.at[:, o], lambda o, w, held=held: held.at[w, o], land,
-            None, lambda ref, w: ref.at[w], ring_send.at[i], ring_recv.at[i],
-        )
-        ring.start()
-        rings.append(ring)
-    h = n // 2
-    for s in range(1, min(h, 2)):
-        for ring in rings:
-            ring.step(s)
-    steps(2, h, lambda s: [ring.step(s) for ring in rings])
-    ends = []
-    for i, (ring, (part, held, land, xbuf, ref)) in enumerate(zip(rings, jobs)):
-        total = ring.result()
-        for xx in range(2):
-            xbuf[xx] = total[xx].astype(BF)
-        ends.append(remote(xbuf.at[1 - x], xbuf.at[2], near_send.at[i, 2], near_recv.at[i, 2], (xd, c)))
-        ends[-1].start()
-    for end, ring, (_, _, _, xbuf, ref) in zip(ends, rings, jobs):
-        end.wait_recv()
-        ref[...] = xbuf[x].astype(F32) + xbuf[2].astype(F32)
-    for copy in swaps + ends:
-        copy.wait_send()
-    for ring in rings:
-        ring.drain()
 
 
 def vmem(n):
@@ -826,8 +882,8 @@
             sds((n_dp, t, width), BF),
             sds((t, width), F32),
         ),
-        in_specs=[SMEM] + vmem(5) + hbm(3),
-        out_specs=tuple(vmem(11) + hbm(2) + vmem(1) + hbm(1) + vmem(1)),
+        in_specs=[SMEM] + vmem(8),
+        out_specs=tuple(vmem(16)),
         scratch_shapes=[
             pltpu.VMEM((2 * AK, 1, nblk * t), F32),
             pltpu.VMEM((2 * BK, nblk * t), F32),
@@ -847,18 +903,12 @@
     )(doc_lengths, x16, cosine, sine, pack, output_weights.astype(BF), gu_in,
       down_weights.astype(BF), cot_own)
 
-    fac = fac.reshape(width, FPAD)
-    wo = wo.reshape(width, width)
     gu = gu.reshape(2, width, ffq)
     wg, wu = gu[0], gu[1]
     wd = wd.reshape(n_ctx * down_rows, width)
     nm_all = nm_all.reshape(n_dp * t, width)
     cot = cot.reshape(n_dp * t, width)
-    g1 = fac[:, FDIM].reshape(1, width).astype(F32)
-    g2 = fac[:, FDIM + 1].reshape(1, width).astype(F32)
-
-    x = x16.astype(F32)
-    r2 = lax.rsqrt(jnp.mean(middle * middle, axis=-1, keepdims=True) + EPS)
+
     gate = nn(nm_all, wg)
     upward = nn(nm_all, wu)
     sig, act = silu_parts(gate)
@@ -868,16 +918,6 @@
     d_up = (d_hidden * act).astype(BF)
     dn_part = (nt(d_gate, wg) + nt(d_up, wu)).astype(BF).reshape(n_dp, t, width)
     out_part = nn(hidden, wd).astype(BF).reshape(n_dp, t, width)
-    d_norm_mid, out_sum = pl.pallas_call(
-        mid_kernel,
-        out_shape=(sds((t, width), F32), sds((t, width), F32)),
-        in_specs=vmem(2),
-        out_specs=tuple(vmem(2)),
-        scratch_shapes=[pltpu.VMEM((2, 3, t, width), BF), DMA((2, 3)), DMA((2, 3))],
-        compiler_params=talks(1),
-        name="mid",
-    )(dn_part, out_part)
-    layer_output = (middle + out_sum).astype(BF)
 
     def tn(a, b):
         return lax.dot_general(a, b, (((0,), (0,)), ((), ())), preferred_element_type=F32)
@@ -886,27 +926,18 @@
     gu_part = gu_part.reshape(2, n_dp, n_ctx, rows, ffq)
     wd_part = tn(hidden, cot).astype(BF).reshape(n_ctx, down_rows, width)
 
-    second_part = jnp.sum(d_norm_mid * middle * r2, axis=0)
-    u2 = d_norm_mid * g2
-    d_middle = (
-        cot_own.astype(F32)
-        + r2 * u2
-        - middle * (r2**3 * jnp.mean(u2 * middle, axis=-1, keepdims=True))
-    )
-    d_branch = d_middle.astype(BF)
-    d_attn_t = nt(wo, d_branch)
-    out_grad_part = nn(attn_t, d_branch)
-
-    dq_rows, d_packet, gu_own, down_sum = pl.pallas_call(
+    layer_output, input_grad, last_own, out_own, gu_own, down_sum = pl.pallas_call(
         functools.partial(back_kernel, n_ctx, nblk),
         out_shape=(
-            sds((AQ + BQ, t), F32),
-            sds((PACK, t), F32),
+            sds((t, width), BF),
+            sds((t, width), BF),
+            sds((rows, FPAD), F32),
+            sds((rows, width), F32),
             sds((n_dp, 2, rows, ffq), BF),
             sds((down_rows, width), F32),
         ),
-        in_specs=vmem(12),
-        out_specs=tuple(vmem(4)),
+        in_specs=vmem(13) + hbm(1) + vmem(6),
+        out_specs=tuple(vmem(6)),
         scratch_shapes=[
             pltpu.VMEM((2 * AK, 1, nblk * t), F32),
             pltpu.VMEM((2 * BK, nblk * t), F32),
@@ -919,53 +950,37 @@
             pltpu.VMEM((2, h, 2, n_dp, rows, ffq), BF),
             pltpu.VMEM((2, h, down_rows, width), BF),
             pltpu.VMEM((n_dp, 2, rows, ffq), BF),
-            DMA,
-            DMA((2, 2, h)),
-            DMA((2, 2, h)),
-            DMA((nblk - 1,)),
-            DMA((nblk - 1,)),
-            DMA((3,)),
-            DMA((3,)),
-        ],
-        compiler_params=talks(2),
-        name="back",
-    )(gu_part, wd_part, d_attn_t, attn_f, inv, probs, q_t, kv, a_t, b_t, cosine, sine)
-    gu_own = gu_own.astype(F32).transpose(1, 2, 0, 3).reshape(2, rows, ff)
-
-    d_bk = rope_back(d_packet[AK : AK + BK], cosine, sine, RKV)
-    d_fac_t = jnp.concatenate([dq_rows, d_packet[:AK], d_bk, d_packet[KEY_ROWS:]], axis=0).astype(BF)
-    d_fac = d_fac_t.T
-    d_norm_in = nt(d_fac, fac[:, :FDIM])
-    r1 = lax.rsqrt(jnp.mean(x * x, axis=-1, keepdims=True) + EPS)
-    first_part = jnp.sum(d_norm_in * x * r1, axis=0)
-    u1 = d_norm_in * g1
-    input_grad = (
-        d_middle + r1 * u1 - x * (r1**3 * jnp.mean(u1 * x, axis=-1, keepdims=True))
-    ).astype(BF)
-    fac_part = nt(normed_t, d_fac_t)
-    last = jnp.concatenate(
-        [fac_part, first_part[:, None], second_part[:, None],
-         jnp.zeros((width, FPAD - FDIM - 2), F32)], axis=1).astype(BF)
-    last_own, out_own = pl.pallas_call(
-        functools.partial(last_kernel, n_ctx),
-        out_shape=(sds((rows, FPAD), F32), sds((rows, width), F32)),
-        in_specs=vmem(2),
-        out_specs=tuple(vmem(2)),
-        scratch_shapes=[
+            pltpu.VMEM((H * DH, t), F32),
+            pltpu.VMEM((AQ + BQ, t), F32),
+            pltpu.VMEM((t, width), F32),
+            pltpu.VMEM((2, 3, t, width), BF),
+            pltpu.VMEM((n_dp, n_ctx, rows, FPAD), BF),
+            pltpu.VMEM((n_dp, n_ctx, rows, width), BF),
             pltpu.VMEM((2, n_ctx, rows, FPAD), BF),
             pltpu.VMEM((2, n_ctx, rows, width), BF),
             pltpu.VMEM((2, h, 2, rows, FPAD), BF),
             pltpu.VMEM((2, h, 2, rows, width), BF),
             pltpu.VMEM((3, rows, FPAD), BF),
             pltpu.VMEM((3, rows, width), BF),
+            DMA,
+            DMA((4, 2, h)),
+            DMA((4, 2, h)),
+            DMA((nblk - 1,)),
+            DMA((nblk - 1,)),
+            DMA((3,)),
+            DMA((3,)),
             DMA((2, 3)),
             DMA((2, 3)),
-            DMA((2, 2, h)),
-            DMA((2, 2, h)),
+            DMA((2, 3)),
+            DMA((2, 3)),
+            pltpu.VMEM((2, nblk * t, 2 * t), BF),
+            DMA((2,)),
         ],
-        compiler_params=talks(3),
-        name="last",
-    )(last.reshape(n_dp, n_ctx, rows, FPAD), out_grad_part.astype(BF).reshape(n_dp, n_ctx, rows, width))
+        compiler_params=talks(1),
+        name="back",
+    )(gu_part, wd_part, dn_part, out_part, middle, cot_own, x16, fac, wo, attn_t, normed_t,
+      attn_f, inv, probs, q_t, kv, a_t, b_t, cosine, sine)
+    gu_own = gu_own.astype(F32).transpose(1, 2, 0, 3).reshape(2, rows, ff)
     return (
         layer_output.reshape(1, t, width),
         input_grad.reshape(1, t, width),

time: 290 us -> 220 us (0.76)
  Pallas kernels: 230 us -> 186 us
  other arithmetic: 20.5 us -> 8.37 us
  matrix products: 22.4 us -> 12.6 us
  local copies, waits for them, and re-layouts: 15 us -> 11.2 us
    pallas_call x2 -> x0, Pallas kernels: 49.8 us -> none  [the longest x1 31.3 us: body(): pl.pallas_call(functools.partial(last_kernel, n_ctx), out_shape=(sds((row...]
    pallas_call x1, Pallas kernels: 72.9 us -> 100 us  [body(): pl.pallas_call(functools.partial(back_kernel, n_ctx, nblk), out_shape=(sd...]
    pallas_call x1, Pallas kernels: 107 us -> 86.2 us  [body(): pl.pallas_call(functools.partial(front_kernel, n_ctx, nblk), out_shape=(s...]
    dot_general x6 -> x3, matrix products: 10.5 us -> 3.98 us  [nt(): lax.dot_general(a, b, (((1,), (1,)), ((), ())), preferred_element_type=F32)]
    unnamed x5 -> x0, other arithmetic: 4.54 us -> none
    another operation x1 -> x0, local copies, waits for them, and re-layouts: 3.05 us -> none
    dot_general x4 -> x3, matrix products: 6.52 us -> 4.6 us  [nn(): return jnp.dot(a, b, preferred_element_type=F32)]
where the time goes in v3:
time: 220 us
  Pallas kernels  186 us (85%)
  matrix products  12.6 us (6%)
  local copies, waits for them, and re-layouts  11.2 us (5%)
  other arithmetic  8.37 us (4%)
    pallas_call x1, Pallas kernels, body(): pl.pallas_call(functools.partial(back_kernel, n_ctx, nblk), out_shape=(sd...  100 us
    pallas_call x1, Pallas kernels, body(): pl.pallas_call(functools.partial(front_kernel, n_ctx, nblk), out_shape=(s...  86.2 us
    dot_general x3, matrix products, nn(): return jnp.dot(a, b, preferred_element_type=F32)  4.6 us

profile of v3, /device:TPU:0, one launch (start us, length us, event | category | flops | bytes accessed | tf_op | source)
XLA Modules:
  0.0 219.5 jit_solution(13578926577526866664)
XLA Ops:
  0.7 1.5 multiply_sine_fusion
  2.1 1.1 convert.33
  3.8 0.8 maximum_bitcast_fusion.gu_in
  4.6 0.7 convert_element_type.39.wd_in
  5.6 0.7 maximum_maximum_fusion.fac_in
  6.3 0.6 convert_element_type.38.wo_in
  7.0 86.2 %front.1 = (bf16[1024,128]{1,0:T(8,128)(2,1)}, bf16[1024,128]{1,0:T(8,128)(2,1)}, f32[96,1,128]{2,1,0:T(1,128)}, f32[384,128]{1,0:T(8,128)}, bf16[320,640]{1,0:T...) custom-call(s32[1,8]{1,0:T(1,128)} %len_ref.1, ...), custom_call_target="tpu_custom_call" | custom-call | tf_op jit(solution)/shard_map/front/pallas_call | solution.py:865
  93.2 2.3 %fusion.5 = (bf16[1,4,8,32,704]{4,3,2,1,0:T(8,128)(2,1)S(1)}, bf16[1,4,8,32,704]{4,3,2,1,0:T(8,128)(2,1)S(1)}) fusion(bf16[2,4,8,32,704]{4,3,2,1,0:T(8,128)(2,1)} %get-tuple-element.34), kind=kLoop, calls=%fused_computation.25 | loop fusion | bytes 5767168 | tf_op jit(solution)/shard_map/slice | solution.py:907
  95.5 1.0 fusion.8
  96.5 0.4 copy-done.10
  96.9 0.3 copy-done.11
  97.2 0.9 fusion.7
  98.1 1.6 multiply_convert_fusion
  99.7 2.1 convolution_convert_fusion.3
  101.8 1.0 fusion.9
  102.8 2.0 add_convert_fusion
  104.8 2.0 convolution_convert_fusion.2
  106.9 0.7 copy.27
  107.6 1.0 fusion
  108.6 1.0 fusion.1
  109.6 1.9 pad_maximum_fusion.gu_part
  111.6 100.2 %back.1 = (bf16[128,1024]{1,0:T(8,128)(2,1)}, bf16[128,1024]{1,0:T(8,128)(2,1)}, f32[32,896]{1,0:T(8,128)}, f32[32,1024]{1,0:T(8,128)}, bf16[4,2,32,704]{3,2,1,0:T(8,128)(2,1)}, /*index=5*/f32[88,1024]{1,0:T(8,128)}) custom-call(bf16[2,4,8,32,704]{4,3,2,1,0:T(8,128)(2,1)} %pad_maximum_fusion.gu_part, bf16[8,88,1024]{2,1,0:T(8,128)(2,1)} %bitcast.58, ...), custom_call_target="tpu_custom_call" | custom-call | tf_op jit(solution)/shard_map/back/pallas_call | solution.py:929
  211.7 1.1 convert_bitcast_fusion
  212.9 0.3 copy.28
  213.1 1.0 squeeze.22
  214.4 1.0 squeeze.23
  215.4 0.7 slice_reduce_fusion
  216.1 0.7 copy.37
  216.8 0.7 copy.38
  217.5 0.6 copy.39
  218.2 0.7 copy.40
  218.8 0.7 copy.41
  (41 shorter events, 1.2 us)
Async XLA Ops:
  0.6 2.9 %copy-start.1 = (f32[32,2816]{1,0:T(8,128)S(1)}, f32[32,2816]{1,0:T(8,128)}, u32[]{:S(2)}) copy-start(f32[32,2816]{1,0:T(8,128)} %param.18) | copy-start | bytes 1081348
  2.1 2.5 %copy-start.2 = (f32[88,1024]{1,0:T(8,128)S(1)}, f32[88,1024]{1,0:T(8,128)}, u32[]{:S(2)}) copy-start(f32[88,1024]{1,0:T(8,128)} %param.19) | copy-start | bytes 1081348
  3.4 1.9 copy-start.9
  3.4 1.9 copy-start.12
  3.5 2.0 copy-start.13
  3.5 2.8 %copy-start.7 = (f32[32,1024]{1,0:T(8,128)S(1)}, f32[32,1024]{1,0:T(8,128)}, u32[]{:S(2)}) copy-start(f32[32,1024]{1,0:T(8,128)} %param.15) | copy-start | bytes 393220
  93.2 2.3 %copy-start = (bf16[4,128,1024]{2,1,0:T(8,128)(2,1)S(1)}, bf16[4,128,1024]{2,1,0:T(8,128)(2,1)}, u32[]{:S(2)}) copy-start(bf16[4,128,1024]{2,1,0:T(8,128)(2,1)} %get-tuple-element.31) | copy-start | bytes 3145732
  95.5 1.4 copy-start.10
  95.5 1.6 copy-start.11
  212.9 2.5 %copy-start.6 = (f32[32,896]{1,0:T(8,128)S(1)}, f32[32,896]{1,0:T(8,128)}, u32[]{:S(2)}) copy-start(f32[32,896]{1,0:T(8,128)} %get-tuple-element.49) | copy-start | bytes 344068
  212.9 3.2 %copy-start.5 = (bf16[128,1024]{1,0:T(8,128)(2,1)S(1)}, bf16[128,1024]{1,0:T(8,128)(2,1)}, u32[]{:S(2)}) copy-start(bf16[128,1024]{1,0:T(8,128)(2,1)} %get-tuple-element.47) | copy-start | bytes 786436
  213.1 3.7 %copy-start.4 = (bf16[128,1024]{1,0:T(8,128)(2,1)S(1)}, bf16[128,1024]{1,0:T(8,128)(2,1)}, u32[]{:S(2)}) copy-start(bf16[128,1024]{1,0:T(8,128)(2,1)} %get-tuple-element.48) | copy-start | bytes 786436
  214.1 4.0 %copy-start.8 = (f32[32,1024]{1,0:T(8,128)S(1)}, f32[32,1024]{1,0:T(8,128)}, u32[]{:S(2)}) copy-start(f32[32,1024]{1,0:T(8,128)} %get-tuple-element.77) | copy-start | bytes 393220
  214.1 4.7 %copy-start.3 = (f32[88,1024]{1,0:T(8,128)S(1)}, f32[88,1024]{1,0:T(8,128)}, u32[]{:S(2)}) copy-start(f32[88,1024]{1,0:T(8,128)} %get-tuple-element.81) | copy-start | bytes 1081348

commit v4 on v3

--- a/solution.py
+++ b/solution.py
@@ -258,25 +258,29 @@
         q_ref[h * DH : (h + 1) * DH, :] = (acc * (1.0 / RQ)).astype(BF)
 
 
-def expand_pair(ka, kb, side, p, lanes):
+def vectors(kv_ref, side, r, lanes):
+    first = side * KEY_ROWS + AK + r * DH
+    return kv_ref[first : first + DH, lanes].astype(F32)
+
+
+def expand_pair(ka, kv_ref, side, p, lanes):
     rows = []
     for hh in range(2):
         acc = 0.0
         for r in range(RKV):
             a = ka[side * AK + r * H + 2 * p + hh, :, lanes]
-            b = kb[side * BK + r * DH : side * BK + (r + 1) * DH, lanes]
+            b = vectors(kv_ref, side, r, lanes)
             acc = acc + a * b
         rows.append(acc * (1.0 / RKV))
     return jnp.concatenate(rows, axis=0)
 
 
-def unpack(kv_ref, ka, kb):
+def unpack(kv_ref, ka):
     for side in range(2):
         first = side * KEY_ROWS
         a = kv_ref[first : first + AK, :].astype(F32)
         for i in range(AK):
             ka[side * AK + i] = a[i : i + 1]
-        kb[side * BK : (side + 1) * BK, :] = kv_ref[first + AK : first + KEY_ROWS, :].astype(F32)
 
 
 def diagonal(pair):
@@ -291,7 +295,7 @@
     return jnp.concatenate([wide[:DH, :t], wide[DH:, t:]], axis=0)
 
 
-def attend_part(nblk, len_ref, q_ref, kv_ref, at_ref, af_ref, inv_ref, p_ref, ka, kb, bias):
+def attend_part(nblk, len_ref, q_ref, kv_ref, at_ref, af_ref, inv_ref, p_out, pbuf, ka, bias):
     t = q_ref.shape[1]
     c = lax.axis_index("ctx")
     tpos = c * t + lax.broadcasted_iota(jnp.int32, (1, t), 1)
@@ -300,7 +304,7 @@
     for j in range(len_ref.shape[1]):
         start = jnp.where(tpos >= run, run, start)
         run = run + len_ref[0, j]
-    unpack(kv_ref, ka, kb)
+    unpack(kv_ref, ka)
 
     def bias_block(j, _):
         spos = (c - nblk + 1 + j) * t + lax.broadcasted_iota(jnp.int32, (t, t), 0)
@@ -310,21 +314,25 @@
 
     blocks(nblk, bias_block, 0)
 
-    def pair(p, _):
+    def pair(p, carry):
+        @pl.when(p > 1)
+        def _():
+            p_out(p - 2).wait()
+
         rows = pl.ds(pl.multiple_of(p * 2 * DH, 2 * DH), 2 * DH)
         qd = diagonal(q_ref[rows, :])
 
         def step(j, state):
             num, tot = state
             lanes = lane_block(j, t)
-            k = expand_pair(ka, kb, 0, p, lanes).T.astype(BF)
-            v = expand_pair(ka, kb, 1, p, lanes).astype(BF)
+            k = expand_pair(ka, kv_ref, 0, p, lanes).T.astype(BF)
+            v = expand_pair(ka, kv_ref, 1, p, lanes).astype(BF)
             b = bias[lanes, :]
             s = nn(k, qd) * (LOG2E * DH**-0.5) + jnp.concatenate([b, b], axis=1)
             e = jnp.exp2(s)
             tot = tot + jnp.sum(e, axis=0, keepdims=True)
             pb = e.astype(BF)
-            p_ref[p, lanes, :] = pb
+            pbuf[p % 2, lanes, :] = pb
             return (num + nn(v, pb), tot)
 
         num, tot = blocks(
@@ -334,18 +342,21 @@
         af = undiagonal(num * inv)
         af_ref[rows, :] = af
         at_ref[rows, :] = af.astype(BF)
+        p_out(p).start()
         inv_ref[p] = jnp.broadcast_to(inv, (8, 2 * t))
-        return _
+        return carry
 
     lax.fori_loop(0, H // 2, pair, 0)
+    for p in range(H // 2 - 2, H // 2):
+        p_out(p).wait()
 
 
 def attend_back_part(
     nblk, serve, da_ref, af_ref, inv_ref, p_copy, pbuf, q_ref, kv_ref, a_ref, b_ref, cos_ref, sin_ref,
-    dq_ref, dkv_ref, ka, kb, dka, dqa, db,
+    dq_ref, dkv_ref, ka, dka, dqa, db,
 ):
     t = q_ref.shape[1]
-    unpack(kv_ref, ka, kb)
+    unpack(kv_ref, ka)
     db[...] = jnp.zeros_like(db)
     for side in range(2):
         first = side * KEY_ROWS + AK
@@ -357,7 +368,7 @@
             for r in range(RKV):
                 row = side * AK + r * H + 2 * p + hh
                 first = side * KEY_ROWS + AK + r * DH
-                b = kb[side * BK + r * DH : side * BK + (r + 1) * DH, lanes]
+                b = vectors(kv_ref, side, r, lanes)
                 dka[row, :, lanes] = jnp.sum(d * b, axis=0, keepdims=True)
                 dkv_ref[first : first + DH, lanes] += d * ka[row, :, lanes]
 
@@ -377,8 +388,8 @@
 
         def step(j, dq):
             lanes = lane_block(j, t)
-            k = expand_pair(ka, kb, 0, p, lanes).astype(BF)
-            v = expand_pair(ka, kb, 1, p, lanes).T.astype(BF)
+            k = expand_pair(ka, kv_ref, 0, p, lanes).astype(BF)
+            v = expand_pair(ka, kv_ref, 1, p, lanes).T.astype(BF)
             pb = pbuf[p % 2, lanes, :]
             ds = (pb.astype(F32) * (nn(v, dn) + dtot)).astype(BF)
             dq = dq + nn(k, ds)
@@ -406,13 +417,63 @@
     dq_ref[AQ : AQ + BQ, :] = rope_back(db[...], cos_ref[...], sin_ref[...], RQ)
 
 
-def front_kernel(
+def gain_rows(w):
+    first = FPAD - 128
+    gains = w[:, first:].astype(F32).T
+    return gains[FDIM - first : FDIM - first + 1], gains[FDIM - first + 1 : FDIM - first + 2]
+
+
+class PairScatter:
+    def __init__(self, n, part, held, land, own, send, recv, ring_send, ring_recv):
+        d, c, core, cd, xd = places()
+        self.core, self.x, self.part, self.held, self.own = core, d // 2, part, held, own
+        self.swaps = [
+            remote(part.at[2 * xx + 1 - core], held.at[xx], send.at[xx], recv.at[xx], (cd, c))
+            for xx in range(2)
+        ]
+        self.end = remote(own.at[1 - self.x], own.at[2], send.at[2], recv.at[2], (xd, c))
+        self.ring = ScatterRing(
+            n, lambda o: held.at[:, o], lambda o, w: held.at[w, o], land,
+            None, lambda ref, w: ref.at[w], ring_send, ring_recv,
+        )
+
+    def start(self):
+        for swap in self.swaps:
+            swap.start()
+
+    def enter(self):
+        for xx in range(2):
+            self.swaps[xx].wait_recv()
+            mine = self.part[2 * xx + self.core].astype(F32)
+            self.held[xx] = (self.held[xx].astype(F32) + mine).astype(BF)
+        self.ring.start()
+
+    def leave(self):
+        total = self.ring.result()
+        for xx in range(2):
+            self.own[xx] = total[xx].astype(BF)
+        self.end.start()
+
+    def result(self):
+        self.end.wait_recv()
+        return self.own[self.x].astype(F32) + self.own[2].astype(F32)
+
+    def drain(self):
+        for copy in self.swaps + [self.end]:
+            copy.wait_send()
+        self.ring.drain()
+
+
+def block_kernel(
     n, nblk,
     len_ref, x_ref, cos_ref, sin_ref, fac_in, wo_in, gu_in, wd_in, cot_in,
-    nt_ref, q_ref, a_ref, b_ref, kv_ref, at_ref, af_ref, inv_ref, p_ref,
-    fac, wo, gu, wd, nm, cot, mid_ref,
-    ka, kb, bias,
+    y_ref, dx_ref, fac_ref, wo_ref, gu_ref, wd_ref, p_ref,
+    nt_ref, q_ref, a_ref, b_ref, kv_ref, at_ref, af_ref, inv_ref, pbuf,
+    fac, wo, gu, wd, nm, cot, mid_ref, dn_in, out_in, gu_part, wd_part,
+    kv_land, gu_land, wd_land, gu_own, da_ref, dq_ref, dmid_ref, dp_land,
+    fac_part, wo_part, fac_held, wo_held, fac_land, wo_land, fac_own, wo_own,
     own_sem, near_send, near_recv, ring_send, ring_recv, kv_send, kv_recv, sp_send, sp_recv,
+    dkv_send, dkv_recv, end_send, end_recv, dp_send, dp_recv, pair_send, pair_recv, p_sem, own_dkv,
 ):
     d, c, core, cd, xd = places()
     t = x_ref.shape[0]
@@ -520,7 +581,17 @@
         @pl.when(c - k >= 0)
         def _():
             kv_copy(k).wait_recv()
-    attend_part(nblk, len_ref, q_ref, kv_ref, at_ref, af_ref, inv_ref, p_ref, ka, kb, bias)
+
+    def p_out(p):
+        return pltpu.make_async_copy(pbuf.at[p % 2], p_ref.at[p], p_sem.at[p % 2])
+
+    pl.run_scoped(
+        functools.partial(
+            attend_part, nblk, len_ref, q_ref, kv_ref, at_ref, af_ref, inv_ref, p_out, pbuf
+        ),
+        pltpu.VMEM((2 * AK, 1, nblk * t), F32),
+        pltpu.VMEM((nblk * t, t), F32),
+    )
 
     full = n // 2 - 1
     middle_step = 1 + full // 2
@@ -540,87 +611,8 @@
         one.last()
     for one in large:
         one.arrive(n // 2 - 1)
-    for k in range(1, nblk):
-        @pl.when(c + k < n)
-        def _():
-            kv_copy(k).wait_send()
-    fswap.wait_send()
-    oswap.wait_send()
-    for out, _ in a2a + near:
-        out.wait_send()
-    for one in small + large:
-        one.drain()
-
-
-def gain_rows(w):
-    first = FPAD - 128
-    gains = w[:, first:].astype(F32).T
-    return gains[FDIM - first : FDIM - first + 1], gains[FDIM - first + 1 : FDIM - first + 2]
-
-
-class PairScatter:
-    def __init__(self, n, part, held, land, own, send, recv, ring_send, ring_recv):
-        d, c, core, cd, xd = places()
-        self.core, self.x, self.part, self.held, self.own = core, d // 2, part, held, own
-        self.swaps = [
-            remote(part.at[2 * xx + 1 - core], held.at[xx], send.at[xx], recv.at[xx], (cd, c))
-            for xx in range(2)
-        ]
-        self.end = remote(own.at[1 - self.x], own.at[2], send.at[2], recv.at[2], (xd, c))
-        self.ring = ScatterRing(
-            n, lambda o: held.at[:, o], lambda o, w: held.at[w, o], land,
-            None, lambda ref, w: ref.at[w], ring_send, ring_recv,
-        )
-
-    def start(self):
-        for swap in self.swaps:
-            swap.start()
-
-    def enter(self):
-        for xx in range(2):
-            self.swaps[xx].wait_recv()
-            mine = self.part[2 * xx + self.core].astype(F32)
-            self.held[xx] = (self.held[xx].astype(F32) + mine).astype(BF)
-        self.ring.start()
-
-    def leave(self):
-        total = self.ring.result()
-        for xx in range(2):
-            self.own[xx] = total[xx].astype(BF)
-        self.end.start()
-
-    def result(self):
-        self.end.wait_recv()
-        return self.own[self.x].astype(F32) + self.own[2].astype(F32)
-
-    def drain(self):
-        for copy in self.swaps + [self.end]:
-            copy.wait_send()
-        self.ring.drain()
-
-
-def back_kernel(
-    n, nblk,
-    gu_part, wd_part, dn_in, out_in, mid_ref, cot_ref, x_ref, fac, wo, at_ref, nt_ref,
-    af_ref, inv_ref, p_ref, q_ref, kv_ref, a_ref, b_ref, cos_ref, sin_ref,
-    y_ref, dx_ref, fac_ref, wo_ref, gu_ref, wd_ref,
-    ka, kb, dka, dqa, db, dkv, dkv16, kv_land, gu_land, wd_land, gu_own,
-    da_ref, dq_ref, dmid_ref, dp_land, fac_part, wo_part, fac_held, wo_held, fac_land, wo_land,
-    fac_own, wo_own,
-    own_sem, ring_send, ring_recv, kv_send, kv_recv, near_send, near_recv, dp_send, dp_recv,
-    pair_send, pair_recv, pbuf, p_sem,
-):
-    d, c, core, cd, xd = places()
+
     x_at = d // 2
-    t = q_ref.shape[1]
-    n_dp = 4
-    width = x_ref.shape[1]
-
-    def p_copy(p):
-        return pltpu.make_async_copy(p_ref.at[p], pbuf.at[p % 2], p_sem.at[p % 2])
-
-    p_copy(0).start()
-    meet(n, False)
     parts = (dn_in, out_in)
     first = []
     for i, part in enumerate(parts):
@@ -631,45 +623,111 @@
                     dp_send.at[i, j], dp_recv.at[i, j], (cd, c),
                 )
             )
-    for j in (0, 1):
-        for i in range(2):
-            first[2 * i + j].start()
+    ffq = gu_in.shape[3]
+
+    def feed(gate, up, dh, hid, dg, du):
+        wg, wu = (gu.at[side] for side in range(2))
+
+        def matrix(ref):
+            return ref[...].reshape(width, ffq)
+
+        down = wd[...].reshape(ffq, width)
+
+        def pair_rows(i, carry):
+            xx = i * x_at + (1 - i) * (1 - x_at)
+            two = pl.ds(2 * xx, 2)
+            both = 2 * t
+            nm_two = nm[two].reshape(both, width)
+            gate[...] = nn(nm_two, matrix(wg))
+            up[...] = nn(nm_two, matrix(wu))
+            dh[...] = nt(cot[two].reshape(both, width), down)
+            base = pl.multiple_of(xx * both, both)
+
+            def rows_of(k, carry):
+                some = pl.ds(pl.multiple_of(k * 32, 32), 32)
+                to = pl.ds(pl.multiple_of(base + k * 32, 32), 32)
+                v, u, g = gate[some, :], up[some, :], dh[some, :]
+                sig, act = silu_parts(v)
+                hid[to, :] = (act * u).astype(BF)
+                dg[to, :] = (g * u * sig * (1.0 + v * (1.0 - sig))).astype(BF)
+                du[to, :] = (g * act).astype(BF)
+                return carry
+
+            lax.fori_loop(0, both // 32, rows_of, 0)
+            all_rows = pl.ds(base, both)
+            dn = nt(dg[all_rows, :], matrix(wg)) + nt(du[all_rows, :], matrix(wu))
+            dn_in[two] = dn.astype(BF).reshape(2, t, width)
+            out_in[two] = nn(hid[all_rows, :], down).astype(BF).reshape(2, t, width)
+
+            @pl.when(i == 0)
+            def _():
+                first[0].start()
+                first[2].start()
+
+            return carry
+
+        lax.fori_loop(0, 2, pair_rows, 0)
+        first[1].start()
+        first[3].start()
+        for i, part in enumerate(parts):
+            first[2 * i].wait_recv()
+            dp_land[i, 0] = (dp_land[i, 0].astype(F32) + part[xd].astype(F32)).astype(BF)
+            dp_next(i).start()
+
+        def tn(a, b):
+            return lax.dot_general(a, b, (((0,), (0,)), ((), ())), preferred_element_type=F32)
+
+        quarter = width // n_dp
+
+        def columns(j, carry):
+            lanes = pl.ds(pl.multiple_of(j * quarter, quarter), quarter)
+            some = nm[:, :, lanes].reshape(n_dp * t, quarter)
+            shape = gu_part.shape[2:]
+            gu_part[0, j] = tn(some, dg[...]).astype(BF).reshape(shape)
+            gu_part[1, j] = tn(some, du[...]).astype(BF).reshape(shape)
+            c_some = cot[:, :, lanes].reshape(n_dp * t, quarter)
+            wd_part[:, :, lanes] = tn(hid[...], c_some).astype(BF).reshape(wd_part.shape[:2] + (quarter,))
+            return carry
+
+        lax.fori_loop(0, n_dp, columns, 0)
+
+    def dp_next(i):
+        return remote(dp_land.at[i, 0], dp_land.at[i, 2], dp_send.at[i, 2], dp_recv.at[i, 2], (xd, c))
+
+    pl.run_scoped(
+        feed,
+        *[pltpu.VMEM((2 * t, ffq), F32)] * 3,
+        *[pltpu.VMEM((n_dp * t, ffq), BF)] * 3,
+    )
+    second = [dp_next(i) for i in range(2)]
     cut = -(-wd_part.shape[1] // 16) * 8
 
     def wd_half(ref, w):
         return ref.at[:cut] if w == 0 else ref.at[cut:]
 
-    gr = ScatterRing(
+    gs = ScatterRing(
         n, lambda o: gu_part.at[:, :, o], lambda o, w: gu_part.at[w, :, o], gu_land,
-        None, lambda ref, w: ref.at[w], ring_send.at[0], ring_recv.at[0],
-    )
-    dr = ScatterRing(
+        None, lambda ref, w: ref.at[w], ring_send.at[6], ring_recv.at[6],
+    )
+    ds_ = ScatterRing(
         n, lambda o: wd_part.at[o], lambda o, w: wd_half(wd_part.at[o], w), wd_land,
-        None, wd_half, ring_send.at[1], ring_recv.at[1],
-    )
-    large = (gr, dr)
-    for one in large:
+        None, wd_half, ring_send.at[7], ring_recv.at[7],
+    )
+    scatter = (gs, ds_)
+    for one in scatter:
         one.start()
-    second = []
-    for i, part in enumerate(parts):
-        first[2 * i].wait_recv()
-        dp_land[i, 0] = (dp_land[i, 0].astype(F32) + part[xd].astype(F32)).astype(BF)
-        second.append(
-            remote(dp_land.at[i, 0], dp_land.at[i, 2], dp_send.at[i, 2], dp_recv.at[i, 2], (xd, c))
-        )
-        second[-1].start()
     fs = PairScatter(
         n, fac_part, fac_held, fac_land, fac_own, pair_send.at[0], pair_recv.at[0],
-        ring_send.at[2], ring_recv.at[2],
+        ring_send.at[8], ring_recv.at[8],
     )
     ws = PairScatter(
         n, wo_part, wo_held, wo_land, wo_own, pair_send.at[1], pair_recv.at[1],
-        ring_send.at[3], ring_recv.at[3],
+        ring_send.at[9], ring_recv.at[9],
     )
     h = n // 2
 
     def advance(s):
-        for one in large:
+        for one in scatter:
             one.step(s)
 
     advance(1)
@@ -677,14 +735,11 @@
         first[2 * i + 1].wait_recv()
     second[0].wait_recv()
     middle = mid_ref[...]
-    r2 = lax.rsqrt(jnp.mean(middle * middle, axis=-1, keepdims=True) + EPS)
-    w = fac[...].reshape(width, FPAD)
-    g1, g2 = gain_rows(w)
     dn = dn_in[d].astype(F32) + dp_land[0, 1].astype(F32) + dp_land[0, 2].astype(F32)
     second_part = jnp.sum(dn * middle * r2, axis=0, keepdims=True)
     u2 = dn * g2
     d_middle = (
-        cot_ref[...].astype(F32)
+        cot_in[...].astype(F32)
         + r2 * u2
         - middle * (r2 * r2 * r2 * jnp.mean(u2 * middle, axis=-1, keepdims=True))
     )
@@ -712,29 +767,51 @@
             ws.ring.step(1)
             serve(2)
 
-    attend_back_part(
-        nblk, serve_pair, da_ref, af_ref, inv_ref, p_copy, pbuf, q_ref, kv_ref, a_ref, b_ref,
-        cos_ref, sin_ref, dq_ref, dkv, ka, kb, dka, dqa, db,
-    )
-    dkv16[...] = dkv[...].astype(BF)
-
-    def kv_copy(k):
-        src = dkv16.at[:, (nblk - 1 - k) * t : (nblk - k) * t]
-        return remote(src, kv_land.at[k - 1], kv_send.at[k - 1], kv_recv.at[k - 1], (d, (c + n - k) % n))
-
-    for k in range(1, nblk):
-        @pl.when(c - k >= 0)
-        def _():
-            kv_copy(k).start()
-    own_kv = dkv.at[:, (nblk - 1) * t :]
-    serve(3)
-    for k in range(1, nblk):
-        @pl.when(c + k < n)
-        def _():
-            kv_copy(k).wait_recv()
-            own_kv[...] += kv_land[k - 1].astype(F32)
+    def p_copy(p):
+        return pltpu.make_async_copy(p_ref.at[p], pbuf.at[p % 2], p_sem.at[p % 2])
+
+    p_copy(0).start()
+
+    def attention_back(ka, dka, dqa, db, dkv, dkv16):
+        attend_back_part(
+            nblk, serve_pair, da_ref, af_ref, inv_ref, p_copy, pbuf, q_ref, kv_ref, a_ref, b_ref,
+            cos_ref, sin_ref, dq_ref, dkv, ka, dka, dqa, db,
+        )
+        dkv16[...] = dkv[...].astype(BF)
+
+        def dkv_copy(k):
+            src = dkv16.at[:, (nblk - 1 - k) * t : (nblk - k) * t]
+            return remote(
+                src, kv_land.at[k - 1], dkv_send.at[k - 1], dkv_recv.at[k - 1], (d, (c + n - k) % n)
+            )
+
+        for k in range(1, nblk):
+            @pl.when(c - k >= 0)
+            def _():
+                dkv_copy(k).start()
+        serve(3)
+        own_dkv[...] = dkv[:, (nblk - 1) * t :]
+        for k in range(1, nblk):
+            @pl.when(c + k < n)
+            def _():
+                dkv_copy(k).wait_recv()
+                own_dkv[...] += kv_land[k - 1].astype(F32)
+        for k in range(1, nblk):
+            @pl.when(c - k >= 0)
+            def _():
+                dkv_copy(k).wait_send()
+
+    pl.run_scoped(
+        attention_back,
+        pltpu.VMEM((2 * AK, 1, nblk * t), F32),
+        pltpu.VMEM((2 * AK, 1, nblk * t), F32),
+        pltpu.VMEM((AQ, 1, t), F32),
+        pltpu.VMEM((BQ, t), F32),
+        pltpu.VMEM((PACK, nblk * t), F32),
+        pltpu.VMEM((PACK, nblk * t), BF),
+    )
     steps(2, h, ws.ring.step)
-    dp = own_kv[...]
+    dp = own_dkv[...]
     d_bk = rope_back(dp[AK : AK + BK], cos_ref[...], sin_ref[...], RKV)
     d_fac_t = jnp.concatenate(
         [dq_ref[...], dp[:AK], d_bk, dp[KEY_ROWS:], jnp.zeros((FPAD - FDIM, t), F32)], axis=0
@@ -757,42 +834,48 @@
         dmid_ref[...] + r1 * u1 - x * (r1 * r1 * r1 * jnp.mean(u1 * x, axis=-1, keepdims=True))
     ).astype(BF)
     fs.enter()
-    total = gr.result().astype(BF)
+    total = gs.result().astype(BF)
     for dd in range(n_dp):
         gu_own[dd] = total[:, dd]
-    keep = pltpu.make_async_copy(gu_own.at[d], gu_ref.at[d], own_sem)
+    keep = pltpu.make_async_copy(gu_own.at[d], gu_ref.at[d], own_sem.at[0])
     keep.start()
-    a2a = []
+    last = []
     for k in range(1, n_dp):
         to = (d + k) % n_dp
-        a2a.append(
+        last.append(
             (
-                remote(gu_own.at[to], gu_ref.at[d], near_send.at[k - 1], near_recv.at[k - 1], (to, c)),
+                remote(gu_own.at[to], gu_ref.at[d], end_send.at[k - 1], end_recv.at[k - 1], (to, c)),
                 remote(
                     gu_own.at[to], gu_ref.at[(d + n_dp - k) % n_dp],
-                    near_send.at[k - 1], near_recv.at[k - 1], (to, c),
+                    end_send.at[k - 1], end_recv.at[k - 1], (to, c),
                 ),
             )
         )
-        a2a[-1][0].start()
+        last[-1][0].start()
     ws.leave()
     fs.ring.step(1)
-    wd_ref[...] = dr.result()
+    wd_ref[...] = ds_.result()
     steps(2, h, fs.ring.step)
     wo_ref[...] = ws.result()
     fs.leave()
-    for out, arrival in a2a:
+    for out, arrival in last:
         arrival.wait_recv()
         out.wait_send()
     keep.wait()
     fac_ref[...] = fs.result()
+    for copy in first + second:
+        copy.wait_send()
+    for one in scatter + (ws, fs):
+        one.drain()
     for k in range(1, nblk):
-        @pl.when(c - k >= 0)
+        @pl.when(c + k < n)
         def _():
             kv_copy(k).wait_send()
-    for copy in first + second:
-        copy.wait_send()
-    for one in large + (ws, fs):
+    fswap.wait_send()
+    oswap.wait_send()
+    for out, _ in a2a + near:
+        out.wait_send()
+    for one in small + large:
         one.drain()
 
 
@@ -810,7 +893,7 @@
 
 def talks(i):
     return pltpu.CompilerParams(
-        collective_id=i, has_side_effects=True, vmem_limit_bytes=60 * 1024 * 1024
+        collective_id=i, has_side_effects=True, vmem_limit_bytes=63 * 1024 * 1024
     )
 
 
@@ -860,74 +943,8 @@
     cot_own = cotangent.reshape(t, width)
     sds = jax.ShapeDtypeStruct
     down_rows = down_weights.shape[0]
-    (
-        normed_t, q_t, a_t, b_t, kv, attn_t, attn_f, inv, probs, fac, wo, gu, wd, nm_all, cot, middle
-    ) = pl.pallas_call(
-        functools.partial(front_kernel, n_ctx, nblk),
-        out_shape=(
-            sds((width, t), BF),
-            sds((H * DH, t), BF),
-            sds((AQ, 1, t), F32),
-            sds((BQ, t), F32),
-            sds((PACK, nblk * t), BF),
-            sds((H * DH, t), BF),
-            sds((H * DH, t), F32),
-            sds((H // 2, 8, 2 * t), F32),
-            sds((H // 2, nblk * t, 2 * t), BF),
-            sds((n_dp, n_ctx, rows, FPAD), BF),
-            sds((n_dp, n_ctx, rows, width), BF),
-            sds((2, n_dp, n_ctx, rows, ffq), BF),
-            sds((n_ctx, down_rows, width), BF),
-            sds((n_dp, t, width), BF),
-            sds((n_dp, t, width), BF),
-            sds((t, width), F32),
-        ),
-        in_specs=[SMEM] + vmem(8),
-        out_specs=tuple(vmem(16)),
-        scratch_shapes=[
-            pltpu.VMEM((2 * AK, 1, nblk * t), F32),
-            pltpu.VMEM((2 * BK, nblk * t), F32),
-            pltpu.VMEM((nblk * t, t), F32),
-            DMA((5,)),
-            DMA((9,)),
-            DMA((9,)),
-            DMA((6, 2, h)),
-            DMA((6, 2, h)),
-            DMA((nblk - 1,)),
-            DMA((nblk - 1,)),
-            DMA((2, 3)),
-            DMA((2, 3)),
-        ],
-        compiler_params=talks(0),
-        name="front",
-    )(doc_lengths, x16, cosine, sine, pack, output_weights.astype(BF), gu_in,
-      down_weights.astype(BF), cot_own)
-
-    gu = gu.reshape(2, width, ffq)
-    wg, wu = gu[0], gu[1]
-    wd = wd.reshape(n_ctx * down_rows, width)
-    nm_all = nm_all.reshape(n_dp * t, width)
-    cot = cot.reshape(n_dp * t, width)
-
-    gate = nn(nm_all, wg)
-    upward = nn(nm_all, wu)
-    sig, act = silu_parts(gate)
-    hidden = (act * upward).astype(BF)
-    d_hidden = nt(cot, wd)
-    d_gate = (d_hidden * upward * sig * (1.0 + gate * (1.0 - sig))).astype(BF)
-    d_up = (d_hidden * act).astype(BF)
-    dn_part = (nt(d_gate, wg) + nt(d_up, wu)).astype(BF).reshape(n_dp, t, width)
-    out_part = nn(hidden, wd).astype(BF).reshape(n_dp, t, width)
-
-    def tn(a, b):
-        return lax.dot_general(a, b, (((0,), (0,)), ((), ())), preferred_element_type=F32)
-
-    gu_part = jnp.stack([tn(nm_all, d_gate), tn(nm_all, d_up)]).astype(BF)
-    gu_part = gu_part.reshape(2, n_dp, n_ctx, rows, ffq)
-    wd_part = tn(hidden, cot).astype(BF).reshape(n_ctx, down_rows, width)
-
-    layer_output, input_grad, last_own, out_own, gu_own, down_sum = pl.pallas_call(
-        functools.partial(back_kernel, n_ctx, nblk),
+    outs = pl.pallas_call(
+        functools.partial(block_kernel, n_ctx, nblk),
         out_shape=(
             sds((t, width), BF),
             sds((t, width), BF),
@@ -935,17 +952,31 @@
             sds((rows, width), F32),
             sds((n_dp, 2, rows, ffq), BF),
             sds((down_rows, width), F32),
+            sds((H // 2, nblk * t, 2 * t), BF),
         ),
-        in_specs=vmem(13) + hbm(1) + vmem(6),
-        out_specs=tuple(vmem(6)),
+        in_specs=[SMEM] + vmem(8),
+        out_specs=tuple(vmem(6) + hbm(1)),
         scratch_shapes=[
-            pltpu.VMEM((2 * AK, 1, nblk * t), F32),
-            pltpu.VMEM((2 * BK, nblk * t), F32),
-            pltpu.VMEM((2 * AK, 1, nblk * t), F32),
+            pltpu.VMEM((width, t), BF),
+            pltpu.VMEM((H * DH, t), BF),
             pltpu.VMEM((AQ, 1, t), F32),
             pltpu.VMEM((BQ, t), F32),
-            pltpu.VMEM((PACK, nblk * t), F32),
             pltpu.VMEM((PACK, nblk * t), BF),
+            pltpu.VMEM((H * DH, t), BF),
+            pltpu.VMEM((H * DH, t), F32),
+            pltpu.VMEM((H // 2, 8, 2 * t), F32),
+            pltpu.VMEM((2, nblk * t, 2 * t), BF),
+            pltpu.VMEM((n_dp, n_ctx, rows, FPAD), BF),
+            pltpu.VMEM((n_dp, n_ctx, rows, width), BF),
+            pltpu.VMEM((2, n_dp, n_ctx, rows, ffq), BF),
+            pltpu.VMEM((n_ctx, down_rows, width), BF),
+            pltpu.VMEM((n_dp, t, width), BF),
+            pltpu.VMEM((n_dp, t, width), BF),
+            pltpu.VMEM((t, width), F32),
+            pltpu.VMEM((n_dp, t, width), BF),
+            pltpu.VMEM((n_dp, t, width), BF),
+            pltpu.VMEM((2, n_dp, n_ctx, rows, ffq), BF),
+            pltpu.VMEM((n_ctx, down_rows, width), BF),
             pltpu.VMEM((nblk - 1, PACK, t), BF),
             pltpu.VMEM((2, h, 2, n_dp, rows, ffq), BF),
             pltpu.VMEM((2, h, down_rows, width), BF),
@@ -962,9 +993,15 @@
             pltpu.VMEM((2, h, 2, rows, width), BF),
             pltpu.VMEM((3, rows, FPAD), BF),
             pltpu.VMEM((3, rows, width), BF),
-            DMA,
-            DMA((4, 2, h)),
-            DMA((4, 2, h)),
+            DMA((5,)),
+            DMA((9,)),
+            DMA((9,)),
+            DMA((10, 2, h)),
+            DMA((10, 2, h)),
+            DMA((nblk - 1,)),
+            DMA((nblk - 1,)),
+            DMA((2, 3)),
+            DMA((2, 3)),
             DMA((nblk - 1,)),
             DMA((nblk - 1,)),
             DMA((3,)),
@@ -973,13 +1010,14 @@
             DMA((2, 3)),
             DMA((2, 3)),
             DMA((2, 3)),
-            pltpu.VMEM((2, nblk * t, 2 * t), BF),
             DMA((2,)),
+            pltpu.VMEM((PACK, t), F32),
         ],
-        compiler_params=talks(1),
-        name="back",
-    )(gu_part, wd_part, dn_part, out_part, middle, cot_own, x16, fac, wo, attn_t, normed_t,
-      attn_f, inv, probs, q_t, kv, a_t, b_t, cosine, sine)
+        compiler_params=talks(0),
+        name="block",
+    )(doc_lengths, x16, cosine, sine, pack, output_weights.astype(BF), gu_in,
+      down_weights.astype(BF), cot_own)
+    layer_output, input_grad, last_own, out_own, gu_own, down_sum = outs[:6]
     gu_own = gu_own.astype(F32).transpose(1, 2, 0, 3).reshape(2, rows, ff)
     return (
         layer_output.reshape(1, t, width),

time: 220 us -> 206 us (0.936)
  matrix products: 12.6 us -> 0 us
  local copies, waits for them, and re-layouts: 11.2 us -> 8.32 us
    dot_general x9 -> x0, matrix products: 12.6 us -> none  [the longest x3 4.6 us: nn(): return jnp.dot(a, b, preferred_element_type=F32)]
    slice x1 -> x0, local copies, waits for them, and re-layouts: 2.3 us -> none  [body(): wg, wu = (gu[0], gu[1])]
    pallas_call x2 -> x1, Pallas kernels: 186 us -> 186 us  [body(): pl.pallas_call(functools.partial(block_kernel, n_ctx, nblk), out_shape=(s...]
where the time goes in v4:
time: 206 us; the launch traced here: 205 us
  Pallas kernels  186 us (90%)
  other arithmetic  10.5 us (5%)
  local copies, waits for them, and re-layouts  8.32 us (4%)
    pallas_call x1, Pallas kernels, body(): pl.pallas_call(functools.partial(block_kernel, n_ctx, nblk), out_shape=(s...  186 us

profile of v4, /device:TPU:0, one launch (start us, length us, event | category | flops | bytes accessed | tf_op | source)
XLA Modules:
  0.0 205.3 jit_solution(7060375963916875740)
XLA Ops:
  0.6 0.0 copy-start
  0.7 0.7 convert_bitcast_fusion.2
  1.4 0.7 convert_bitcast_fusion.1
  2.0 0.1 pad.5.clone
  2.1 0.1 copy.23
  2.2 0.1 copy.22
  2.3 1.4 multiply_sine_fusion
  3.7 0.9 convert.22
  4.6 0.7 maximum_maximum_fusion.fac_in
  5.3 1.5 convert_element_type.18.wo_in
  6.9 1.0 convert.25
  7.9 0.2 stack.9
  8.2 1.0 convert.26
  9.2 0.2 stack.10
  9.4 0.8 maximum_bitcast_fusion.gu_in
  10.3 0.0 copy-done
  10.3 0.7 convert_element_type.19.wd_in
  11.0 185.7 %block.1 = (bf16[128,1024]{1,0:T(8,128)(2,1)}, bf16[128,1024]{1,0:T(8,128)(2,1)}, f32[32,896]{1,0:T(8,128)}, f32[32,1024]{1,0:T(8,128)}, bf16[4,2,32,704]{3,2,1,...) custom-call(s32[1,8]{1,0:T(1,128)} %len_ref.1, bf16[128,1024]{1,0:T(8,128)(2,1)} %bitcast.15, ...), custom_call_target="tpu_custom_call" | custom-call | tf_op jit(solution)/shard_map/block/pallas_call | solution.py:946
  196.7 1.5 slice_reduce_fusion
  198.2 1.1 convert_bitcast_fusion
  199.3 0.1 fusion
  199.4 0.3 copy.27
  199.6 1.0 squeeze.15
  200.6 0.3 copy.26
  200.9 1.0 squeeze.14
  201.9 0.0 copy-done.3
  201.9 0.7 copy.33
  202.6 0.7 copy.34
  203.3 0.0 copy-done.4
  203.3 0.6 copy.35
  203.9 0.7 copy.36
  204.6 0.7 copy.37
  (12 shorter events, 0.1 us)
Async XLA Ops:
  0.6 9.6 %copy-start = (f32[88,1024]{1,0:T(8,128)S(1)}, f32[88,1024]{1,0:T(8,128)}, u32[]{:S(2)}) copy-start(f32[88,1024]{1,0:T(8,128)} %param.19) | copy-start | bytes 1081348
  199.3 2.6 %copy-start.3 = (bf16[128,1024]{1,0:T(8,128)(2,1)S(1)}, bf16[128,1024]{1,0:T(8,128)(2,1)}, u32[]{:S(2)}) copy-start(bf16[128,1024]{1,0:T(8,128)(2,1)} %get-tuple-element.15) | copy-start | bytes 786436
  199.3 3.3 %copy-start.2 = (bf16[128,1024]{1,0:T(8,128)(2,1)S(1)}, bf16[128,1024]{1,0:T(8,128)(2,1)}, u32[]{:S(2)}) copy-start(bf16[128,1024]{1,0:T(8,128)(2,1)} %get-tuple-element.16) | copy-start | bytes 786436
  199.3 4.0 %copy-start.4 = (f32[32,896]{1,0:T(8,128)S(1)}, f32[32,896]{1,0:T(8,128)}, u32[]{:S(2)}) copy-start(f32[32,896]{1,0:T(8,128)} %get-tuple-element.17) | copy-start | bytes 344068
  199.3 4.6 %copy-start.5 = (f32[32,1024]{1,0:T(8,128)S(1)}, f32[32,1024]{1,0:T(8,128)}, u32[]{:S(2)}) copy-start(f32[32,1024]{1,0:T(8,128)} %get-tuple-element.40) | copy-start | bytes 393220
  199.4 5.2 %copy-start.1 = (f32[88,1024]{1,0:T(8,128)S(1)}, f32[88,1024]{1,0:T(8,128)}, u32[]{:S(2)}) copy-start(f32[88,1024]{1,0:T(8,128)} %get-tuple-element.44) | copy-start | bytes 1081348

commit v5 on v4

--- a/solution.py
+++ b/solution.py
@@ -60,26 +60,18 @@
     return d, c, core, d + 1 - 2 * core, (d + 2) % 4
 
 
-def meet(n, near):
+def greet(n):
     d, c, _, _, _ = places()
     barrier = pltpu.get_barrier_semaphore()
-    count = 0
     n_dp = lax.axis_size("dp")
     for k in range(1, n_dp):
         pl.semaphore_signal(barrier, inc=1, device_id=((d + k) % n_dp, c), device_id_type=MESH)
-        count += 1
-    if near:
-        r = ring_place(c, n)
-        for way in (1, -1):
-            pl.semaphore_signal(
-                barrier, inc=1, device_id=(d, ring_index(r + way, n)), device_id_type=MESH
-            )
-            count += 1
-    else:
-        for k in range(1, n):
-            pl.semaphore_signal(barrier, inc=1, device_id=(d, (c + k) % n), device_id_type=MESH)
-            count += 1
-    pl.semaphore_wait(barrier, count)
+    for k in range(1, n):
+        pl.semaphore_signal(barrier, inc=1, device_id=(d, (c + k) % n), device_id_type=MESH)
+
+
+def met(n):
+    pl.semaphore_wait(pltpu.get_barrier_semaphore(), n + lax.axis_size("dp") - 2)
 
 
 def steps(lo, hi, step):
@@ -124,6 +116,53 @@
         steps(0, self.h - 1, lambda s: [self.copy(s, i).wait_send() for i in range(2)])
         for i in range(2):
             self.copy(self.h - 1, i).wait_send()
+
+
+class WideGather:
+    def __init__(self, n, ref, half, send, recv, x_send, x_recv):
+        self.d, self.c, _, _, self.xd = places()
+        self.n, self.h, self.ref = n, n // 2, ref
+        self.x_send, self.x_recv = x_send, x_recv
+        self.ring = GatherRing(
+            n, lambda o: ref.at[self.d, o], lambda o, w: half(ref.at[self.d, o], w), send, recv
+        )
+
+    def pass_on(self, i, owner, arriving=False):
+        ref = self.ref.at[self.xd if arriving else self.d, owner]
+        return remote(ref, ref, self.x_send.at[i], self.x_recv.at[i], (self.xd, self.c))
+
+    def owner(self, s, i):
+        return ring_index(self.ring.r - (1 - 2 * i) * (s + 1), self.n)
+
+    def start(self, now):
+        if now:
+            self.pass_on(0, self.c).start()
+        self.ring.start(0)
+
+    def step(self, s, now):
+        self.ring.step(s)
+        if now:
+            for i in range(2):
+                self.pass_on(2 * s - 1 + i, self.owner(s - 1, i)).start()
+
+    def finish(self, now):
+        self.ring.arrive(self.h - 1)
+        if now:
+            self.pass_on(self.n - 1, self.owner(self.h - 1, 0)).start()
+        else:
+            self.passed(lambda i, o: self.pass_on(i, o).start())
+
+    def passed(self, wait):
+        wait(0, self.c)
+        steps(0, self.h - 1, lambda s: [wait(1 + 2 * s + i, self.owner(s, i)) for i in range(2)])
+        wait(self.n - 1, self.owner(self.h - 1, 0))
+
+    def arrive(self):
+        self.passed(lambda i, o: self.pass_on(i, o, True).wait_recv())
+
+    def drain(self):
+        self.ring.drain()
+        self.passed(lambda i, o: self.pass_on(i, o).wait_send())
 
 
 class ScatterRing:
@@ -423,14 +462,26 @@
     return gains[FDIM - first : FDIM - first + 1], gains[FDIM - first + 1 : FDIM - first + 2]
 
 
+def lane_half(ref, w):
+    return ref.at[:, :512] if w == 0 else ref.at[:, 512:]
+
+
 class PairScatter:
-    def __init__(self, n, part, held, land, own, send, recv, ring_send, ring_recv):
+    def __init__(self, n, part, held, land, own, send, recv, ring_send, ring_recv, x_first=None):
         d, c, core, cd, xd = places()
+        self.x_first = x_first
         self.core, self.x, self.part, self.held, self.own = core, d // 2, part, held, own
         self.swaps = [
             remote(part.at[2 * xx + 1 - core], held.at[xx], send.at[xx], recv.at[xx], (cd, c))
             for xx in range(2)
         ]
+        if x_first is not None:
+            self.end = remote(held.at[1 - self.x], x_first, send.at[2], recv.at[2], (xd, c))
+            self.ring = ScatterRing(
+                n, lambda o: x_first.at[o], lambda o, w: lane_half(x_first.at[o], w), land,
+                None, lane_half, ring_send, ring_recv,
+            )
+            return
         self.end = remote(own.at[1 - self.x], own.at[2], send.at[2], recv.at[2], (xd, c))
         self.ring = ScatterRing(
             n, lambda o: held.at[:, o], lambda o, w: held.at[w, o], land,
@@ -446,6 +497,15 @@
             self.swaps[xx].wait_recv()
             mine = self.part[2 * xx + self.core].astype(F32)
             self.held[xx] = (self.held[xx].astype(F32) + mine).astype(BF)
+        if self.x_first is None:
+            self.ring.start()
+        else:
+            self.end.start()
+
+    def across(self):
+        self.end.wait_recv()
+        total = self.x_first[...].astype(F32) + self.held[self.x].astype(F32)
+        self.x_first[...] = total.astype(BF)
         self.ring.start()
 
     def leave(self):
@@ -466,66 +526,72 @@
 
 def block_kernel(
     n, nblk,
-    len_ref, x_ref, cos_ref, sin_ref, fac_in, wo_in, gu_in, wd_in, cot_in,
-    y_ref, dx_ref, fac_ref, wo_ref, gu_ref, wd_ref, p_ref,
+    len_ref, x_ref, cos_ref, sin_ref, fw_ref, g1_ref, g2_ref, ow_ref, gw_ref, uw_ref, dw_ref, cot_in,
+    y_ref, dx_ref, fac_ref, gain1_ref, gain2_ref, wo_ref, gate_ref, up_ref, wd_ref, p_ref,
     nt_ref, q_ref, a_ref, b_ref, kv_ref, at_ref, af_ref, inv_ref, pbuf,
     fac, wo, gu, wd, nm, cot, mid_ref, dn_in, out_in, gu_part, wd_part,
     kv_land, gu_land, wd_land, gu_own, da_ref, dq_ref, dmid_ref, dp_land,
     fac_part, wo_part, fac_held, wo_held, fac_land, wo_land, fac_own, wo_own,
     own_sem, near_send, near_recv, ring_send, ring_recv, kv_send, kv_recv, sp_send, sp_recv,
     dkv_send, dkv_recv, end_send, end_recv, dp_send, dp_recv, pair_send, pair_recv, p_sem, own_dkv,
+    gu_in, gu_ref, x_send, x_recv,
 ):
     d, c, core, cd, xd = places()
     t = x_ref.shape[0]
     n_dp = 4
-    locals_ = [
-        pltpu.make_async_copy(fac_in, fac.at[d, c], own_sem.at[0]),
-        pltpu.make_async_copy(wo_in, wo.at[d, c], own_sem.at[1]),
-        pltpu.make_async_copy(gu_in.at[d], gu.at[:, d, c], own_sem.at[2]),
-        pltpu.make_async_copy(wd_in, wd.at[c], own_sem.at[3]),
-        pltpu.make_async_copy(cot_in, cot.at[d], own_sem.at[4]),
-    ]
-    for copy in locals_:
-        copy.start()
+    rows, ffq = gu_in.shape[1], gu_in.shape[2] // 2
+    greet(n)
+    keep_cot = pltpu.make_async_copy(cot_in, cot.at[d], own_sem.at[4])
+    keep_cot.start()
+    tail = FPAD - 128
+    lane = lax.broadcasted_iota(jnp.int32, (rows, 128), 1)
+    diag = lax.broadcasted_iota(jnp.int32, (rows, rows), 0) == lax.broadcasted_iota(
+        jnp.int32, (rows, rows), 1
+    )
+
+    def column(ref):
+        return jnp.sum(jnp.where(diag, ref[...], 0.0), axis=1, keepdims=True)
+
+    gains = jnp.where(lane == FDIM - tail, column(g1_ref), 0.0)
+    gains = jnp.where(lane == FDIM + 1 - tail, column(g2_ref), gains)
+    fac[d, c, :, :tail] = fw_ref[:, :tail].astype(BF)
+    fac[d, c, :, tail:] = gains.astype(BF)
+    fac[d, c, :, tail:FDIM] = fw_ref[:, tail:].astype(BF)
+    wo[d, c] = ow_ref[...].astype(BF)
+    wd[c] = dw_ref[...].astype(BF)
+    for dd in range(n_dp):
+        for side, ref in enumerate((gw_ref, uw_ref)):
+            gu_in[dd, :, side * ffq : (side + 1) * ffq] = ref[:, dd * ffq : (dd + 1) * ffq].astype(BF)
+    keep_gu = pltpu.make_async_copy(gu_in.at[d], gu.at[d, c], own_sem.at[2])
+    keep_gu.start()
     for k in range(1, nblk):
         @pl.when(c - k < 0)
         def _():
             kv_ref[:, (nblk - 1 - k) * t : (nblk - k) * t] = jnp.zeros((PACK, t), BF)
-    meet(n, False)
-    for copy in locals_:
-        copy.wait()
-
-    def ring(i, slot, half):
-        return GatherRing(n, slot, half, ring_send.at[i], ring_recv.at[i])
-
-    rows = fac_in.shape[0] // 2
-
-    def shard(ref, dd):
-        return (lambda o: ref.at[dd, o]), (lambda o, w: ref.at[dd, o, w * rows : (w + 1) * rows])
-
-    fo, fx = ring(0, *shard(fac, d)), ring(1, *shard(fac, xd))
-    oo, ox = ring(2, *shard(wo, d)), ring(3, *shard(wo, xd))
-    cut = -(-wd_in.shape[0] // 16) * 8
-    gr = ring(4, lambda o: gu.at[:, :, o], lambda o, w: gu.at[w, :, o])
-    dr = ring(
-        5, lambda o: wd.at[o],
-        lambda o, w: wd.at[o, :cut] if w == 0 else wd.at[o, cut:],
-    )
-    small, large = (fo, fx, oo, ox), (gr, dr)
-    fswap = remote(fac.at[d, c], fac.at[d, c], near_send.at[0], near_recv.at[0], (xd, c))
-    oswap = remote(wo.at[d, c], wo.at[d, c], near_send.at[1], near_recv.at[1], (xd, c))
-    fswap.start()
-    oswap.start()
-    fo.start(0)
-    oo.start(0)
+    met(n)
+
+    fo = WideGather(n, fac, lane_half, ring_send.at[0], ring_recv.at[0], x_send.at[0], x_recv.at[0])
+    oo = WideGather(n, wo, lane_half, ring_send.at[1], ring_recv.at[1], x_send.at[1], x_recv.at[1])
+    cut = -(-dw_ref.shape[0] // 16) * 8
+    gr = GatherRing(
+        n, lambda o: gu.at[:, o], lambda o, w: gu.at[2 * w : 2 * w + 2, o],
+        ring_send.at[4], ring_recv.at[4],
+    )
+    dr = GatherRing(
+        n, lambda o: wd.at[o], lambda o, w: wd.at[o, :cut] if w == 0 else wd.at[o, cut:],
+        ring_send.at[5], ring_recv.at[5],
+    )
+    small, large = (fo, oo), (gr, dr)
+    fo.start(True)
+    oo.start(False)
     a2a = []
     for k in range(1, n_dp):
         to = (d + k) % n_dp
         a2a.append(
             (
-                remote(gu_in.at[to], gu.at[:, d, c], near_send.at[1 + k], near_recv.at[1 + k], (to, c)),
+                remote(gu_in.at[to], gu.at[d, c], near_send.at[1 + k], near_recv.at[1 + k], (to, c)),
                 remote(
-                    gu_in.at[to], gu.at[:, (d + n_dp - k) % n_dp, c],
+                    gu_in.at[to], gu.at[(d + n_dp - k) % n_dp, c],
                     near_send.at[1 + k], near_recv.at[1 + k], (to, c),
                 ),
             )
@@ -533,18 +599,14 @@
         a2a[-1][0].start()
     cots = Spread(cot, sp_send.at[0], sp_recv.at[0])
     nms = Spread(nm, sp_send.at[1], sp_recv.at[1])
-    cots.start()
-    fswap.wait_recv()
-    fx.start(0)
-    oswap.wait_recv()
-    ox.start(0)
-    steps(1, n // 2 - 1, lambda s: [one.step(s) for one in small])
-    for one in small:
-        one.last()
+    steps(1, n // 2 - 1, lambda s: (fo.step(s, True), oo.step(s, False)))
+    fo.step(n // 2 - 1, True)
+    oo.step(n // 2 - 1, False)
+    keep_gu.wait()
     for _, arrival in a2a:
         arrival.wait_recv()
-    for one in large:
-        one.start(0)
+    gr.start(0)
+
     def core_swap(ref, i, dd, da):
         return (
             remote(ref.at[dd], ref.at[dd], near_send.at[5 + i], near_recv.at[5 + i], (cd, c)),
@@ -552,14 +614,20 @@
         )
 
     near = []
-    for i, (one, ref, dd, da) in enumerate(
-        ((fo, fac, d, cd), (fx, fac, xd, (cd + 2) % 4), (oo, wo, d, cd), (ox, wo, xd, (cd + 2) % 4))
-    ):
-        one.arrive(n // 2 - 1)
+
+    def swap(i, ref, dd, da):
         near.append(core_swap(ref, i, dd, da))
         near[-1][0].start()
-    cots.forward()
-    for _, arrival in near[:2]:
+
+    fo.finish(True)
+    swap(0, fac, d, cd)
+    oo.finish(False)
+    swap(2, wo, d, cd)
+    fo.arrive()
+    swap(1, fac, xd, (cd + 2) % 4)
+    keep_cot.wait()
+    cots.start()
+    for _, arrival in (near[0], near[2]):
         arrival.wait_recv()
 
     width = x_ref.shape[1]
@@ -577,10 +645,16 @@
         @pl.when(c + k < n)
         def _():
             kv_copy(k).start()
+    dr.start(0)
+    oo.arrive()
+    swap(3, wo, xd, (cd + 2) % 4)
     for k in range(1, nblk):
         @pl.when(c - k >= 0)
         def _():
             kv_copy(k).wait_recv()
+    full = n // 2 - 1
+    middle_step = 1 + full // 2
+    steps(1, middle_step, lambda s: [one.step(s) for one in large])
 
     def p_out(p):
         return pltpu.make_async_copy(pbuf.at[p % 2], p_ref.at[p], p_sem.at[p % 2])
@@ -593,20 +667,18 @@
         pltpu.VMEM((nblk * t, t), F32),
     )
 
-    full = n // 2 - 1
-    middle_step = 1 + full // 2
-    steps(1, middle_step, lambda s: [one.step(s) for one in large])
-    for _, arrival in near[2:]:
+    for _, arrival in (near[1], near[3]):
         arrival.wait_recv()
     middle = x + nn(at_ref[...].T, wo[...].reshape(width, width))
     mid_ref[...] = middle
     r2 = lax.rsqrt(jnp.mean(middle * middle, axis=-1, keepdims=True) + EPS)
     nm[d] = (middle * r2 * g2).astype(BF)
     nms.start()
+    cots.forward()
+    steps(middle_step, full, lambda s: [one.step(s) for one in large])
     nms.forward()
     nms.finish()
     cots.finish()
-    steps(middle_step, full, lambda s: [one.step(s) for one in large])
     for one in large:
         one.last()
     for one in large:
@@ -623,40 +695,34 @@
                     dp_send.at[i, j], dp_recv.at[i, j], (cd, c),
                 )
             )
-    ffq = gu_in.shape[3]
-
-    def feed(gate, up, dh, hid, dg, du):
-        wg, wu = (gu.at[side] for side in range(2))
-
-        def matrix(ref):
-            return ref[...].reshape(width, ffq)
-
+
+    def feed(both_ff, dh, hid, dgu):
         down = wd[...].reshape(ffq, width)
+
+        def matrix():
+            return gu[...].reshape(width, 2 * ffq)
 
         def pair_rows(i, carry):
             xx = i * x_at + (1 - i) * (1 - x_at)
             two = pl.ds(2 * xx, 2)
             both = 2 * t
-            nm_two = nm[two].reshape(both, width)
-            gate[...] = nn(nm_two, matrix(wg))
-            up[...] = nn(nm_two, matrix(wu))
+            both_ff[...] = nn(nm[two].reshape(both, width), matrix())
             dh[...] = nt(cot[two].reshape(both, width), down)
             base = pl.multiple_of(xx * both, both)
 
             def rows_of(k, carry):
                 some = pl.ds(pl.multiple_of(k * 32, 32), 32)
                 to = pl.ds(pl.multiple_of(base + k * 32, 32), 32)
-                v, u, g = gate[some, :], up[some, :], dh[some, :]
+                v, u, g = both_ff[some, :ffq], both_ff[some, ffq:], dh[some, :]
                 sig, act = silu_parts(v)
                 hid[to, :] = (act * u).astype(BF)
-                dg[to, :] = (g * u * sig * (1.0 + v * (1.0 - sig))).astype(BF)
-                du[to, :] = (g * act).astype(BF)
+                dgu[to, :ffq] = (g * u * sig * (1.0 + v * (1.0 - sig))).astype(BF)
+                dgu[to, ffq:] = (g * act).astype(BF)
                 return carry
 
             lax.fori_loop(0, both // 32, rows_of, 0)
             all_rows = pl.ds(base, both)
-            dn = nt(dg[all_rows, :], matrix(wg)) + nt(du[all_rows, :], matrix(wu))
-            dn_in[two] = dn.astype(BF).reshape(2, t, width)
+            dn_in[two] = nt(dgu[all_rows, :], matrix()).astype(BF).reshape(2, t, width)
             out_in[two] = nn(hid[all_rows, :], down).astype(BF).reshape(2, t, width)
 
             @pl.when(i == 0)
@@ -682,9 +748,7 @@
         def columns(j, carry):
             lanes = pl.ds(pl.multiple_of(j * quarter, quarter), quarter)
             some = nm[:, :, lanes].reshape(n_dp * t, quarter)
-            shape = gu_part.shape[2:]
-            gu_part[0, j] = tn(some, dg[...]).astype(BF).reshape(shape)
-            gu_part[1, j] = tn(some, du[...]).astype(BF).reshape(shape)
+            gu_part[j] = tn(some, dgu[...]).astype(BF).reshape(gu_part.shape[1:])
             c_some = cot[:, :, lanes].reshape(n_dp * t, quarter)
             wd_part[:, :, lanes] = tn(hid[...], c_some).astype(BF).reshape(wd_part.shape[:2] + (quarter,))
             return carry
@@ -696,8 +760,10 @@
 
     pl.run_scoped(
         feed,
-        *[pltpu.VMEM((2 * t, ffq), F32)] * 3,
-        *[pltpu.VMEM((n_dp * t, ffq), BF)] * 3,
+        pltpu.VMEM((2 * t, 2 * ffq), F32),
+        pltpu.VMEM((2 * t, ffq), F32),
+        pltpu.VMEM((n_dp * t, ffq), BF),
+        pltpu.VMEM((n_dp * t, 2 * ffq), BF),
     )
     second = [dp_next(i) for i in range(2)]
     cut = -(-wd_part.shape[1] // 16) * 8
@@ -706,8 +772,8 @@
         return ref.at[:cut] if w == 0 else ref.at[cut:]
 
     gs = ScatterRing(
-        n, lambda o: gu_part.at[:, :, o], lambda o, w: gu_part.at[w, :, o], gu_land,
-        None, lambda ref, w: ref.at[w], ring_send.at[6], ring_recv.at[6],
+        n, lambda o: gu_part.at[:, o], lambda o, w: gu_part.at[2 * w : 2 * w + 2, o], gu_land,
+        None, lambda ref, w: ref.at[2 * w : 2 * w + 2], ring_send.at[6], ring_recv.at[6],
     )
     ds_ = ScatterRing(
         n, lambda o: wd_part.at[o], lambda o, w: wd_half(wd_part.at[o], w), wd_land,
@@ -722,7 +788,7 @@
     )
     ws = PairScatter(
         n, wo_part, wo_held, wo_land, wo_own, pair_send.at[1], pair_recv.at[1],
-        ring_send.at[9], ring_recv.at[9],
+        ring_send.at[9], ring_recv.at[9], wo_own,
     )
     h = n // 2
 
@@ -764,8 +830,8 @@
     def serve_pair(p):
         @pl.when(p == H // 2 - 3)
         def _():
-            ws.ring.step(1)
             serve(2)
+            ws.across()
 
     def p_copy(p):
         return pltpu.make_async_copy(p_ref.at[p], pbuf.at[p % 2], p_sem.at[p % 2])
@@ -810,7 +876,8 @@
         pltpu.VMEM((PACK, nblk * t), F32),
         pltpu.VMEM((PACK, nblk * t), BF),
     )
-    steps(2, h, ws.ring.step)
+    ws.ring.step(1)
+    steps(2, h - 1, ws.ring.step)
     dp = own_dkv[...]
     d_bk = rope_back(dp[AK : AK + BK], cos_ref[...], sin_ref[...], RKV)
     d_fac_t = jnp.concatenate(
@@ -834,9 +901,7 @@
         dmid_ref[...] + r1 * u1 - x * (r1 * r1 * r1 * jnp.mean(u1 * x, axis=-1, keepdims=True))
     ).astype(BF)
     fs.enter()
-    total = gs.result().astype(BF)
-    for dd in range(n_dp):
-        gu_own[dd] = total[:, dd]
+    gu_own[...] = gs.result().astype(BF)
     keep = pltpu.make_async_copy(gu_own.at[d], gu_ref.at[d], own_sem.at[0])
     keep.start()
     last = []
@@ -852,17 +917,25 @@
             )
         )
         last[-1][0].start()
-    ws.leave()
+    ws.ring.step(h - 1)
     fs.ring.step(1)
     wd_ref[...] = ds_.result()
     steps(2, h, fs.ring.step)
-    wo_ref[...] = ws.result()
+    wo_ref[...] = ws.ring.result()
     fs.leave()
     for out, arrival in last:
         arrival.wait_recv()
         out.wait_send()
     keep.wait()
-    fac_ref[...] = fs.result()
+    for dd in range(n_dp):
+        lanes = slice(dd * ffq, (dd + 1) * ffq)
+        gate_ref[:, lanes] = gu_ref[dd, :, :ffq].astype(F32)
+        up_ref[:, lanes] = gu_ref[dd, :, ffq:].astype(F32)
+    total = fs.result()
+    fac_ref[...] = total[:, :FDIM]
+    for i, ref in enumerate((gain1_ref, gain2_ref)):
+        one = total[:, FDIM + i : FDIM + i + 1]
+        ref[...] = jnp.sum(jnp.where(diag, one, 0.0), axis=0, keepdims=True)
     for copy in first + second:
         copy.wait_send()
     for one in scatter + (ws, fs):
@@ -871,12 +944,24 @@
         @pl.when(c + k < n)
         def _():
             kv_copy(k).wait_send()
-    fswap.wait_send()
-    oswap.wait_send()
     for out, _ in a2a + near:
         out.wait_send()
     for one in small + large:
         one.drain()
+
+
+def emit_kernel(*refs):
+    k = (len(refs) - 2) // 3
+    ins, outs, bufs, sems = refs[:k], refs[k : 2 * k], refs[2 * k : 3 * k], refs[3 * k :]
+    into = [pltpu.make_async_copy(a, b, sems[0].at[i]) for i, (a, b) in enumerate(zip(ins, bufs))]
+    out = [pltpu.make_async_copy(a, b, sems[1].at[i]) for i, (a, b) in enumerate(zip(bufs, outs))]
+    for copy in into:
+        copy.start()
+    for one, two in zip(into, out):
+        one.wait()
+        two.start()
+    for copy in out:
+        copy.wait()
 
 
 def vmem(n):
@@ -927,12 +1012,6 @@
 
     h = n_ctx // 2
 
-    pack = jnp.concatenate(
-        [factor_weights, first_gain[:, None], second_gain[:, None],
-         jnp.zeros((rows, FPAD - FDIM - 2), F32)], axis=1).astype(BF)
-    gu_in = jnp.stack([gate_weights, up_weights]).astype(BF).reshape(2, rows, n_dp, ffq)
-    gu_in = gu_in.transpose(2, 0, 1, 3)
-
     half = DH // 2
     freq = 10000.0 ** (-(np.arange(half) * 2.0 / DH))
     pos = (c * t + jnp.arange(t, dtype=jnp.int32)).astype(F32)
@@ -948,14 +1027,17 @@
         out_shape=(
             sds((t, width), BF),
             sds((t, width), BF),
-            sds((rows, FPAD), F32),
+            sds((rows, FDIM), F32),
+            sds((1, rows), F32),
+            sds((1, rows), F32),
             sds((rows, width), F32),
-            sds((n_dp, 2, rows, ffq), BF),
+            sds((rows, ff), F32),
+            sds((rows, ff), F32),
             sds((down_rows, width), F32),
             sds((H // 2, nblk * t, 2 * t), BF),
         ),
-        in_specs=[SMEM] + vmem(8),
-        out_specs=tuple(vmem(6) + hbm(1)),
+        in_specs=[SMEM] + vmem(11),
+        out_specs=tuple(vmem(9) + hbm(1)),
         scratch_shapes=[
             pltpu.VMEM((width, t), BF),
             pltpu.VMEM((H * DH, t), BF),
@@ -968,19 +1050,19 @@
             pltpu.VMEM((2, nblk * t, 2 * t), BF),
             pltpu.VMEM((n_dp, n_ctx, rows, FPAD), BF),
             pltpu.VMEM((n_dp, n_ctx, rows, width), BF),
-            pltpu.VMEM((2, n_dp, n_ctx, rows, ffq), BF),
+            pltpu.VMEM((n_dp, n_ctx, rows, 2 * ffq), BF),
             pltpu.VMEM((n_ctx, down_rows, width), BF),
             pltpu.VMEM((n_dp, t, width), BF),
             pltpu.VMEM((n_dp, t, width), BF),
             pltpu.VMEM((t, width), F32),
             pltpu.VMEM((n_dp, t, width), BF),
             pltpu.VMEM((n_dp, t, width), BF),
-            pltpu.VMEM((2, n_dp, n_ctx, rows, ffq), BF),
+            pltpu.VMEM((n_dp, n_ctx, rows, 2 * ffq), BF),
             pltpu.VMEM((n_ctx, down_rows, width), BF),
             pltpu.VMEM((nblk - 1, PACK, t), BF),
-            pltpu.VMEM((2, h, 2, n_dp, rows, ffq), BF),
+            pltpu.VMEM((2, h, n_dp, rows, 2 * ffq), BF),
             pltpu.VMEM((2, h, down_rows, width), BF),
-            pltpu.VMEM((n_dp, 2, rows, ffq), BF),
+            pltpu.VMEM((n_dp, rows, 2 * ffq), BF),
             pltpu.VMEM((H * DH, t), F32),
             pltpu.VMEM((AQ + BQ, t), F32),
             pltpu.VMEM((t, width), F32),
@@ -990,9 +1072,9 @@
             pltpu.VMEM((2, n_ctx, rows, FPAD), BF),
             pltpu.VMEM((2, n_ctx, rows, width), BF),
             pltpu.VMEM((2, h, 2, rows, FPAD), BF),
-            pltpu.VMEM((2, h, 2, rows, width), BF),
+            pltpu.VMEM((2, h, rows, width), BF),
             pltpu.VMEM((3, rows, FPAD), BF),
-            pltpu.VMEM((3, rows, width), BF),
+            pltpu.VMEM((n_ctx, rows, width), BF),
             DMA((5,)),
             DMA((9,)),
             DMA((9,)),
@@ -1012,23 +1094,34 @@
             DMA((2, 3)),
             DMA((2,)),
             pltpu.VMEM((PACK, t), F32),
+            pltpu.VMEM((n_dp, rows, 2 * ffq), BF),
+            pltpu.VMEM((n_dp, rows, 2 * ffq), BF),
+            DMA((2, n_ctx)),
+            DMA((2, n_ctx)),
         ],
         compiler_params=talks(0),
         name="block",
-    )(doc_lengths, x16, cosine, sine, pack, output_weights.astype(BF), gu_in,
-      down_weights.astype(BF), cot_own)
-    layer_output, input_grad, last_own, out_own, gu_own, down_sum = outs[:6]
-    gu_own = gu_own.astype(F32).transpose(1, 2, 0, 3).reshape(2, rows, ff)
+    )(doc_lengths, x16, cosine, sine, factor_weights, first_gain.reshape(1, rows),
+      second_gain.reshape(1, rows), output_weights, gate_weights, up_weights, down_weights, cot_own)
+    outs = outs[:9]
+    y, dx, fac_own, gain1, gain2, out_own, gate_own, up_own, down_own = pl.pallas_call(
+        emit_kernel,
+        out_shape=tuple(sds(o.shape, o.dtype) for o in outs),
+        in_specs=hbm(9),
+        out_specs=tuple(hbm(9)),
+        scratch_shapes=[pltpu.VMEM(o.shape, o.dtype) for o in outs] + [DMA((9,)), DMA((9,))],
+        name="emit",
+    )(*outs)
     return (
-        layer_output.reshape(1, t, width),
-        input_grad.reshape(1, t, width),
-        last_own[:, FDIM],
-        last_own[:, :FDIM],
+        y.reshape(1, t, width),
+        dx.reshape(1, t, width),
+        gain1.reshape(rows),
+        fac_own,
         out_own,
-        last_own[:, FDIM + 1],
-        gu_own[0],
-        gu_own[1],
-        down_sum,
+        gain2.reshape(rows),
+        gate_own,
+        up_own,
+        down_own,
     )
 
 

time: 206 us -> 169 us (0.82)
  Pallas kernels: 186 us -> 166 us
  other arithmetic: 10.5 us -> 1.42 us
  local copies, waits for them, and re-layouts: 8.32 us -> 0 us
    pallas_call x1, Pallas kernels: 186 us -> 164 us  [body(): pl.pallas_call(functools.partial(block_kernel, n_ctx, nblk), out_shape=(s...]
    unnamed x17 -> x0, local copies, waits for them, and re-layouts: 3.47 us -> none
    another operation x3 -> x0, other arithmetic: 2.92 us -> none
    pallas_call x0 -> x1, Pallas kernels: none -> 2.36 us  [body(): pl.pallas_call(emit_kernel, out_shape=tuple((sds(o.shape, o.dtype) for o...]
    convert_element_type x2 -> x0, other arithmetic: 2.23 us -> none  [the longest x1 1.54 us: body(): output_weights.astype(BF)]
    slice x4 -> x0, local copies, waits for them, and re-layouts: 2.06 us -> none  [the longest x1 1.5 us: body(): last_own[:, FDIM + 1]]
where the time goes in v5:
time: 169 us
  Pallas kernels  166 us (98%)
    pallas_call x1, Pallas kernels, body(): pl.pallas_call(functools.partial(block_kernel, n_ctx, nblk), out_shape=(s...  164 us

profile of v5, /device:TPU:0, one launch (start us, length us, event | category | flops | bytes accessed | tf_op | source)
XLA Modules:
  0.0 168.6 jit_solution(10087237443934039907)
XLA Ops:
  0.7 1.4 multiply_sine_fusion
  2.1 164.0 %block.1 = (bf16[128,1024]{1,0:T(8,128)(2,1)}, bf16[128,1024]{1,0:T(8,128)(2,1)}, f32[32,800]{1,0:T(8,128)}, f32[1,32]{1,0:T(1,128)}, f32[1,32]{1,0:T(1,128)}, /...) custom-call(s32[1,8]{1,0:T(1,128)} %len_ref.1, ...), custom_call_target="tpu_custom_call" | custom-call | tf_op jit(solution)/shard_map/block/pallas_call | solution.py:1025
  166.1 2.4 %emit.1 = (bf16[128,1024]{1,0:T(8,128)(2,1)}, bf16[128,1024]{1,0:T(8,128)(2,1)}, f32[32,800]{1,0:T(8,128)}, f32[1,32]{1,0:T(1,128)}, f32[1,32]{1,0:T(1,128)}, /*...) custom-call(bf16[128,1024]{1,0:T(8,128)(2,1)} %get-tuple-element.27.refs_0_, ...), custom_call_target="tpu_custom_call" | custom-call | tf_op jit(solution)/shard_map/emit/pallas_call | solution.py:1107
  (1 shorter events, 0.0 us)

commit v6 on v5

--- a/solution.py
+++ b/solution.py
@@ -307,19 +307,34 @@
     for hh in range(2):
         acc = 0.0
         for r in range(RKV):
-            a = ka[side * AK + r * H + 2 * p + hh, :, lanes]
-            b = vectors(kv_ref, side, r, lanes)
-            acc = acc + a * b
+            acc = acc + ka[side * AK + r * H + 2 * p + hh] * vectors(kv_ref, side, r, lanes)
         rows.append(acc * (1.0 / RKV))
     return jnp.concatenate(rows, axis=0)
 
 
-def unpack(kv_ref, ka):
+def unpack(kv_ref, ka, lanes):
     for side in range(2):
         first = side * KEY_ROWS
-        a = kv_ref[first : first + AK, :].astype(F32)
+        a = kv_ref[first : first + AK, lanes].astype(F32)
         for i in range(AK):
             ka[side * AK + i] = a[i : i + 1]
+
+
+def unrolled(pair, some):
+    def group(q, carry):
+        for u in range(some):
+            pair(q * some + u, carry)
+        return carry
+
+    lax.fori_loop(0, H // 2 // some, group, 0)
+
+
+def when(condition, run):
+    if isinstance(condition, bool):
+        if condition:
+            run()
+    else:
+        pl.when(condition)(run)
 
 
 def diagonal(pair):
@@ -334,7 +349,10 @@
     return jnp.concatenate([wide[:DH, :t], wide[DH:, t:]], axis=0)
 
 
-def attend_part(nblk, len_ref, q_ref, kv_ref, at_ref, af_ref, inv_ref, p_out, pbuf, ka, bias):
+def attend_part(
+    nblk, arrive, len_ref, q_ref, kv_ref, at_ref, af_ref, inv_ref, p_out, pbuf, ka, bias, qd_ref,
+    num_ref, tot_ref,
+):
     t = q_ref.shape[1]
     c = lax.axis_index("ctx")
     tpos = c * t + lax.broadcasted_iota(jnp.int32, (1, t), 1)
@@ -343,63 +361,63 @@
     for j in range(len_ref.shape[1]):
         start = jnp.where(tpos >= run, run, start)
         run = run + len_ref[0, j]
-    unpack(kv_ref, ka)
-
-    def bias_block(j, _):
-        spos = (c - nblk + 1 + j) * t + lax.broadcasted_iota(jnp.int32, (t, t), 0)
+
+    def prepare(p, carry):
+        rows = pl.ds(pl.multiple_of(p * 2 * DH, 2 * DH), 2 * DH)
+        qd_ref[p] = diagonal(q_ref[rows, :])
+        return carry
+
+    lax.fori_loop(0, H // 2, prepare, 0)
+    num_ref[...] = jnp.zeros_like(num_ref)
+    tot_ref[...] = jnp.zeros_like(tot_ref)
+
+    def block(i, carry):
+        j = nblk - 1 - i
+        when(i > 0, lambda: arrive(i))
+        when(i > 1, lambda: p_out(j + 2).wait())
+        lanes = lane_block(j, t)
+        unpack(kv_ref, ka, lanes)
+        spos = (c - i) * t + lax.broadcasted_iota(jnp.int32, (t, t), 0)
         ok = (spos >= start) & (spos <= tpos)
-        bias[lane_block(j, t), :] = jnp.where(ok, 0.0, NEG)
-        return _
-
-    blocks(nblk, bias_block, 0)
-
-    def pair(p, carry):
-        @pl.when(p > 1)
-        def _():
-            p_out(p - 2).wait()
-
-        rows = pl.ds(pl.multiple_of(p * 2 * DH, 2 * DH), 2 * DH)
-        qd = diagonal(q_ref[rows, :])
-
-        def step(j, state):
-            num, tot = state
-            lanes = lane_block(j, t)
+        bias[...] = jnp.where(ok, 0.0, NEG)
+
+        def pair(p, carry):
             k = expand_pair(ka, kv_ref, 0, p, lanes).T.astype(BF)
             v = expand_pair(ka, kv_ref, 1, p, lanes).astype(BF)
-            b = bias[lanes, :]
-            s = nn(k, qd) * (LOG2E * DH**-0.5) + jnp.concatenate([b, b], axis=1)
+            b = bias[...]
+            s = nn(k, qd_ref[p]) * (LOG2E * DH**-0.5) + jnp.concatenate([b, b], axis=1)
             e = jnp.exp2(s)
-            tot = tot + jnp.sum(e, axis=0, keepdims=True)
+            tot_ref[p] += jnp.sum(e, axis=0, keepdims=True)
             pb = e.astype(BF)
-            pbuf[p % 2, lanes, :] = pb
-            return (num + nn(v, pb), tot)
-
-        num, tot = blocks(
-            nblk, step, (jnp.zeros((2 * DH, 2 * t), F32), jnp.zeros((1, 2 * t), F32))
-        )
-        inv = 1.0 / tot
-        af = undiagonal(num * inv)
+            pbuf[j % 2, p] = pb
+            num_ref[p] += nn(v, pb)
+            return carry
+
+        unrolled(pair, 4)
+        p_out(j).start()
+        return carry
+
+    blocks(nblk, block, 0)
+
+    def finish(p, carry):
+        rows = pl.ds(pl.multiple_of(p * 2 * DH, 2 * DH), 2 * DH)
+        inv = 1.0 / tot_ref[p]
+        af = undiagonal(num_ref[p] * inv)
         af_ref[rows, :] = af
         at_ref[rows, :] = af.astype(BF)
-        p_out(p).start()
-        inv_ref[p] = jnp.broadcast_to(inv, (8, 2 * t))
+        inv_ref[p] = inv
         return carry
 
-    lax.fori_loop(0, H // 2, pair, 0)
-    for p in range(H // 2 - 2, H // 2):
-        p_out(p).wait()
+    lax.fori_loop(0, H // 2, finish, 0)
+    for j in range(2):
+        p_out(j).wait()
 
 
 def attend_back_part(
-    nblk, serve, da_ref, af_ref, inv_ref, p_copy, pbuf, q_ref, kv_ref, a_ref, b_ref, cos_ref, sin_ref,
-    dq_ref, dkv_ref, ka, dka, dqa, db,
+    nblk, serve, ship, da_ref, af_ref, inv_ref, p_copy, pbuf, q_ref, kv_ref, a_ref, b_ref,
+    cos_ref, sin_ref, dq_ref, ka, dka, dqa, db, dkv, qd_ref, dn_ref, dtot_ref, dqs,
 ):
     t = q_ref.shape[1]
-    unpack(kv_ref, ka)
-    db[...] = jnp.zeros_like(db)
-    for side in range(2):
-        first = side * KEY_ROWS + AK
-        dkv_ref[first : first + BK, :] = jnp.zeros((BK, nblk * t), F32)
 
     def factor_back(dwide, side, p, lanes):
         for hh in range(2):
@@ -408,51 +426,67 @@
                 row = side * AK + r * H + 2 * p + hh
                 first = side * KEY_ROWS + AK + r * DH
                 b = vectors(kv_ref, side, r, lanes)
-                dka[row, :, lanes] = jnp.sum(d * b, axis=0, keepdims=True)
-                dkv_ref[first : first + DH, lanes] += d * ka[row, :, lanes]
-
-    def pair(p, carry):
-        @pl.when(p + 1 < H // 2)
-        def _():
-            p_copy(p + 1).start()
-
-        p_copy(p).wait()
+                dka[row] = jnp.sum(d * b, axis=0, keepdims=True)
+                dkv[first : first + DH, :] += d * ka[row]
+
+    def prepare(p, carry):
         rows = pl.ds(pl.multiple_of(p * 2 * DH, 2 * DH), 2 * DH)
-        da = da_ref[rows, :]
-        inv = inv_ref[p][:1]
-        dd = diagonal(da)
-        dn = (dd * inv).astype(BF)
-        dtot = -jnp.sum(dd * diagonal(af_ref[rows, :]), axis=0, keepdims=True) * inv
-        qd = diagonal(q_ref[rows, :])
-
-        def step(j, dq):
-            lanes = lane_block(j, t)
+        inv = inv_ref[p]
+        dd = diagonal(da_ref[rows, :])
+        dn_ref[p] = (dd * inv).astype(BF)
+        dtot_ref[p] = -jnp.sum(dd * diagonal(af_ref[rows, :]), axis=0, keepdims=True) * inv
+        qd_ref[p] = diagonal(q_ref[rows, :])
+        return carry
+
+    lax.fori_loop(0, H // 2, prepare, 0)
+    dqs[...] = jnp.zeros_like(dqs)
+
+    def block(j, carry):
+        when(j + 1 < nblk, lambda: p_copy(j + 1).start())
+        p_copy(j).wait()
+        lanes = lane_block(j, t)
+        unpack(kv_ref, ka, lanes)
+        for side in range(2):
+            first = side * KEY_ROWS + AK
+            dkv[first : first + BK, :] = jnp.zeros((BK, t), F32)
+
+        def pair(p, carry):
+            rows = pl.ds(pl.multiple_of(p * 2 * DH, 2 * DH), 2 * DH)
             k = expand_pair(ka, kv_ref, 0, p, lanes).astype(BF)
             v = expand_pair(ka, kv_ref, 1, p, lanes).T.astype(BF)
-            pb = pbuf[p % 2, lanes, :]
-            ds = (pb.astype(F32) * (nn(v, dn) + dtot)).astype(BF)
-            dq = dq + nn(k, ds)
-            factor_back(nt(qd, ds) * (DH**-0.5), 0, p, lanes)
+            pb = pbuf[j % 2, p]
+            dn = dn_ref[p]
+            ds = (pb.astype(F32) * (nn(v, dn) + dtot_ref[p])).astype(BF)
+            dqs[rows, :] += undiagonal(nn(k, ds))
+            factor_back(nt(qd_ref[p], ds) * (DH**-0.5), 0, p, lanes)
             factor_back(nt(dn, pb), 1, p, lanes)
-            return dq
-
-        dq = undiagonal(blocks(nblk, step, jnp.zeros((2 * DH, 2 * t), F32)))
-        dq = dq * (DH**-0.5 / RQ)
+            return carry
+
+        unrolled(pair, 4)
+        for side in range(2):
+            for i in range(AK):
+                dkv[side * KEY_ROWS + i : side * KEY_ROWS + i + 1, :] = dka[side * AK + i]
+        ship(j)
+        serve(j)
+        return carry
+
+    blocks(nblk, block, 0)
+    db[...] = jnp.zeros_like(db)
+
+    def pair_q(p, carry):
+        rows = pl.ds(pl.multiple_of(p * 2 * DH, 2 * DH), 2 * DH)
+        dq = dqs[rows, :] * (DH**-0.5 / RQ)
         for hh in range(2):
             d = dq[hh * DH : (hh + 1) * DH]
             for r in range(RQ):
                 row = r * H + 2 * p + hh
                 dqa[row] = jnp.sum(d * b_ref[r * DH : (r + 1) * DH, :], axis=0, keepdims=True)
                 db[r * DH : (r + 1) * DH, :] += d * a_ref[row]
-        serve(p)
         return carry
 
-    lax.fori_loop(0, H // 2, pair, 0)
+    lax.fori_loop(0, H // 2, pair_q, 0)
     for i in range(AQ):
         dq_ref[i : i + 1, :] = dqa[i]
-    for side in range(2):
-        for i in range(AK):
-            dkv_ref[side * KEY_ROWS + i : side * KEY_ROWS + i + 1, :] = dka[side * AK + i]
     dq_ref[AQ : AQ + BQ, :] = rope_back(db[...], cos_ref[...], sin_ref[...], RQ)
 
 
@@ -638,7 +672,7 @@
     pre_part(x, g1, w, cos_ref[...], sin_ref[...], nt_ref, q_ref, own_kv, a_ref, b_ref)
 
     def kv_copy(k):
-        dst = kv_ref.at[:, (nblk - 1 - k) * t : (nblk - k) * t]
+        dst = kv_ref.at[:, lane_block(nblk - 1 - k, t)]
         return remote(own_kv, dst, kv_send.at[k - 1], kv_recv.at[k - 1], (d, (c + k) % n))
 
     for k in range(1, nblk):
@@ -648,25 +682,32 @@
     dr.start(0)
     oo.arrive()
     swap(3, wo, xd, (cd + 2) % 4)
-    for k in range(1, nblk):
-        @pl.when(c - k >= 0)
-        def _():
-            kv_copy(k).wait_recv()
     full = n // 2 - 1
     middle_step = 1 + full // 2
-    steps(1, middle_step, lambda s: [one.step(s) for one in large])
-
-    def p_out(p):
-        return pltpu.make_async_copy(pbuf.at[p % 2], p_ref.at[p], p_sem.at[p % 2])
+
+    def arrive(i):
+        @pl.when(c - i >= 0)
+        def _():
+            kv_copy(i).wait_recv()
+
+        when(i == 2, lambda: steps(1, middle_step, gr.step))
+
+
+    def p_out(j):
+        return pltpu.make_async_copy(pbuf.at[j % 2], p_ref.at[j], p_sem.at[j % 2])
 
     pl.run_scoped(
         functools.partial(
-            attend_part, nblk, len_ref, q_ref, kv_ref, at_ref, af_ref, inv_ref, p_out, pbuf
+            attend_part, nblk, arrive, len_ref, q_ref, kv_ref, at_ref, af_ref, inv_ref, p_out, pbuf
         ),
-        pltpu.VMEM((2 * AK, 1, nblk * t), F32),
-        pltpu.VMEM((nblk * t, t), F32),
-    )
-
+        pltpu.VMEM((2 * AK, 1, t), F32),
+        pltpu.VMEM((t, t), F32),
+        pltpu.VMEM((H // 2, 2 * DH, 2 * t), BF),
+        pltpu.VMEM((H // 2, 2 * DH, 2 * t), F32),
+        pltpu.VMEM((H // 2, 1, 2 * t), F32),
+    )
+
+    steps(1, middle_step, dr.step)
     for _, arrival in (near[1], near[3]):
         arrival.wait_recv()
     middle = x + nn(at_ref[...].T, wo[...].reshape(width, width))
@@ -696,6 +737,39 @@
                 )
             )
 
+    cut = -(-wd_part.shape[1] // 16) * 8
+
+    def wd_half(ref, w):
+        return ref.at[:cut] if w == 0 else ref.at[cut:]
+
+    gs = ScatterRing(
+        n, lambda o: gu_part.at[:, o], lambda o, w: gu_part.at[2 * w : 2 * w + 2, o], gu_land,
+        None, lambda ref, w: ref.at[2 * w : 2 * w + 2], ring_send.at[6], ring_recv.at[6],
+    )
+    ds_ = ScatterRing(
+        n, lambda o: wd_part.at[o], lambda o, w: wd_half(wd_part.at[o], w), wd_land,
+        None, wd_half, ring_send.at[7], ring_recv.at[7],
+    )
+    scatter = (gs, ds_)
+    fs = PairScatter(
+        n, fac_part, fac_held, fac_land, fac_own, pair_send.at[0], pair_recv.at[0],
+        ring_send.at[8], ring_recv.at[8],
+    )
+    ws = PairScatter(
+        n, wo_part, wo_held, wo_land, wo_own, pair_send.at[1], pair_recv.at[1],
+        ring_send.at[9], ring_recv.at[9], wo_own,
+    )
+    h = n // 2
+
+    def advance(s):
+        for one in scatter:
+            one.step(s)
+
+    points = 2
+
+    def serve(k):
+        steps(2 + -(-(k - 1) * (h - 2) // points), 2 + -(-k * (h - 2) // points), advance)
+
     def feed(both_ff, dh, hid, dgu):
         down = wd[...].reshape(ffq, width)
 
@@ -721,7 +795,13 @@
                 return carry
 
             lax.fori_loop(0, both // 32, rows_of, 0)
-            all_rows = pl.ds(base, both)
+            return carry
+
+        def pair_back(i, carry):
+            xx = i * x_at + (1 - i) * (1 - x_at)
+            two = pl.ds(2 * xx, 2)
+            both = 2 * t
+            all_rows = pl.ds(pl.multiple_of(xx * both, both), both)
             dn_in[two] = nt(dgu[all_rows, :], matrix()).astype(BF).reshape(2, t, width)
             out_in[two] = nn(hid[all_rows, :], down).astype(BF).reshape(2, t, width)
 
@@ -733,12 +813,6 @@
             return carry
 
         lax.fori_loop(0, 2, pair_rows, 0)
-        first[1].start()
-        first[3].start()
-        for i, part in enumerate(parts):
-            first[2 * i].wait_recv()
-            dp_land[i, 0] = (dp_land[i, 0].astype(F32) + part[xd].astype(F32)).astype(BF)
-            dp_next(i).start()
 
         def tn(a, b):
             return lax.dot_general(a, b, (((0,), (0,)), ((), ())), preferred_element_type=F32)
@@ -754,6 +828,16 @@
             return carry
 
         lax.fori_loop(0, n_dp, columns, 0)
+        for one in scatter:
+            one.start()
+        lax.fori_loop(0, 2, pair_back, 0)
+        first[1].start()
+        first[3].start()
+        for i, part in enumerate(parts):
+            first[2 * i].wait_recv()
+            dp_land[i, 0] = (dp_land[i, 0].astype(F32) + part[xd].astype(F32)).astype(BF)
+            dp_next(i).start()
+        advance(1)
 
     def dp_next(i):
         return remote(dp_land.at[i, 0], dp_land.at[i, 2], dp_send.at[i, 2], dp_recv.at[i, 2], (xd, c))
@@ -766,37 +850,6 @@
         pltpu.VMEM((n_dp * t, 2 * ffq), BF),
     )
     second = [dp_next(i) for i in range(2)]
-    cut = -(-wd_part.shape[1] // 16) * 8
-
-    def wd_half(ref, w):
-        return ref.at[:cut] if w == 0 else ref.at[cut:]
-
-    gs = ScatterRing(
-        n, lambda o: gu_part.at[:, o], lambda o, w: gu_part.at[2 * w : 2 * w + 2, o], gu_land,
-        None, lambda ref, w: ref.at[2 * w : 2 * w + 2], ring_send.at[6], ring_recv.at[6],
-    )
-    ds_ = ScatterRing(
-        n, lambda o: wd_part.at[o], lambda o, w: wd_half(wd_part.at[o], w), wd_land,
-        None, wd_half, ring_send.at[7], ring_recv.at[7],
-    )
-    scatter = (gs, ds_)
-    for one in scatter:
-        one.start()
-    fs = PairScatter(
-        n, fac_part, fac_held, fac_land, fac_own, pair_send.at[0], pair_recv.at[0],
-        ring_send.at[8], ring_recv.at[8],
-    )
-    ws = PairScatter(
-        n, wo_part, wo_held, wo_land, wo_own, pair_send.at[1], pair_recv.at[1],
-        ring_send.at[9], ring_recv.at[9], wo_own,
-    )
-    h = n // 2
-
-    def advance(s):
-        for one in scatter:
-            one.step(s)
-
-    advance(1)
     for i in range(2):
         first[2 * i + 1].wait_recv()
     second[0].wait_recv()
@@ -810,6 +863,7 @@
         - middle * (r2 * r2 * r2 * jnp.mean(u2 * middle, axis=-1, keepdims=True))
     )
     dmid_ref[...] = d_middle
+    serve(1)
     d_branch = d_middle.astype(BF)
     wo_part[...] = nn(at_ref[...], d_branch).astype(BF).reshape(wo_part.shape)
     ws.start()
@@ -820,43 +874,42 @@
         + (out_in[d].astype(F32) + dp_land[1, 1].astype(F32) + dp_land[1, 2].astype(F32))
     ).astype(BF)
     ws.enter()
-    points = 3
-
-    def serve(k):
-        steps(2 + -(-(k - 1) * (h - 2) // points), 2 + -(-k * (h - 2) // points), advance)
-
-    serve(1)
-
-    def serve_pair(p):
-        @pl.when(p == H // 2 - 3)
-        def _():
-            serve(2)
-            ws.across()
-
-    def p_copy(p):
-        return pltpu.make_async_copy(p_ref.at[p], pbuf.at[p % 2], p_sem.at[p % 2])
+    def serve_block(j):
+        when(j == nblk - 1, lambda: serve(2))
+
+    def p_copy(j):
+        return pltpu.make_async_copy(p_ref.at[j], pbuf.at[j % 2], p_sem.at[j % 2])
 
     p_copy(0).start()
 
-    def attention_back(ka, dka, dqa, db, dkv, dkv16):
+    def attention_back(dkv16, dkv, *scratch):
+        def dkv_copy(k):
+            return remote(
+                dkv16.at[k - 1], kv_land.at[k - 1], dkv_send.at[k - 1], dkv_recv.at[k - 1],
+                (d, (c + n - k) % n),
+            )
+
+        def ship(j):
+            k = nblk - 1 - j
+
+            def away():
+                dkv16[k - 1] = dkv[...].astype(BF)
+
+                @pl.when(c - k >= 0)
+                def _():
+                    dkv_copy(k).start()
+
+            def home():
+                own_dkv[...] = dkv[...]
+
+            when(k > 0, away)
+            when(k == 0, home)
+
+        ka, dka, dqa, db, qd, dn, dtot, dqs = scratch
         attend_back_part(
-            nblk, serve_pair, da_ref, af_ref, inv_ref, p_copy, pbuf, q_ref, kv_ref, a_ref, b_ref,
-            cos_ref, sin_ref, dq_ref, dkv, ka, dka, dqa, db,
+            nblk, serve_block, ship, da_ref, af_ref, inv_ref, p_copy, pbuf, q_ref, kv_ref, a_ref,
+            b_ref, cos_ref, sin_ref, dq_ref, ka, dka, dqa, db, dkv, qd, dn, dtot, dqs,
         )
-        dkv16[...] = dkv[...].astype(BF)
-
-        def dkv_copy(k):
-            src = dkv16.at[:, (nblk - 1 - k) * t : (nblk - k) * t]
-            return remote(
-                src, kv_land.at[k - 1], dkv_send.at[k - 1], dkv_recv.at[k - 1], (d, (c + n - k) % n)
-            )
-
-        for k in range(1, nblk):
-            @pl.when(c - k >= 0)
-            def _():
-                dkv_copy(k).start()
-        serve(3)
-        own_dkv[...] = dkv[:, (nblk - 1) * t :]
         for k in range(1, nblk):
             @pl.when(c + k < n)
             def _():
@@ -869,15 +922,18 @@
 
     pl.run_scoped(
         attention_back,
-        pltpu.VMEM((2 * AK, 1, nblk * t), F32),
-        pltpu.VMEM((2 * AK, 1, nblk * t), F32),
+        pltpu.VMEM((nblk - 1, PACK, t), BF),
+        pltpu.VMEM((PACK, t), F32),
+        pltpu.VMEM((2 * AK, 1, t), F32),
+        pltpu.VMEM((2 * AK, 1, t), F32),
         pltpu.VMEM((AQ, 1, t), F32),
         pltpu.VMEM((BQ, t), F32),
-        pltpu.VMEM((PACK, nblk * t), F32),
-        pltpu.VMEM((PACK, nblk * t), BF),
-    )
-    ws.ring.step(1)
-    steps(2, h - 1, ws.ring.step)
+        pltpu.VMEM((H // 2, 2 * DH, 2 * t), BF),
+        pltpu.VMEM((H // 2, 2 * DH, 2 * t), BF),
+        pltpu.VMEM((H // 2, 1, 2 * t), F32),
+        pltpu.VMEM((H * DH, t), F32),
+    )
+    ws.across()
     dp = own_dkv[...]
     d_bk = rope_back(dp[AK : AK + BK], cos_ref[...], sin_ref[...], RKV)
     d_fac_t = jnp.concatenate(
@@ -900,6 +956,7 @@
     dx_ref[...] = (
         dmid_ref[...] + r1 * u1 - x * (r1 * r1 * r1 * jnp.mean(u1 * x, axis=-1, keepdims=True))
     ).astype(BF)
+    ws.ring.step(1)
     fs.enter()
     gu_own[...] = gs.result().astype(BF)
     keep = pltpu.make_async_copy(gu_own.at[d], gu_ref.at[d], own_sem.at[0])
@@ -917,7 +974,7 @@
             )
         )
         last[-1][0].start()
-    ws.ring.step(h - 1)
+    steps(2, h, ws.ring.step)
     fs.ring.step(1)
     wd_ref[...] = ds_.result()
     steps(2, h, fs.ring.step)
@@ -1034,7 +1091,7 @@
             sds((rows, ff), F32),
             sds((rows, ff), F32),
             sds((down_rows, width), F32),
-            sds((H // 2, nblk * t, 2 * t), BF),
+            sds((nblk, H // 2, t, 2 * t), BF),
         ),
         in_specs=[SMEM] + vmem(11),
         out_specs=tuple(vmem(9) + hbm(1)),
@@ -1046,8 +1103,8 @@
             pltpu.VMEM((PACK, nblk * t), BF),
             pltpu.VMEM((H * DH, t), BF),
             pltpu.VMEM((H * DH, t), F32),
-            pltpu.VMEM((H // 2, 8, 2 * t), F32),
-            pltpu.VMEM((2, nblk * t, 2 * t), BF),
+            pltpu.VMEM((H // 2, 1, 2 * t), F32),
+            pltpu.VMEM((2, H // 2, t, 2 * t), BF),
             pltpu.VMEM((n_dp, n_ctx, rows, FPAD), BF),
             pltpu.VMEM((n_dp, n_ctx, rows, width), BF),
             pltpu.VMEM((n_dp, n_ctx, rows, 2 * ffq), BF),

time: 169 us -> 161 us (0.953)
  Pallas kernels: 166 us -> 159 us
    pallas_call x1, Pallas kernels: 164 us -> 156 us  [body(): pl.pallas_call(functools.partial(block_kernel, n_ctx, nblk), out_shape=(s...]
where the time goes in v6:
time: 161 us
  Pallas kernels  159 us (99%)
    pallas_call x1, Pallas kernels, body(): pl.pallas_call(functools.partial(block_kernel, n_ctx, nblk), out_shape=(s...  156 us

profile of v6, /device:TPU:0, one launch (start us, length us, event | category | flops | bytes accessed | tf_op | source)
XLA Modules:
  0.0 160.7 jit_solution(16960073089265372113)
XLA Ops:
  0.7 1.4 multiply_sine_fusion
  2.1 156.1 %block.1 = (bf16[128,1024]{1,0:T(8,128)(2,1)}, bf16[128,1024]{1,0:T(8,128)(2,1)}, f32[32,800]{1,0:T(8,128)}, f32[1,32]{1,0:T(1,128)}, f32[1,32]{1,0:T(1,128)}, /...) custom-call(s32[1,8]{1,0:T(1,128)} %len_ref.1, ...), custom_call_target="tpu_custom_call" | custom-call | tf_op jit(solution)/shard_map/block/pallas_call | solution.py:1082
  158.2 2.4 %emit.1 = (bf16[128,1024]{1,0:T(8,128)(2,1)}, bf16[128,1024]{1,0:T(8,128)(2,1)}, f32[32,800]{1,0:T(8,128)}, f32[1,32]{1,0:T(1,128)}, f32[1,32]{1,0:T(1,128)}, /*...) custom-call(bf16[128,1024]{1,0:T(8,128)(2,1)} %get-tuple-element.27.refs_0_, ...), custom_call_target="tpu_custom_call" | custom-call | tf_op jit(solution)/shard_map/emit/pallas_call | solution.py:1164
  (1 shorter events, 0.0 us)

commit v7 on v6

--- a/solution.py
+++ b/solution.py
@@ -771,8 +771,6 @@
         steps(2 + -(-(k - 1) * (h - 2) // points), 2 + -(-k * (h - 2) // points), advance)
 
     def feed(both_ff, dh, hid, dgu):
-        down = wd[...].reshape(ffq, width)
-
         def matrix():
             return gu[...].reshape(width, 2 * ffq)
 
@@ -781,7 +779,7 @@
             two = pl.ds(2 * xx, 2)
             both = 2 * t
             both_ff[...] = nn(nm[two].reshape(both, width), matrix())
-            dh[...] = nt(cot[two].reshape(both, width), down)
+            dh[...] = nt(cot[two].reshape(both, width), wd[...].reshape(ffq, width))
             base = pl.multiple_of(xx * both, both)
 
             def rows_of(k, carry):
@@ -797,20 +795,34 @@
             lax.fori_loop(0, both // 32, rows_of, 0)
             return carry
 
-        def pair_back(i, carry):
+        def ends(i):
             xx = i * x_at + (1 - i) * (1 - x_at)
-            two = pl.ds(2 * xx, 2)
-            both = 2 * t
-            all_rows = pl.ds(pl.multiple_of(xx * both, both), both)
-            dn_in[two] = nt(dgu[all_rows, :], matrix()).astype(BF).reshape(2, t, width)
-            out_in[two] = nn(hid[all_rows, :], down).astype(BF).reshape(2, t, width)
+            return pl.ds(2 * xx, 2), pl.ds(pl.multiple_of(xx * 2 * t, 2 * t), 2 * t)
+
+        def norm_back(i, carry):
+            two, these = ends(i)
+            dn_in[two] = nt(dgu[these, :], matrix()).astype(BF).reshape(2, t, width)
 
             @pl.when(i == 0)
             def _():
                 first[0].start()
+
+            return carry
+
+        def down(i, carry):
+            two, these = ends(i)
+            out_in[two] = nn(hid[these, :], wd[...].reshape(ffq, width)).astype(BF).reshape(2, t, width)
+
+            @pl.when(i == 0)
+            def _():
                 first[2].start()
 
             return carry
+
+        def onward(i, part):
+            first[2 * i].wait_recv()
+            dp_land[i, 0] = (dp_land[i, 0].astype(F32) + part[xd].astype(F32)).astype(BF)
+            dp_next(i).start()
 
         lax.fori_loop(0, 2, pair_rows, 0)
 
@@ -818,25 +830,29 @@
             return lax.dot_general(a, b, (((0,), (0,)), ((), ())), preferred_element_type=F32)
 
         quarter = width // n_dp
+
+        def down_columns(j, carry):
+            lanes = pl.ds(pl.multiple_of(j * quarter, quarter), quarter)
+            some = cot[:, :, lanes].reshape(n_dp * t, quarter)
+            wd_part[:, :, lanes] = tn(hid[...], some).astype(BF).reshape(wd_part.shape[:2] + (quarter,))
+            return carry
 
         def columns(j, carry):
             lanes = pl.ds(pl.multiple_of(j * quarter, quarter), quarter)
             some = nm[:, :, lanes].reshape(n_dp * t, quarter)
             gu_part[j] = tn(some, dgu[...]).astype(BF).reshape(gu_part.shape[1:])
-            c_some = cot[:, :, lanes].reshape(n_dp * t, quarter)
-            wd_part[:, :, lanes] = tn(hid[...], c_some).astype(BF).reshape(wd_part.shape[:2] + (quarter,))
             return carry
 
+        lax.fori_loop(0, n_dp, down_columns, 0)
+        ds_.start()
         lax.fori_loop(0, n_dp, columns, 0)
-        for one in scatter:
-            one.start()
-        lax.fori_loop(0, 2, pair_back, 0)
+        gs.start()
+        lax.fori_loop(0, 2, norm_back, 0)
         first[1].start()
+        onward(0, dn_in)
+        lax.fori_loop(0, 2, down, 0)
         first[3].start()
-        for i, part in enumerate(parts):
-            first[2 * i].wait_recv()
-            dp_land[i, 0] = (dp_land[i, 0].astype(F32) + part[xd].astype(F32)).astype(BF)
-            dp_next(i).start()
+        onward(1, out_in)
         advance(1)
 
     def dp_next(i):

time: 161 us -> 162 us (level)
  no operation moved by 1% of the time
where the time goes in v7:
time: 162 us; the launch traced here: 161 us
  Pallas kernels  159 us (98%)
    pallas_call x1, Pallas kernels, body(): pl.pallas_call(functools.partial(block_kernel, n_ctx, nblk), out_shape=(s...  157 us

profile of v7, /device:TPU:0, one launch (start us, length us, event | category | flops | bytes accessed | tf_op | source)
XLA Modules:
  0.0 161.4 jit_solution(9737325689313440499)
XLA Ops:
  0.7 1.4 multiply_sine_fusion
  2.1 156.8 %block.1 = (bf16[128,1024]{1,0:T(8,128)(2,1)}, bf16[128,1024]{1,0:T(8,128)(2,1)}, f32[32,800]{1,0:T(8,128)}, f32[1,32]{1,0:T(1,128)}, f32[1,32]{1,0:T(1,128)}, /...) custom-call(s32[1,8]{1,0:T(1,128)} %len_ref.1, ...), custom_call_target="tpu_custom_call" | custom-call | tf_op jit(solution)/shard_map/block/pallas_call | solution.py:1098
  158.8 2.4 %emit.1 = (bf16[128,1024]{1,0:T(8,128)(2,1)}, bf16[128,1024]{1,0:T(8,128)(2,1)}, f32[32,800]{1,0:T(8,128)}, f32[1,32]{1,0:T(1,128)}, f32[1,32]{1,0:T(1,128)}, /*...) custom-call(bf16[128,1024]{1,0:T(8,128)(2,1)} %get-tuple-element.27.refs_0_, ...), custom_call_target="tpu_custom_call" | custom-call | tf_op jit(solution)/shard_map/emit/pallas_call | solution.py:1180
  (1 shorter events, 0.0 us)
